TPU v7x, 16 devices: a whole 2x2x2 slice. The times are simulated.
16 devices in a mesh: rep: 1, dp: 16 (over x, y, z, core).
Axes of the slice: x: 2, y: 2, z: 2, core: 2. Of those that a mesh axis runs over, the one named last changes fastest.
Arguments:
- x: bfloat16 [16, 2048, 896], P(('rep', 'dp'))
- dy: bfloat16 [16, 2048, 896], P(('rep', 'dp'))
- w_gate: bfloat16 [2, 896, 2560], replicated
- w_up: bfloat16 [2, 896, 2560], replicated
- w_down: bfloat16 [2, 2560, 896], replicated
- m_w_gate: float32 [2, 896, 2560], P(None, 'dp')
- m_w_up: float32 [2, 896, 2560], P(None, 'dp')
- m_w_down: float32 [2, 2560, 896], P(None, 'dp')
- v_w_gate: float32 [2, 896, 2560], P(None, 'dp')
- v_w_up: float32 [2, 896, 2560], P(None, 'dp')
- v_w_down: float32 [2, 2560, 896], P(None, 'dp')
Outputs:
- output 1: bfloat16 [2, 896, 2560], P('rep')
- output 2: bfloat16 [2, 896, 2560], P('rep')
- output 3: bfloat16 [2, 2560, 896], P('rep')
- output 4: float32 [2, 896, 2560], P('rep', 'dp')
- output 5: float32 [2, 896, 2560], P('rep', 'dp')
- output 6: float32 [2, 2560, 896], P('rep', 'dp')
- output 7: float32 [2, 896, 2560], P('rep', 'dp')
- output 8: float32 [2, 896, 2560], P('rep', 'dp')
- output 9: float32 [2, 2560, 896], P('rep', 'dp')
All inputs are finite; a program needn't handle non-finite values.
Results may differ from a plain program's by a relative error of at most 0.022.
Values are sent between devices in bfloat16 or wider.
A program may use at most 2 GiB of HBM per device.

v0:
```python
import jax
import jax.numpy as jnp
from jax import lax

NAMES = ("w_gate", "w_up", "w_down")


def matmul(a, w):
    return jnp.dot(a, w, preferred_element_type=jnp.float32).astype(jnp.bfloat16)


def normed(h):
    wide = h.astype(jnp.float32)
    scale = lax.rsqrt(jnp.mean(wide**2, -1, keepdims=True) + 1e-6)
    return (wide * scale).astype(jnp.bfloat16)


def layer(h, w):
    a = normed(h)
    gate = jnp.dot(a, w["w_gate"], preferred_element_type=jnp.float32)
    up = jnp.dot(a, w["w_up"], preferred_element_type=jnp.float32)
    return h + matmul((jax.nn.silu(gate) * up).astype(jnp.bfloat16), w["w_down"])


def adamw(w, m, v, g):
    m = 0.9 * m + 0.1 * g
    v = 0.95 * v + 0.05 * g * g
    step = m * lax.rsqrt(v + 1e-8) + 0.1 * w
    return (w - 0.02 * step).astype(jnp.bfloat16), m, v


def clipped(gradients, sum_of_squares, count):
    factor = jnp.minimum(1.0, 0.5 * lax.rsqrt(sum_of_squares / count + 1e-30))
    return [g * factor for g in gradients]


def stack(weights, h):
    for number in range(weights["w_gate"].shape[0]):
        h = layer(h, {name: w[number] for name, w in weights.items()})
    return h


def solution(mesh):
    groups = mesh.shape["rep"]

    def step(x, dy, *arrays):
        weights, m, v = (arrays[i : i + 3] for i in (0, 3, 6))
        x, dy = (t.reshape(groups, -1, *t.shape[1:]) for t in (x, dy))

        def of_a_group(x, dy):
            _, back = jax.vjp(lambda w: stack(w, x), dict(zip(NAMES, weights, strict=True)))
            by_weights = back(dy)[0]
            gradients = [by_weights[name].astype(jnp.float32) for name in NAMES]
            gradients = clipped(gradients, sum(jnp.sum(g * g) for g in gradients), sum(g.size for g in gradients))
            new = [adamw(w.astype(jnp.float32), m, v, g) for w, m, v, g in zip(weights, m, v, gradients, strict=True)]
            return tuple(one[which] for which in range(3) for one in new)

        return tuple(t.reshape(-1, *t.shape[2:]) for t in jax.vmap(of_a_group)(x, dy))

    return step
```

profile of v0, /device:TPU:0, one launch (start us, length us, event | category | flops | bytes accessed | tf_op | source)
XLA Modules:
  0.0 1287.7 jit_solution(14579125824935540466)
XLA Ops:
  17.6 18.5 %fusion.173 = f32[2048,2560]{1,0:T(8,128)} fusion(bf16[2,896,2560]{2,1,0:T(8,128)(2,1)} %param.12, bf16[1,2048,896]{1,2,0:T(8,128)(2,1)S(1)} %fusion.157), kind=kOutput, calls=%fused_computation.224 | convolution fusion | flops 9395240960 | bytes 29229056 | tf_op jit(solution)/vmap(jvp())/dot_general | solution.py:20
  36.1 24.3 %fusion.150 = (bf16[1,2048,2560]{2,1,0:T(8,128)(2,1)}, f32[2048,2560]{1,0:T(8,128)}) fusion(f32[2048,2560]{1,0:T(8,128)} %fusion.173, bf16[2,896,2560]{2,1,0:T(8,128)(2,1)} %param.17, bf16[1,2048,896]{1,2,0:T(8,128)(2,1)S(1)} %fusion.157), kind=kOutput, calls=%fused_computation.189 | convolution fusion | flops 9426698240 | bytes 60686336 | tf_op jit(solution)/vmap(jvp())/dot_general | solution.py:21
  60.4 15.9 %fusion.160 = (f32[2048]{0:T(1024)S(1)}, bf16[1,2048,896]{1,2,0:T(8,128)(2,1)}) fusion(bf16[1,2048,896]{1,2,0:T(8,128)(2,1)S(1)} %copy-done.11, bf16[2,2560,896]{2,1,0:T(8,128)(2,1)} %param.15, bf16[1,2048,2560]{2,1,0:T(8,128)(2,1)} %get-tuple-element.263), kind=kOutput, calls=%fused_computation.211 | convolution fusion | flops 9404413952 | bytes 22421504 | tf_op jit(solution)/vmap(jvp())/dot_general | solution.py:9
  80.0 18.5 %fusion.163 = f32[2048,2560]{1,0:T(8,128)} fusion(bf16[2,896,2560]{2,1,0:T(8,128)(2,1)} %param.12, bf16[1,2048,896]{1,2,0:T(8,128)(2,1)S(1)} %fusion.161), kind=kOutput, calls=%fused_computation.214 | convolution fusion | flops 9395240960 | bytes 29229056 | tf_op jit(solution)/vmap(jvp())/dot_general | solution.py:20
  98.4 24.6 %fusion.149 = (bf16[1,2048,2560]{2,1,0:T(8,128)(2,1)}, f32[2048,2560]{1,0:T(8,128)}) fusion(f32[2048,2560]{1,0:T(8,128)} %fusion.163, bf16[2,896,2560]{2,1,0:T(8,128)(2,1)} %param.17, bf16[1,2048,896]{1,2,0:T(8,128)(2,1)S(1)} %fusion.161), kind=kOutput, calls=%fused_computation.187 | convolution fusion | flops 9426698240 | bytes 60686336 | tf_op jit(solution)/vmap(jvp())/dot_general | solution.py:21
  123.0 14.6 %copy.3 = bf16[1,2048,2560]{1,2,0:T(8,128)(2,1)} copy(bf16[1,2048,2560]{2,1,0:T(8,128)(2,1)} %get-tuple-element.269) | data formatting | bytes 20971520
  137.6 123.9 %while.16 = (bf16[1,2048,2560]{1,2,0:T(8,128)(2,1)}, bf16[1,2048,896]{2,1,0:T(8,128)(2,1)}, f32[160,896]{1,0:T(8,128)S(1)}, f32[160,896]{1,0:T(8,128)}, u32[]{:T...) while((bf16[1,2048,2560]{1,2,0:T(8,128)(2,1)}, ...), condition=%wide.windowed_dot_general_cond_rs.4.clone, body=%wide.windowed_dot_general_body_rs.4.clone.sunk | while | flops 2354913280 | bytes 48955984 | solution.py:9
  149.9 12.1 collective-permute-start.18
  275.7 14.5 %copy.5 = bf16[1,2048,2560]{1,2,0:T(8,128)(2,1)} copy(bf16[1,2048,2560]{2,1,0:T(8,128)(2,1)} %get-tuple-element.263) | data formatting | bytes 20971520
  290.2 27.7 %convert_multiply_fusion.2 = (bf16[1,2048,2560]{2,1,0:T(8,128)(2,1)}, bf16[1,2048,2560]{2,1,0:T(8,128)(2,1)S(1)}) fusion(f32[2048,2560]{1,0:T(8,128)} %fusion.163, f32[2048,2560]{1,0:T(8,128)} %get-tuple-element.270, bf16[2,2560,896]{2,1,0:T(8,128)(2,1)} %param.15, bf16[1,2048,896]{2,1,0:T(8,128)(2,1)} %get-tuple-element.744), kind=kOutput, calls=%fused_computation.170 | convolution fusion | flops 9479127040 | bytes 71172096 | tf_op jit(solution)/vmap(transpose(jvp()))/dot_general | solution.py:9
  317.9 14.9 %fusion.142 = bf16[2048,896]{0,1:T(8,128)(2,1)} fusion(bf16[1,2048,2560]{2,1,0:T(8,128)(2,1)S(1)} %get-tuple-element.541, bf16[2,896,2560]{2,1,0:T(8,128)(2,1)} %param.12), kind=kOutput, calls=%fused_computation.176 | convolution fusion | flops 9395240960 | bytes 18743296 | tf_op jit(solution)/vmap(transpose(jvp()))/dot_general | solution.py:20
  332.8 15.8 %fusion.162 = (f32[2048]{0:T(1024)S(1)}, bf16[2048,896]{0,1:T(8,128)(2,1)S(1)}) fusion(bf16[1,2048,896]{1,2,0:T(8,128)(2,1)} %get-tuple-element.266, bf16[2048,896]{0,1:T(8,128)(2,1)} %fusion.142, bf16[2,896,2560]{2,1,0:T(8,128)(2,1)} %param.17, bf16[1,2048,2560]{2,1,0:T(8,128)(2,1)} %get-tuple-element.613), kind=kOutput, calls=%fused_computation.213 | convolution fusion | flops 9404413952 | bytes 26091520 | tf_op jit(solution)/vmap(transpose(jvp()))/dot_general | solution.py:21
  359.4 121.4 %while.17 = (bf16[1,2048,896]{2,1,0:T(8,128)(2,1)}, bf16[1,2048,2560]{1,2,0:T(8,128)(2,1)}, f32[896,160]{0,1:T(8,128)S(1)}, f32[896,160]{0,1:T(8,128)}, u32[]{:T...) while((bf16[1,2048,896]{2,1,0:T(8,128)(2,1)}, ...), condition=%wide.windowed_dot_general_cond_rs.5.clone, body=%wide.windowed_dot_general_body_rs.5.clone.sunk | while | flops 2354913280 | bytes 48955984 | solution.py:9
  370.5 12.1 collective-permute-start.22
  488.9 124.7 %while.14 = (bf16[1,2048,2560]{2,1,0:T(8,128)(2,1)}, bf16[1,2048,896]{1,2,0:T(8,128)(2,1)}, f32[2560,56]{0,1:T(8,128)S(1)}, f32[2560,56]{0,1:T(8,128)}, u32[]{:T...) while((bf16[1,2048,2560]{2,1,0:T(8,128)(2,1)}, ...), condition=%wide.windowed_dot_general_cond_rs.2.clone, body=%wide.windowed_dot_general_body_rs.2.clone.sunk | while | flops 2351505408 | bytes 105579144 | solution.py:21
  500.3 12.1 collective-permute-start.10
  621.7 31.3 %convert_multiply_fusion = (bf16[1,2048,2560]{2,1,0:T(8,128)(2,1)}, bf16[1,2048,2560]{2,1,0:T(8,128)(2,1)}) fusion(f32[2048,2560]{1,0:T(8,128)} %fusion.173, f32[2048,2560]{1,0:T(8,128)} %get-tuple-element.264, bf16[2,2560,896]{2,1,0:T(8,128)(2,1)} %param.15, bf16[1,2048,896]{1,2,0:T(8,128)(2,1)} %fusion.185), kind=kOutput, calls=%fused_computation.168 | convolution fusion | flops 9479127040 | bytes 71172096 | tf_op jit(solution)/vmap(transpose(jvp()))/dot_general | solution.py:9
  652.9 122.9 %while.15 = (bf16[1,2048,2560]{2,1,0:T(8,128)(2,1)}, bf16[1,2048,896]{1,2,0:T(8,128)(2,1)}, f32[2560,56]{0,1:T(8,128)S(1)}, f32[2560,56]{0,1:T(8,128)}, u32[]{:T...) while((bf16[1,2048,2560]{2,1,0:T(8,128)(2,1)}, ...), condition=%wide.windowed_dot_general_cond_rs.3.clone, body=%wide.windowed_dot_general_body_rs.3.clone.sunk | while | flops 2351505408 | bytes 105579144 | solution.py:21
  775.8 119.6 %while.12 = (bf16[1,2048,2560]{2,1,0:T(8,128)(2,1)}, bf16[1,2048,896]{1,2,0:T(8,128)(2,1)}, f32[2560,56]{0,1:T(8,128)S(1)}, f32[2560,56]{0,1:T(8,128)S(1)}, u32[...) while((bf16[1,2048,2560]{2,1,0:T(8,128)(2,1)}, ...), condition=%wide.windowed_dot_general_cond_rs.clone, body=%wide.windowed_dot_general_body_rs.clone.sunk | while | flops 2351505408 | bytes 105579144 | solution.py:20
  896.2 130.1 %while.13 = (bf16[1,2048,2560]{2,1,0:T(8,128)(2,1)}, bf16[1,2048,896]{1,2,0:T(8,128)(2,1)}, f32[2560,56]{0,1:T(8,128)S(1)}, f32[2560,56]{0,1:T(8,128)}, u32[]{:T...) while((bf16[1,2048,2560]{2,1,0:T(8,128)(2,1)}, ...), condition=%wide.windowed_dot_general_cond_rs.1.clone, body=%wide.windowed_dot_general_body_rs.1.clone.sunk | while | flops 2351505408 | bytes 105579144 | solution.py:20
  1054.4 37.1 %all-reduce.10 = f32[]{:T(128)} all-reduce(f32[]{:T(128)S(6)} %add.180), channel_id=13, replica_groups=mesh['rep'=1,'dp'=16] {'dp'}, use_global_device_ids=true, to_apply=%region_3.4.clone | all-reduce | flops 1 | bytes 8 | tf_op jit(solution)/vmap()/reduce_sum | solution.py:54
  1104.3 44.3 %all-gather.14.cloned.1.call-done = bf16[1,2,2560,896]{3,2,1,0:T(8,128)(2,1)} async-done(((bf16[1,2,160,896]{3,2,1,0:T(8,128)(2,1)}), bf16[1,2,2560,896]{3,2,1,0:T(8,128)(2,1)}) %all-gather.14.cloned.1.call-update) | async-done | bytes 9175056 | tf_op jit(solution)/reshape | solution.py:58
  1148.7 54.2 %all-gather.12.cloned.1.call-done = bf16[1,2,896,2560]{3,2,1,0:T(8,128)(2,1)} async-done(((bf16[1,2,56,2560]{3,2,1,0:T(8,128)(2,1)}), bf16[1,2,896,2560]{3,2,1,0:T(8,128)(2,1)}) %all-gather.12.cloned.1.call-update) | async-done | bytes 9175056 | tf_op jit(solution)/reshape | solution.py:58
  1202.9 54.2 %all-gather.10.cloned.1.call-done = bf16[1,2,896,2560]{3,2,1,0:T(8,128)(2,1)} async-done(((bf16[1,2,56,2560]{3,2,1,0:T(8,128)(2,1)}), bf16[1,2,896,2560]{3,2,1,0:T(8,128)(2,1)}) %all-gather.10.cloned.1.call-update) | async-done | bytes 9175056 | tf_op jit(solution)/reshape | solution.py:58
  (499 shorter events, 822.0 us)
Async XLA Ops:
  7.2 1141.5 %all-gather.14.cloned.1.call-start = ((), (), s32[]{:S(2)}) async-start(), calls=%async_computation.2 | async-start | bytes 9748480 | tf_op jit(solution)/reshape | solution.py:58
  149.9 16.1 %collective-permute-start.18 = (f32[160,896]{1,0:T(8,128)S(1)}, f32[160,896]{1,0:T(8,128)S(1)}, u32[]{:S(2)}, u32[]{:S(2)}) collective-permute-start(f32[160,896]{1,0:T(8,128)S(1)} %get-tuple-element.492), channel_id=31, source_target_pairs={{0,1},{1,2},{2,3},{3,4},{4,5},{5,6},{6,7},{7,8},{8,9},{9,10},{10,1... | collective-permute-start | bytes 1720328 | tf_op jit(solution)/vmap(transpose(jvp()))/dot_general | solution.py:9
  261.5 775.3 %collective-permute-start.28 = (f32[160,896]{1,0:T(8,128)}, f32[160,896]{1,0:T(8,128)}, u32[]{:S(2)}, u32[]{:S(2)}) collective-permute-start(f32[160,896]{1,0:T(8,128)} %get-tuple-element.45), channel_id=32, source_target_pairs={{0,1},{1,2},{2,3},{3,4},{4,5},{5,6},{6,7},{7,8},{8,9},{9,10},{10,1... | collective-permute-start | bytes 1720328 | tf_op jit(solution)/vmap(transpose(jvp()))/dot_general | solution.py:9
  370.5 16.1 %collective-permute-start.22 = (f32[896,160]{0,1:T(8,128)S(1)}, f32[896,160]{0,1:T(8,128)S(1)}, u32[]{:S(2)}, u32[]{:S(2)}) collective-permute-start(f32[896,160]{0,1:T(8,128)S(1)} %get-tuple-element.501), channel_id=37, source_target_pairs={{0,1},{1,2},{2,3},{3,4},{4,5},{5,6},{6,7},{7,8},{8,9},{9,10},{10,1... | collective-permute-start | bytes 1720328 | tf_op jit(solution)/vmap(transpose(jvp()))/dot_general | solution.py:9
  480.8 557.2 %collective-permute-start.29 = (f32[896,160]{0,1:T(8,128)}, f32[896,160]{0,1:T(8,128)}, u32[]{:S(2)}, u32[]{:S(2)}) collective-permute-start(f32[896,160]{0,1:T(8,128)} %get-tuple-element.47), channel_id=38, source_target_pairs={{0,1},{1,2},{2,3},{3,4},{4,5},{5,6},{6,7},{7,8},{8,9},{9,10},{10,1... | collective-permute-start | bytes 1720328 | tf_op jit(solution)/vmap(transpose(jvp()))/dot_general | solution.py:9
  500.3 13.9 %collective-permute-start.10 = (f32[2560,56]{0,1:T(8,128)S(1)}, f32[2560,56]{0,1:T(8,128)S(1)}, u32[]{:S(2)}, u32[]{:S(2)}) collective-permute-start(f32[2560,56]{0,1:T(8,128)S(1)} %get-tuple-element.474), channel_id=18, source_target_pairs={{0,1},{1,2},{2,3},{3,4},{4,5},{5,6},{6,7},{7,8},{8,9},{9,10},{10,1... | collective-permute-start | bytes 1720328 | tf_op jit(solution)/vmap(transpose(jvp()))/dot_general | solution.py:21
  552.6 14.3 %collective-permute-start.8 = (f32[2560,56]{0,1:T(8,128)S(1)}, f32[2560,56]{0,1:T(8,128)S(1)}, u32[]{:S(2)}, u32[]{:S(2)}) collective-permute-start(f32[2560,56]{0,1:T(8,128)S(1)} %broadcast_select_fusion.28), channel_id=16, source_target_pairs={{0,1},{1,2},{2,3},{3,4},{4,5},{5,6},{6,7},{7,8},{8,9},{9,10},{10,1... | collective-permute-start | bytes 1720328 | tf_op jit(solution)/vmap(transpose(jvp()))/dot_general | solution.py:21
  583.0 14.3 %collective-permute-start.8 = (f32[2560,56]{0,1:T(8,128)S(1)}, f32[2560,56]{0,1:T(8,128)S(1)}, u32[]{:S(2)}, u32[]{:S(2)}) collective-permute-start(f32[2560,56]{0,1:T(8,128)S(1)} %broadcast_select_fusion.28), channel_id=16, source_target_pairs={{0,1},{1,2},{2,3},{3,4},{4,5},{5,6},{6,7},{7,8},{8,9},{9,10},{10,1... | collective-permute-start | bytes 1720328 | tf_op jit(solution)/vmap(transpose(jvp()))/dot_general | solution.py:21
  613.6 426.6 %collective-permute-start.26 = (f32[2560,56]{0,1:T(8,128)}, f32[2560,56]{0,1:T(8,128)}, u32[]{:S(2)}, u32[]{:S(2)}) collective-permute-start(f32[2560,56]{0,1:T(8,128)} %get-tuple-element.41), channel_id=19, source_target_pairs={{0,1},{1,2},{2,3},{3,4},{4,5},{5,6},{6,7},{7,8},{8,9},{9,10},{10,1... | collective-permute-start | bytes 1720328 | tf_op jit(solution)/vmap(transpose(jvp()))/dot_general | solution.py:21
  664.8 13.3 %collective-permute-start.14 = (f32[2560,56]{0,1:T(8,128)S(1)}, f32[2560,56]{0,1:T(8,128)S(1)}, u32[]{:S(2)}, u32[]{:S(2)}) collective-permute-start(f32[2560,56]{0,1:T(8,128)S(1)} %get-tuple-element.483), channel_id=24, source_target_pairs={{0,1},{1,2},{2,3},{3,4},{4,5},{5,6},{6,7},{7,8},{8,9},{9,10},{10,1... | collective-permute-start | bytes 1720328 | tf_op jit(solution)/vmap(transpose(jvp()))/dot_general | solution.py:21
  713.9 15.0 %collective-permute-start.12 = (f32[2560,56]{0,1:T(8,128)S(1)}, f32[2560,56]{0,1:T(8,128)S(1)}, u32[]{:S(2)}, u32[]{:S(2)}) collective-permute-start(f32[2560,56]{0,1:T(8,128)S(1)} %broadcast_select_fusion.30), channel_id=22, source_target_pairs={{0,1},{1,2},{2,3},{3,4},{4,5},{5,6},{6,7},{7,8},{8,9},{9,10},{10,1... | collective-permute-start | bytes 1720328 | tf_op jit(solution)/vmap(transpose(jvp()))/dot_general | solution.py:21
  745.3 15.0 %collective-permute-start.12 = (f32[2560,56]{0,1:T(8,128)S(1)}, f32[2560,56]{0,1:T(8,128)S(1)}, u32[]{:S(2)}, u32[]{:S(2)}) collective-permute-start(f32[2560,56]{0,1:T(8,128)S(1)} %broadcast_select_fusion.30), channel_id=22, source_target_pairs={{0,1},{1,2},{2,3},{3,4},{4,5},{5,6},{6,7},{7,8},{8,9},{9,10},{10,1... | collective-permute-start | bytes 1720328 | tf_op jit(solution)/vmap(transpose(jvp()))/dot_general | solution.py:21
  776.1 14.3 %collective-permute-start = (f32[2560,56]{0,1:T(8,128)S(1)}, f32[2560,56]{0,1:T(8,128)S(1)}, u32[]{:S(2)}, u32[]{:S(2)}) collective-permute-start(f32[2560,56]{0,1:T(8,128)S(1)} %broadcast_select_fusion.24), channel_id=3, source_target_pairs={{0,1},{1,2},{2,3},{3,4},{4,5},{5,6},{6,7},{7,8},{8,9},{9,10},{10,1... | collective-permute-start | bytes 1720328 | tf_op jit(solution)/vmap(transpose(jvp()))/dot_general | solution.py:20
  805.3 14.3 %collective-permute-start = (f32[2560,56]{0,1:T(8,128)S(1)}, f32[2560,56]{0,1:T(8,128)S(1)}, u32[]{:S(2)}, u32[]{:S(2)}) collective-permute-start(f32[2560,56]{0,1:T(8,128)S(1)} %broadcast_select_fusion.24), channel_id=3, source_target_pairs={{0,1},{1,2},{2,3},{3,4},{4,5},{5,6},{6,7},{7,8},{8,9},{9,10},{10,1... | collective-permute-start | bytes 1720328 | tf_op jit(solution)/vmap(transpose(jvp()))/dot_general | solution.py:20
  835.4 14.3 %collective-permute-start = (f32[2560,56]{0,1:T(8,128)S(1)}, f32[2560,56]{0,1:T(8,128)S(1)}, u32[]{:S(2)}, u32[]{:S(2)}) collective-permute-start(f32[2560,56]{0,1:T(8,128)S(1)} %broadcast_select_fusion.24), channel_id=3, source_target_pairs={{0,1},{1,2},{2,3},{3,4},{4,5},{5,6},{6,7},{7,8},{8,9},{9,10},{10,1... | collective-permute-start | bytes 1720328 | tf_op jit(solution)/vmap(transpose(jvp()))/dot_general | solution.py:20
  865.4 14.3 %collective-permute-start = (f32[2560,56]{0,1:T(8,128)S(1)}, f32[2560,56]{0,1:T(8,128)S(1)}, u32[]{:S(2)}, u32[]{:S(2)}) collective-permute-start(f32[2560,56]{0,1:T(8,128)S(1)} %broadcast_select_fusion.24), channel_id=3, source_target_pairs={{0,1},{1,2},{2,3},{3,4},{4,5},{5,6},{6,7},{7,8},{8,9},{9,10},{10,1... | collective-permute-start | bytes 1720328 | tf_op jit(solution)/vmap(transpose(jvp()))/dot_general | solution.py:20
  897.0 14.9 %collective-permute-start.4 = (f32[2560,56]{0,1:T(8,128)}, f32[2560,56]{0,1:T(8,128)S(1)}, u32[]{:S(2)}, u32[]{:S(2)}) collective-permute-start(f32[2560,56]{0,1:T(8,128)} %broadcast_select_fusion.26), channel_id=9, source_target_pairs={{0,1},{1,2},{2,3},{3,4},{4,5},{5,6},{6,7},{7,8},{8,9},{9,10},{10,1... | collective-permute-start | bytes 1720328 | tf_op jit(solution)/vmap(transpose(jvp()))/dot_general | solution.py:20
  930.4 14.9 %collective-permute-start.4 = (f32[2560,56]{0,1:T(8,128)}, f32[2560,56]{0,1:T(8,128)S(1)}, u32[]{:S(2)}, u32[]{:S(2)}) collective-permute-start(f32[2560,56]{0,1:T(8,128)} %broadcast_select_fusion.26), channel_id=9, source_target_pairs={{0,1},{1,2},{2,3},{3,4},{4,5},{5,6},{6,7},{7,8},{8,9},{9,10},{10,1... | collective-permute-start | bytes 1720328 | tf_op jit(solution)/vmap(transpose(jvp()))/dot_general | solution.py:20
  963.0 14.9 %collective-permute-start.4 = (f32[2560,56]{0,1:T(8,128)}, f32[2560,56]{0,1:T(8,128)S(1)}, u32[]{:S(2)}, u32[]{:S(2)}) collective-permute-start(f32[2560,56]{0,1:T(8,128)} %broadcast_select_fusion.26), channel_id=9, source_target_pairs={{0,1},{1,2},{2,3},{3,4},{4,5},{5,6},{6,7},{7,8},{8,9},{9,10},{10,1... | collective-permute-start | bytes 1720328 | tf_op jit(solution)/vmap(transpose(jvp()))/dot_general | solution.py:20
  995.6 14.9 %collective-permute-start.4 = (f32[2560,56]{0,1:T(8,128)}, f32[2560,56]{0,1:T(8,128)S(1)}, u32[]{:S(2)}, u32[]{:S(2)}) collective-permute-start(f32[2560,56]{0,1:T(8,128)} %broadcast_select_fusion.26), channel_id=9, source_target_pairs={{0,1},{1,2},{2,3},{3,4},{4,5},{5,6},{6,7},{7,8},{8,9},{9,10},{10,1... | collective-permute-start | bytes 1720328 | tf_op jit(solution)/vmap(transpose(jvp()))/dot_general | solution.py:20
  1026.3 15.0 %collective-permute-start.27 = (f32[2560,56]{0,1:T(8,128)}, f32[2560,56]{0,1:T(8,128)}, u32[]{:S(2)}, u32[]{:S(2)}) collective-permute-start(f32[2560,56]{0,1:T(8,128)} %get-tuple-element.43), channel_id=25, source_target_pairs={{0,1},{1,2},{2,3},{3,4},{4,5},{5,6},{6,7},{7,8},{8,9},{9,10},{10,1... | collective-permute-start | bytes 1720328 | tf_op jit(solution)/vmap(transpose(jvp()))/dot_general | solution.py:21
  1036.9 14.6 %collective-permute-start.25 = (f32[2560,56]{0,1:T(8,128)}, f32[2560,56]{0,1:T(8,128)S(1)}, u32[]{:S(2)}, u32[]{:S(2)}) collective-permute-start(f32[2560,56]{0,1:T(8,128)} %get-tuple-element.39), channel_id=12, source_target_pairs={{0,1},{1,2},{2,3},{3,4},{4,5},{5,6},{6,7},{7,8},{8,9},{9,10},{10,1... | collective-permute-start | bytes 1720328 | tf_op jit(solution)/vmap(transpose(jvp()))/dot_general | solution.py:20
  1096.3 106.5 %all-gather.12.cloned.1.call-start = ((), (), s32[]{:S(2)}) async-start(), calls=%async_computation.1 | async-start | bytes 9748480 | tf_op jit(solution)/reshape | solution.py:58
  1100.0 157.0 %all-gather.10.cloned.1.call-start = ((), (), s32[]{:S(2)}) async-start(), calls=%async_computation | async-start | bytes 9748480 | tf_op jit(solution)/reshape | solution.py:58
  (136 other events, 1920.4 us)
Sparse Core Ops, SparseCore 0:
  1096.5 52.1 all-gather.13
  1151.5 51.3 all-gather.11
  1205.7 51.3 all-gather.9
where the time goes:
time: 1300 us; the launch traced here: 1290 us
  starting transfers between devices  379 us (29%)
  matrix products  379 us (29%)
  waiting for transfers between devices  319 us (25%)
  other arithmetic  81.6 us (6%)
  local copies, waits for them, and re-layouts  72.7 us (6%)
  blocking collectives  37.1 us (3%)
  between operations  17.1 us (1%)
    reshape x3, waiting for transfers between devices, step(): t.reshape(-1, *t.shape[2:])  153 us
    dot_general x19, matrix products, matmul(): jnp.dot(a, w, preferred_element_type=jnp.float32).astype(jnp.bfloat16)  138 us
    dot_general x34, starting transfers between devices, matmul(): jnp.dot(a, w, preferred_element_type=jnp.float32).astype(jnp.bfloat16)  130 us
    dot_general x34, starting transfers between devices, layer(): up = jnp.dot(a, w['w_up'], preferred_element_type=jnp.float32)  129 us
    dot_general x19, matrix products, layer(): up = jnp.dot(a, w['w_up'], preferred_element_type=jnp.float32)  127 us
    dot_general x34, starting transfers between devices, layer(): gate = jnp.dot(a, w['w_gate'], preferred_element_type=jnp.float32)  120 us
    dot_general x19, matrix products, layer(): gate = jnp.dot(a, w['w_gate'], preferred_element_type=jnp.float32)  114 us
    unnamed x54, local copies, waits for them, and re-layouts  72.6 us
  transfers between devices with their start and end apart: 105, of which 76 were waited for; matrix products, arithmetic and copies ran while one was open for 28% of the time, Pallas kernels for 0%

commit v1 on v0

v1 whole, which is shorter than its diff:
```python
import jax
import jax.numpy as jnp
from jax import lax
from jax.sharding import PartitionSpec as P

NAMES = ("w_gate", "w_up", "w_down")
DEVICES = 16


def matmul(a, w):
    return jnp.dot(a, w, preferred_element_type=jnp.float32).astype(jnp.bfloat16)


def normed(h):
    wide = h.astype(jnp.float32)
    scale = lax.rsqrt(jnp.mean(wide**2, -1, keepdims=True) + 1e-6)
    return (wide * scale).astype(jnp.bfloat16)


def layer(h, w):
    a = normed(h)
    gate = jnp.dot(a, w["w_gate"], preferred_element_type=jnp.float32)
    up = jnp.dot(a, w["w_up"], preferred_element_type=jnp.float32)
    return h + matmul((jax.nn.silu(gate) * up).astype(jnp.bfloat16), w["w_down"])


def adamw(w, m, v, g):
    m = 0.9 * m + 0.1 * g
    v = 0.95 * v + 0.05 * g * g
    step = m * lax.rsqrt(v + 1e-8) + 0.1 * w
    return (w - 0.02 * step).astype(jnp.bfloat16), m, v


def solution(mesh):
    def step(x, dy, wg, wu, wd, *moments):
        m, v = moments[:3], moments[3:]
        layers = [dict(zip(NAMES, (wg[i], wu[i], wd[i]), strict=True)) for i in range(2)]
        h = x[0]
        backs = []
        for w in layers:
            h, back = jax.vjp(layer, h, w)
            backs.append(back)
        shards = [None, None]
        d = dy[0]
        for i in (1, 0):
            d, dw = backs[i](d)
            shards[i] = [lax.psum_scatter(dw[n], "dp", scatter_dimension=0, tiled=True) for n in NAMES]
        g = [jnp.stack([shards[0][k], shards[1][k]]).astype(jnp.float32) for k in range(3)]
        total = lax.psum(sum(jnp.sum(t * t) for t in g), "dp")
        count = sum(t.size for t in g) * DEVICES
        factor = jnp.minimum(1.0, 0.5 * lax.rsqrt(total / count + 1e-30))
        me = lax.axis_index("dp")
        news, ms, vs = [], [], []
        for k, w in enumerate((wg, wu, wd)):
            rows = w.shape[1] // DEVICES
            own = lax.dynamic_slice_in_dim(w, me * rows, rows, 1).astype(jnp.float32)
            nw, nm, nv = adamw(own, m[k], v[k], g[k] * factor)
            news.append(lax.all_gather(nw, "dp", axis=1, tiled=True))
            ms.append(nm)
            vs.append(nv)
        return (*news, *ms, *vs)

    seq = P(("rep", "dp"), None, None)
    whole = P(None, None, None)
    part = P(None, "dp", None)
    return jax.shard_map(
        step,
        mesh=mesh,
        in_specs=(seq, seq, whole, whole, whole) + (part,) * 6,
        out_specs=(P("rep", None, None),) * 3 + (P("rep", "dp", None),) * 6,
        check_vma=False,
    )
```

time: 1300 us -> 834 us (0.64)
  starting transfers between devices: 379 us -> 0.37 us
  waiting for transfers between devices: 319 us -> 420 us
  matrix products: 379 us -> 294 us
  other arithmetic: 81.6 us -> 21.5 us
  local copies, waits for them, and re-layouts: 72.7 us -> 39.4 us
    dot_general x102 -> x0, starting transfers between devices: 379 us -> none  [the longest x34 130 us: matmul(): jnp.dot(a, w, preferred_element_type=jnp.float32).astype(jnp.bfloat16)]
    reduce_scatter x0 -> x6, waiting for transfers between devices: none -> 266 us  [step(): lax.psum_scatter(dw[n], 'dp', scatter_dimension=0, tiled=True)]
    dot_general x102 -> x0, waiting for transfers between devices: 166 us -> none  [the longest x34 61.1 us: layer(): gate = jnp.dot(a, w['w_gate'], preferred_element_type=jnp.float32)]
    all_gather x0 -> x3, waiting for transfers between devices: none -> 154 us  [step(): news.append(lax.all_gather(nw, 'dp', axis=1, tiled=True))]
    reshape x3 -> x0, waiting for transfers between devices: 153 us -> none  [step(): t.reshape(-1, *t.shape[2:])]
    dot_general x19 -> x5, matrix products: 138 us -> 84.4 us  [matmul(): jnp.dot(a, w, preferred_element_type=jnp.float32).astype(jnp.bfloat16)]
    dot_general x96 -> x0, other arithmetic: 50.8 us -> none
    reduce_sum x1 -> x0, blocking collectives: 37.1 us -> none  [of_a_group(): jnp.sum(g * g)]
  transfers between devices with their start and end apart: 105 -> 9, of which waited for: 76 -> 8; matrix products, arithmetic and copies ran while one was open for 28% -> 15% of each run, Pallas kernels for 0% -> 0%
where the time goes in v1:
time: 834 us; the launch traced here: 826 us
  waiting for transfers between devices  420 us (50%)
  matrix products  294 us (35%)
  local copies, waits for them, and re-layouts  39.4 us (5%)
  blocking collectives  32.6 us (4%)
  other arithmetic  21.5 us (3%)
  between operations  17.1 us (2%)
    reduce_scatter x6, waiting for transfers between devices, step(): lax.psum_scatter(dw[n], 'dp', scatter_dimension=0, tiled=True)  266 us
    all_gather x3, waiting for transfers between devices, step(): news.append(lax.all_gather(nw, 'dp', axis=1, tiled=True))  154 us
    dot_general x5, matrix products, layer(): gate = jnp.dot(a, w['w_gate'], preferred_element_type=jnp.float32)  112 us
    dot_general x5, matrix products, layer(): up = jnp.dot(a, w['w_up'], preferred_element_type=jnp.float32)  97.3 us
    dot_general x5, matrix products, matmul(): jnp.dot(a, w, preferred_element_type=jnp.float32).astype(jnp.bfloat16)  84.4 us
    unnamed x31, local copies, waits for them, and re-layouts  39.4 us
    psum x1, blocking collectives, step(): total = lax.psum(sum((jnp.sum(t * t) for t in g)), 'dp')  32.6 us
  transfers between devices with their start and end apart: 9, of which 8 were waited for; matrix products, arithmetic and copies ran while one was open for 15% of the time, Pallas kernels for 0%

profile of v1, /device:TPU:0, one launch (start us, length us, event | category | flops | bytes accessed | tf_op | source)
XLA Modules:
  0.0 825.6 jit_solution(14655270285962992490)
XLA Ops:
  22.2 16.5 %convolution_convert_fusion.1 = bf16[2048,2560]{1,0:T(8,128)(2,1)} fusion(bf16[2,2560,896]{2,1,0:T(8,128)(2,1)} %param.15, bf16[1,2048,896]{2,1,0:T(8,128)(2,1)} %param.12), kind=kOutput, calls=%fused_computation.27 | convolution fusion | flops 9400483840 | bytes 18743296 | tf_op jit(solution)/shard_map/transpose(jvp())/dot_general | solution.py:11
  38.7 17.1 %fusion.41 = f32[2048,2560]{1,0:T(8,128)} fusion(bf16[2,896,2560]{2,1,0:T(8,128)(2,1)} %param.13, bf16[1,2048,896]{2,1,0:T(8,128)(2,1)S(1)} %copy-done.2, f32[2048]{0:T(1024)S(1)} %add_rsqrt_fusion), kind=kOutput, calls=%fused_computation.60 | convolution fusion | flops 9400745984 | bytes 29237248 | tf_op jit(solution)/shard_map/jvp()/dot_general | solution.py:22
  55.8 24.9 %multiply_convert_fusion.1 = (bf16[2048,2560]{1,0:T(8,128)(2,1)}, f32[2048,2560]{1,0:T(8,128)}) fusion(f32[2048,2560]{1,0:T(8,128)} %fusion.41, bf16[2,896,2560]{2,1,0:T(8,128)(2,1)} %param.14, bf16[1,2048,896]{2,1,0:T(8,128)(2,1)S(1)} %copy-done.2, f32[2048]{0:T(1024)S(1)} %add_rsqrt_fusion), kind=kOutput, calls=%fused_computation.17 | convolution fusion | flops 9432203264 | bytes 60694528 | tf_op jit(solution)/shard_map/jvp()/dot_general | solution.py:23
  80.7 14.6 %fusion.19 = (f32[2048]{0:T(1024)S(1)}, bf16[2048,896]{0,1:T(8,128)(2,1)S(1)}) fusion(bf16[2048,2560]{1,0:T(8,128)(2,1)} %get-tuple-element.18, bf16[2,2560,896]{2,1,0:T(8,128)(2,1)} %param.15, bf16[1,2048,896]{1,2,0:T(8,128)(2,1)S(1)} %copy-done), kind=kOutput, calls=%fused_computation.37 | convolution fusion | flops 9404413952 | bytes 22421504 | tf_op jit(solution)/shard_map/jvp()/dot_general | solution.py:11
  97.1 17.0 %fusion.28 = f32[2048,2560]{1,0:T(8,128)} fusion(bf16[2,896,2560]{2,1,0:T(8,128)(2,1)} %param.14, bf16[2048,896]{0,1:T(8,128)(2,1)S(1)} %get-tuple-element.21, f32[2048]{0:T(1024)S(1)} %fusion.90), kind=kOutput, calls=%fused_computation.47 | convolution fusion | flops 9400745984 | bytes 29237248 | tf_op jit(solution)/shard_map/jvp()/dot_general | solution.py:23
  114.1 40.0 %fusion.2 = (bf16[2048,2560]{1,0:T(8,128)(2,1)}, f32[2048,2560]{1,0:T(8,128)}) fusion(f32[2048,2560]{1,0:T(8,128)} %fusion.28, bf16[2048,2560]{1,0:T(8,128)(2,1)} %convolution_convert_fusion.1, bf16[2,896,2560]{2,1,0:T(8,128)(2,1)} %param.13, bf16[2048,896]{0,1:T(8,128)(2,1)} %copy-done.3, f32[2048]{0:T(1024)S(1)} %fusion.90), kind=kOutput, calls=%fused_computation.8 | convolution fusion | flops 9463660544 | bytes 71180288 | tf_op jit(solution)/shard_map/jvp()/dot_general | solution.py:22
  154.1 18.1 %fusion.12 = bf16[2048,896]{0,1:T(8,128)(2,1)} fusion(bf16[2048,2560]{1,0:T(8,128)(2,1)} %convolution_convert_fusion.1, bf16[2,896,2560]{2,1,0:T(8,128)(2,1)} %param.14, f32[2048,2560]{1,0:T(8,128)} %get-tuple-element.23), kind=kOutput, calls=%fused_computation.21 | convolution fusion | flops 9426698240 | bytes 39714816 | tf_op jit(solution)/shard_map/transpose(jvp())/dot_general | solution.py:23
  172.2 16.2 %fusion.21 = (f32[2048]{0:T(1024)S(1)}, bf16[2048,896]{0,1:T(8,128)(2,1)S(1)}) fusion(bf16[2048,896]{0,1:T(8,128)(2,1)} %copy-done.3, bf16[2048,896]{0,1:T(8,128)(2,1)} %fusion.12, bf16[2048,2560]{1,0:T(8,128)(2,1)} %get-tuple-element.22, bf16[2,896,2560]{2,1,0:T(8,128)(2,1)} %param.13), kind=kOutput, calls=%fused_computation.39 | convolution fusion | flops 9404413952 | bytes 26091520 | tf_op jit(solution)/shard_map/transpose(jvp())/dot_general | solution.py:22
  193.4 15.2 %convolution_convert_fusion.2 = bf16[2560,896]{1,0:T(8,128)(2,1)} fusion(bf16[2048,2560]{1,0:T(8,128)(2,1)} %get-tuple-element.18, bf16[2048,896]{0,1:T(8,128)(2,1)S(1)} %fusion.53), kind=kOutput, calls=%fused_computation.45 | convolution fusion | flops 9397534720 | bytes 18743296 | tf_op jit(solution)/shard_map/transpose(jvp())/dot_general | solution.py:11
  208.7 21.6 %fusion.27 = bf16[2560,896]{1,0:T(8,128)(2,1)} fusion(f32[2048,2560]{1,0:T(8,128)} %fusion.28, bf16[1,2048,896]{2,1,0:T(8,128)(2,1)} %param.12, f32[2048,2560]{1,0:T(8,128)} %get-tuple-element.23), kind=kOutput, calls=%fused_computation.44 | convolution fusion | flops 9428992000 | bytes 50200576 | tf_op jit(solution)/shard_map/transpose(jvp())/dot_general | solution.py:11
  230.3 16.5 %convolution_convert_fusion = bf16[2048,2560]{1,0:T(8,128)(2,1)} fusion(bf16[2048,896]{0,1:T(8,128)(2,1)} %copy-done.5, bf16[2,2560,896]{2,1,0:T(8,128)(2,1)} %param.15), kind=kOutput, calls=%fused_computation.26 | convolution fusion | flops 9400483840 | bytes 18743296 | tf_op jit(solution)/shard_map/transpose(jvp())/dot_general | solution.py:11
  246.9 18.5 %fusion.26 = bf16[896,2560]{1,0:T(8,128)(2,1)} fusion(bf16[2048,2560]{1,0:T(8,128)(2,1)} %convolution_convert_fusion, f32[2048,2560]{1,0:T(8,128)} %fusion.41, bf16[1,2048,896]{1,2,0:T(8,128)(2,1)} %copy.20, f32[2048]{0:T(1024)S(1)} %copy-done.12), kind=kOutput, calls=%fused_computation.43 | convolution fusion | flops 9434497024 | bytes 39723008 | tf_op jit(solution)/shard_map/transpose(jvp())/dot_general | solution.py:23
  265.4 18.7 %fusion.25 = bf16[896,2560]{1,0:T(8,128)(2,1)} fusion(bf16[2048,2560]{1,0:T(8,128)(2,1)} %convolution_convert_fusion.1, bf16[2048,896]{0,1:T(8,128)(2,1)} %copy-done.3, f32[2048]{0:T(1024)S(1)} %fusion.90, f32[2048,2560]{1,0:T(8,128)} %get-tuple-element.23), kind=kOutput, calls=%fused_computation.42 | convolution fusion | flops 9434497024 | bytes 39723008 | tf_op jit(solution)/shard_map/transpose(jvp())/dot_general | solution.py:23
  284.2 24.1 %fusion.22 = bf16[896,2560]{1,0:T(8,128)(2,1)} fusion(f32[2048,2560]{1,0:T(8,128)} %fusion.41, f32[2048,2560]{1,0:T(8,128)} %get-tuple-element.19, bf16[2048,2560]{1,0:T(8,128)(2,1)} %convolution_convert_fusion, bf16[1,2048,896]{1,2,0:T(8,128)(2,1)} %copy.20, f32[2048]{0:T(1024)S(1)} %copy-done.12), kind=kOutput, calls=%fused_computation.41 | convolution fusion | flops 9460711424 | bytes 60694528 | tf_op jit(solution)/shard_map/transpose(jvp())/dot_general | solution.py:22
  308.4 15.1 %convolution_convert_fusion.3 = bf16[896,2560]{1,0:T(8,128)(2,1)} fusion(bf16[2048,2560]{1,0:T(8,128)(2,1)} %get-tuple-element.22, bf16[2048,896]{0,1:T(8,128)(2,1)} %copy-done.3, f32[2048]{0:T(1024)S(1)} %fusion.90), kind=kOutput, calls=%fused_computation.46 | convolution fusion | flops 9400745984 | bytes 18751488 | tf_op jit(solution)/shard_map/transpose(jvp())/dot_general | solution.py:22
  323.6 13.0 %reduce-scatter.17.cloned.1.call-done = bf16[160,896]{1,0:T(8,128)(2,1)} async-done(((bf16[2560,896]{1,0:T(8,128)(2,1)}), bf16[160,896]{1,0:T(8,128)(2,1)}) %reduce-scatter.17.cloned.1.call-update) | async-done | bytes 286736 | tf_op jit(solution)/shard_map/reduce_scatter | solution.py:47
  338.5 60.9 %reduce-scatter.11.cloned.1.call-done = bf16[56,2560]{1,0:T(8,128)(2,1)} async-done(((bf16[896,2560]{1,0:T(8,128)(2,1)}), bf16[56,2560]{1,0:T(8,128)(2,1)}) %reduce-scatter.11.cloned.1.call-update) | async-done | bytes 286736 | tf_op jit(solution)/shard_map/reduce_scatter | solution.py:47
  399.4 65.1 %reduce-scatter.13.cloned.1.call-done = bf16[56,2560]{1,0:T(8,128)(2,1)} async-done(((bf16[896,2560]{1,0:T(8,128)(2,1)}), bf16[56,2560]{1,0:T(8,128)(2,1)}) %reduce-scatter.13.cloned.1.call-update) | async-done | bytes 286736 | tf_op jit(solution)/shard_map/reduce_scatter | solution.py:47
  466.5 62.8 %reduce-scatter.7.cloned.1.call-done = bf16[56,2560]{1,0:T(8,128)(2,1)} async-done(((bf16[896,2560]{1,0:T(8,128)(2,1)}), bf16[56,2560]{1,0:T(8,128)(2,1)}) %reduce-scatter.7.cloned.1.call-update) | async-done | bytes 286736 | tf_op jit(solution)/shard_map/reduce_scatter | solution.py:47
  529.3 64.6 %reduce-scatter.9.cloned.1.call-done = bf16[56,2560]{1,0:T(8,128)(2,1)} async-done(((bf16[896,2560]{1,0:T(8,128)(2,1)}), bf16[56,2560]{1,0:T(8,128)(2,1)}) %reduce-scatter.9.cloned.1.call-update) | async-done | bytes 286736 | tf_op jit(solution)/shard_map/reduce_scatter | solution.py:47
  597.7 32.6 %psum.7 = f32[]{:T(128)} all-reduce(f32[]{:T(128)S(6)} %add.104), channel_id=1, replica_groups=mesh['rep'=1,'dp'=16] {'dp'}, use_global_device_ids=true, to_apply=%region_12.13 | all-reduce | flops 1 | bytes 8 | tf_op jit(solution)/shard_map/psum | solution.py:49
  641.1 45.4 %all-gather.8.cloned.1.call-done = bf16[2,2560,896]{2,1,0:T(8,128)(2,1)} async-done(((bf16[2,160,896]{2,1,0:T(8,128)(2,1)}), bf16[2,2560,896]{2,1,0:T(8,128)(2,1)}) %all-gather.8.cloned.1.call-update) | async-done | bytes 9175056 | tf_op jit(solution)/shard_map/all_gather | solution.py:58
  686.5 54.2 %all-gather.6.cloned.1.call-done = bf16[2,896,2560]{2,1,0:T(8,128)(2,1)} async-done(((bf16[2,56,2560]{2,1,0:T(8,128)(2,1)}), bf16[2,896,2560]{2,1,0:T(8,128)(2,1)}) %all-gather.6.cloned.1.call-update) | async-done | bytes 9175056 | tf_op jit(solution)/shard_map/all_gather | solution.py:58
  740.7 54.2 %all-gather.4.cloned.1.call-done = bf16[2,896,2560]{2,1,0:T(8,128)(2,1)} async-done(((bf16[2,56,2560]{2,1,0:T(8,128)(2,1)}), bf16[2,896,2560]{2,1,0:T(8,128)(2,1)}) %all-gather.4.cloned.1.call-update) | async-done | bytes 9175056 | tf_op jit(solution)/shard_map/all_gather | solution.py:58
  (61 shorter events, 61.5 us)
Async XLA Ops:
  7.2 316.4 %reduce-scatter.15.cloned.1.call-start = ((), (), s32[]{:S(2)}) async-start(), calls=%async_computation.10 | async-start | bytes 4874240 | tf_op jit(solution)/shard_map/reduce_scatter | solution.py:47
  16.1 39.7 %copy-start.11 = (f32[2048]{0:T(1024)}, f32[2048]{0:T(1024)S(1)}, u32[]{:S(2)}) copy-start(f32[2048]{0:T(1024)S(1)} %add_rsqrt_fusion) | copy-start | bytes 24580
  22.2 16.5 %copy-start.2 = (bf16[1,2048,896]{2,1,0:T(8,128)(2,1)S(1)}, bf16[1,2048,896]{2,1,0:T(8,128)(2,1)}, u32[]{:S(2)}) copy-start(bf16[1,2048,896]{2,1,0:T(8,128)(2,1)} %param.11) | copy-start | bytes 11010052
  55.8 24.9 %copy-start = (bf16[1,2048,896]{1,2,0:T(8,128)(2,1)S(1)}, bf16[1,2048,896]{1,2,0:T(8,128)(2,1)}, u32[]{:S(2)}) copy-start(bf16[1,2048,896]{1,2,0:T(8,128)(2,1)} %copy.20) | copy-start | bytes 11010052
  95.3 1.8 copy-start.3
  172.2 16.3 %copy-start.1 = (bf16[1,2048,896]{1,2,0:T(8,128)(2,1)S(1)}, bf16[1,2048,896]{1,2,0:T(8,128)(2,1)}, u32[]{:S(2)}) copy-start(bf16[1,2048,896]{1,2,0:T(8,128)(2,1)} %copy.21) | copy-start | bytes 11010052
  172.2 16.3 %copy-start.4 = (bf16[2048,896]{0,1:T(8,128)(2,1)S(1)}, bf16[2048,896]{0,1:T(8,128)(2,1)}, u32[]{:S(2)}) copy-start(bf16[2048,896]{0,1:T(8,128)(2,1)} %copy-done.3) | copy-start | bytes 11010052
  191.5 1.8 copy-start.5
  208.6 128.0 %reduce-scatter.17.cloned.1.call-start = ((), (), s32[]{:S(2)}) async-start(), calls=%async_computation.11 | async-start | bytes 4874240 | tf_op jit(solution)/shard_map/reduce_scatter | solution.py:47
  230.3 16.6 %copy-start.12 = (f32[2048]{0:T(1024)S(1)}, f32[2048]{0:T(1024)}, u32[]{:S(2)}) copy-start(f32[2048]{0:T(1024)} %copy-done.11) | copy-start | bytes 24580
  230.3 169.1 %reduce-scatter.11.cloned.1.call-start = ((), (), s32[]{:S(2)}) async-start(), calls=%async_computation.8 | async-start | bytes 4874240 | tf_op jit(solution)/shard_map/reduce_scatter | solution.py:47
  265.4 199.1 %reduce-scatter.13.cloned.1.call-start = ((), (), s32[]{:S(2)}) async-start(), calls=%async_computation.9 | async-start | bytes 4874240 | tf_op jit(solution)/shard_map/reduce_scatter | solution.py:47
  284.2 245.1 %reduce-scatter.7.cloned.1.call-start = ((), (), s32[]{:S(2)}) async-start(), calls=%async_computation.6 | async-start | bytes 4874240 | tf_op jit(solution)/shard_map/reduce_scatter | solution.py:47
  308.3 285.5 %reduce-scatter.9.cloned.1.call-start = ((), (), s32[]{:S(2)}) async-start(), calls=%async_computation.7 | async-start | bytes 4874240 | tf_op jit(solution)/shard_map/reduce_scatter | solution.py:47
  323.5 307.6 %copy-start.6 = (f32[2,160,896]{2,1,0:T(8,128)S(1)}, f32[2,160,896]{2,1,0:T(8,128)}, u32[]{:S(2)}) copy-start(f32[2,160,896]{2,1,0:T(8,128)} %param.21) | copy-start | bytes 3440644
  323.5 307.6 %copy-start.7 = (f32[2,160,896]{2,1,0:T(8,128)S(1)}, f32[2,160,896]{2,1,0:T(8,128)}, u32[]{:S(2)}) copy-start(f32[2,160,896]{2,1,0:T(8,128)} %param.18) | copy-start | bytes 3440644
  323.5 310.7 %copy-start.8 = (f32[2,56,2560]{2,1,0:T(8,128)S(1)}, f32[2,56,2560]{2,1,0:T(8,128)}, u32[]{:S(2)}) copy-start(f32[2,56,2560]{2,1,0:T(8,128)} %param.20) | copy-start | bytes 3440644
  323.5 363.0 %all-gather.8.cloned.1.call-start = ((), (), s32[]{:S(2)}) async-start(), calls=%async_computation.14 | async-start | bytes 9748480 | tf_op jit(solution)/shard_map/all_gather | solution.py:58
  634.1 3.8 copy-start.9
  634.1 3.8 copy-start.10
  634.2 106.5 %all-gather.6.cloned.1.call-start = ((), (), s32[]{:S(2)}) async-start(), calls=%async_computation.13 | async-start | bytes 9748480 | tf_op jit(solution)/shard_map/all_gather | solution.py:58
  637.9 157.0 %all-gather.4.cloned.1.call-start = ((), (), s32[]{:S(2)}) async-start(), calls=%async_computation.12 | async-start | bytes 9748480 | tf_op jit(solution)/shard_map/all_gather | solution.py:58
Sparse Core Ops, SparseCore 0:
  208.7 64.0 reduce-scatter.14
  275.1 61.4 reduce-scatter.16
  338.9 60.4 reduce-scatter.10
  402.1 62.3 reduce-scatter.12
  467.2 61.9 reduce-scatter.6
  532.0 61.7 reduce-scatter.8
  634.3 52.1 all-gather.7
  689.3 51.3 all-gather.5
  743.5 51.3 all-gather.3

commit v2 on v1

v2 whole, which is shorter than its diff:
```python
import functools

import jax
import jax.numpy as jnp
from jax import lax
from jax.experimental import pallas as pl
from jax.experimental.pallas import tpu as pltpu
from jax.sharding import PartitionSpec as P

MESH = pl.DeviceIdType.MESH
F32, BF16 = jnp.float32, jnp.bfloat16
DEVICES, TOKENS, D, FF = 16, 2048, 896, 2560
COUNT = 2 * 3 * D * FF
TM = 256
NB = 256
ANY = pl.BlockSpec(memory_space=pl.ANY)
WHOLE = pl.BlockSpec(memory_space=pltpu.VMEM)

STRIDE = (8, 4, 2)
ORDER = ((0, 1, 2), (1, 2, 0), (2, 0, 1))
WIDE = (56, 2560, tuple((slice(0, 56), s) for s in (slice(0, 896), slice(896, 1792), slice(1792, 2560))))
TALL = (160, 896, tuple((s, slice(0, 896)) for s in (slice(0, 56), slice(56, 112), slice(112, 160))))


def size(s):
    return s.stop - s.start


def place():
    me = lax.axis_index("dp")
    return me, (me // 8 % 2, me // 4 % 2, me // 2 % 2), me % 2


def beside(me, xyz, axis):
    return me + STRIDE[axis] * (1 - 2 * xyz[axis])


def partner(me, core):
    return me + 1 - 2 * core


def rs_scratch(kind):
    r, c, parts = kind
    flat = [pltpu.VMEM((8, r, c), BF16), pltpu.VMEM((8, r, c), BF16)]
    for rows, cols in parts:
        flat += [pltpu.VMEM((7, size(rows), size(cols)), BF16)] * 2
    return flat + [pltpu.SemaphoreType.DMA((10,)), pltpu.SemaphoreType.DMA((10,)), pltpu.SemaphoreType.DMA(())]


RS_SCRATCH = 11


class Reduce:
    def __init__(self, kind, g, out, scratch):
        self.kind, self.g, self.out = kind, g, out
        self.own, self.other = scratch[:2]
        self.send, self.got = scratch[2:8:2], scratch[3:8:2]
        self.ssem, self.rsem, self.lsem = scratch[8:]
        self.me, self.xyz, self.core = place()

    def swap(self):
        return pltpu.make_async_remote_copy(
            self.g.at[:, 1 - self.core],
            self.other,
            self.ssem.at[9],
            self.rsem.at[9],
            device_id={"dp": partner(self.me, self.core)},
            device_id_type=MESH,
        )

    def load(self):
        return pltpu.make_async_copy(self.g.at[:, self.core], self.own, self.lsem)

    def hop(self, t, phase):
        at = pl.ds((0, 4, 6)[phase], (4, 2, 1)[phase])
        return pltpu.make_async_remote_copy(
            self.send[t].at[at],
            self.got[t].at[at],
            self.ssem.at[3 * t + phase],
            self.rsem.at[3 * t + phase],
            device_id={"dp": beside(self.me, self.xyz, ORDER[t][phase])},
            device_id_type=MESH,
        )

    def total(self, t, at, got):
        rows, cols = self.kind[2][t]
        block = sum(p * (4, 2, 1)[axis] for p, axis in zip(at, ORDER[t], strict=True))
        sum_ = self.own[block, rows, cols].astype(F32) + self.other[block, rows, cols].astype(F32)
        for i in got:
            sum_ = sum_ + self.got[t][i].astype(F32)
        return sum_

    def start(self):
        self.swap().start()
        self.load().start()

    def stage(self, n):
        if n == 0:
            self.load().wait()
            self.swap().wait_recv()
        for t in range(3):
            p1, p2, p3 = (self.xyz[axis] for axis in ORDER[t])
            if n:
                self.hop(t, n - 1).wait_recv()
            if n == 0:
                for j in range(2):
                    for k in range(2):
                        self.send[t][2 * j + k] = self.total(t, (1 - p1, j, k), ()).astype(BF16)
            elif n == 1:
                for k in range(2):
                    self.send[t][4 + k] = self.total(t, (p1, 1 - p2, k), (2 * (1 - p2) + k,)).astype(BF16)
            elif n == 2:
                self.send[t][6] = self.total(t, (p1, p2, 1 - p3), (2 * p2 + 1 - p3, 5 - p3)).astype(BF16)
            else:
                rows, cols = self.kind[2][t]
                self.out[rows, cols] = self.total(t, (p1, p2, p3), (2 * p2 + p3, 4 + p3, 6)).astype(BF16)
            if n < 3:
                self.hop(t, n).start()

    def finish(self):
        self.swap().wait_send()
        for t in range(3):
            for phase in range(3):
                self.hop(t, phase).wait_send()


def squares(g):
    wide = g.astype(F32)
    rows, cols = wide.shape
    s = jnp.sum((wide * wide).reshape(rows // 8, 8, cols), 0)
    return sum(s[:, i : i + 128] for i in range(0, cols, 128))


def clip_factor(shards, factor, squared, sums, ssem, rsem):
    me = lax.axis_index("dp")
    squared[...] = sum(squares(g[...]) for g in shards)

    def give(k, slot):
        to = (me + k) % DEVICES
        return pltpu.make_async_remote_copy(
            squared, sums.at[slot], ssem.at[k], rsem.at[slot], device_id={"dp": to}, device_id_type=MESH
        )

    for k in range(1, DEVICES):
        give(k, me).start()
    sums[me] = squared[...]
    for k in range(1, DEVICES):
        give(k, (me + k) % DEVICES).wait_recv()
    for k in range(1, DEVICES):
        give(k, me).wait_send()
    total = jnp.sum(jnp.sum(jnp.sum(sums[...], 0), 0, keepdims=True), 1, keepdims=True)
    f = jnp.minimum(1.0, 0.5 * lax.rsqrt(total / COUNT + 1e-30))
    factor[...] = jnp.broadcast_to(f, factor.shape)


def reduce_kernel(kinds, earlier, *refs):
    n = len(kinds)
    grads, before, outs, factor = refs[:n], refs[n : n + earlier], refs[n + earlier : 2 * n + earlier], refs[2 * n + earlier]
    scratch = refs[2 * n + earlier + 1 :]
    units = [
        Reduce(kinds[i], grads[i], outs[i], scratch[RS_SCRATCH * i : RS_SCRATCH * (i + 1)]) for i in range(n)
    ]
    for u in units:
        u.start()
    for s in range(4):
        for u in units:
            u.stage(s)
    for u in units:
        u.finish()
    clip_factor([*before, *outs], factor, *scratch[RS_SCRATCH * n :])


def reduce_scatter(kinds, grads, before):
    scratch = sum((rs_scratch(k) for k in kinds), [])
    scratch += [
        pltpu.VMEM((8, 128), F32),
        pltpu.VMEM((DEVICES, 8, 128), F32),
        pltpu.SemaphoreType.DMA((DEVICES,)),
        pltpu.SemaphoreType.DMA((DEVICES,)),
    ]
    return pl.pallas_call(
        functools.partial(reduce_kernel, kinds, len(before)),
        out_shape=[jax.ShapeDtypeStruct(k[:2], BF16) for k in kinds] + [jax.ShapeDtypeStruct((8, 128), F32)],
        in_specs=[ANY] * len(kinds) + [WHOLE] * len(before),
        out_specs=[WHOLE] * (len(kinds) + 1),
        scratch_shapes=scratch,
        compiler_params=pltpu.CompilerParams(has_side_effects=True, vmem_limit_bytes=60 * 1024 * 1024),
        name="reduce_scatter",
    )(*[g.reshape(8, 2, *k[:2]) for g, k in zip(grads, kinds, strict=True)], *before)


class Gather:
    def __init__(self, kind, own, out, layer, ssem, rsem, csem):
        self.kind, self.own, self.out, self.layer = kind, own, out, layer
        self.ssem, self.rsem, self.csem = ssem, rsem, csem
        self.me, self.xyz, self.core = place()

    def local(self):
        x, y, z = self.xyz
        return pltpu.make_async_copy(self.own, self.out.at[self.layer, x, y, z, self.core], self.csem)

    def blocks(self, t, core, known, other=None):
        rows, cols = self.kind[2][t]
        index = []
        for axis in range(3):
            p = self.xyz[axis]
            index.append(slice(None) if axis in known else (1 - p if axis == other else p))
        return self.out.at[(self.layer, *index, core, rows, cols)]

    def hop(self, t, phase, arriving=False):
        axis = ORDER[t][phase]
        known = ORDER[t][:phase]
        src = self.blocks(t, self.core, known)
        dst = self.blocks(t, self.core, known, axis) if arriving else src
        if phase == 0 and not arriving:
            src = self.own.at[self.kind[2][t]]
        return pltpu.make_async_remote_copy(
            src,
            dst,
            self.ssem.at[3 * t + phase],
            self.rsem.at[3 * t + phase],
            device_id={"dp": beside(self.me, self.xyz, axis)},
            device_id_type=MESH,
        )

    def share(self, t, phase, core):
        ref = self.blocks(t, core, ORDER[t][:phase], ORDER[t][phase])
        return pltpu.make_async_remote_copy(
            ref,
            ref,
            self.ssem.at[10 + 3 * t + phase],
            self.rsem.at[10 + 3 * t + phase],
            device_id={"dp": partner(self.me, self.core)},
            device_id_type=MESH,
        )

    def share_own(self, core):
        x, y, z = self.xyz
        return pltpu.make_async_remote_copy(
            self.own,
            self.out.at[self.layer, x, y, z, core],
            self.ssem.at[9],
            self.rsem.at[9],
            device_id={"dp": partner(self.me, self.core)},
            device_id_type=MESH,
        )

    def start(self):
        self.local().start()
        for t in range(3):
            self.hop(t, 0).start()
        self.share_own(self.core).start()

    def stage(self, phase):
        if phase == 0:
            self.local().wait()
        for t in range(3):
            self.hop(t, phase, True).wait_recv()
            if phase < 2:
                self.hop(t, phase + 1).start()
            self.share(t, phase, self.core).start()

    def finish(self):
        self.share_own(1 - self.core).wait_recv()
        self.share_own(self.core).wait_send()
        for t in range(3):
            for phase in range(3):
                self.share(t, phase, 1 - self.core).wait_recv()
                self.share(t, phase, self.core).wait_send()
                self.hop(t, phase).wait_send()


def gather_kernel(*refs):
    owns, outs, (ssem, rsem, csem) = refs[:3], refs[3:6], refs[6:]
    units = []
    for layer in range(2):
        for i, kind in enumerate((WIDE, WIDE, TALL)):
            u = 3 * layer + i
            units.append(Gather(kind, owns[i].at[layer], outs[i], layer, ssem.at[u], rsem.at[u], csem.at[u]))
    for u in units:
        u.start()
    for phase in range(3):
        for u in units:
            u.stage(phase)
    for u in units:
        u.finish()


def all_gather(owns):
    outs = pl.pallas_call(
        gather_kernel,
        out_shape=[jax.ShapeDtypeStruct((2, 2, 2, 2, 2, *o.shape[1:]), BF16) for o in owns],
        in_specs=[WHOLE] * 3,
        out_specs=[ANY] * 3,
        scratch_shapes=[
            pltpu.SemaphoreType.DMA((6, 19)),
            pltpu.SemaphoreType.DMA((6, 19)),
            pltpu.SemaphoreType.DMA((6,)),
        ],
        compiler_params=pltpu.CompilerParams(has_side_effects=True),
        name="all_gather",
    )(*owns)
    return [o.reshape(2, DEVICES * o.shape[-2], o.shape[-1]) for o in outs]


def dot(a, b):
    return jnp.dot(a, b, preferred_element_type=F32)


def dot_t(a, b):
    return lax.dot_general(a, b, (((1,), (1,)), ((), ())), preferred_element_type=F32)


def norm(h):
    wide = h.astype(F32)
    scale = lax.rsqrt(jnp.mean(wide * wide, -1, keepdims=True) + 1e-6)
    return wide, scale, (wide * scale).astype(BF16)


def gated_back(gate, up, dact):
    sig = jax.nn.sigmoid(gate)
    d = dact.astype(F32)
    dup = d * (gate * sig)
    dgate = d * up * (sig * (1 + gate * (1 - sig)))
    return dgate.astype(BF16), dup.astype(BF16)


def forward_kernel(x, wg, wu, wd, h1, at, act, gate, up):
    h = x[...]
    _, _, a = norm(h)
    at[...] = a.T
    g = dot(a, wg[...])
    u = dot(a, wu[...])
    gate[...] = g
    up[...] = u
    s = (g * jax.nn.sigmoid(g) * u).astype(BF16)
    act[...] = s
    h1[...] = h + dot(s, wd[...]).astype(BF16)


def last_kernel(h1, dy, wg, wu, wd, at, dyt, act, dgate, dup):
    _, _, a = norm(h1[...])
    at[...] = a.T
    dyt[...] = dy[...].T
    g = dot(a, wg[...])
    u = dot(a, wu[...])
    act[...] = (g * jax.nn.sigmoid(g) * u).astype(BF16)
    dact = dot_t(dy[...], wd[...]).astype(BF16)
    dgate[...], dup[...] = gated_back(g, u, dact)


def between_kernel(dg1, du1, h1, dy, gate, up, wg, wu, wd, dht, dgate, dup):
    da = dot_t(dg1[...], wg[...]).astype(BF16) + dot_t(du1[...], wu[...]).astype(BF16)
    wide, scale, _ = norm(h1[...])
    d = da.astype(F32)
    through = d * scale - wide * (scale * scale * scale * (jnp.sum(d * wide, -1, keepdims=True) / D))
    dh = dy[...] + through.astype(BF16)
    dht[...] = dh.T
    dact = dot_t(dh, wd[...]).astype(BF16)
    dgate[...], dup[...] = gated_back(gate[...], up[...], dact)


def rows(cols):
    return pl.BlockSpec((TM, cols), lambda i: (i, 0))


SEQ = pl.BlockSpec((None, TM, D), lambda i: (0, i, 0))
COLUMNS = pl.BlockSpec((D, TM), lambda i: (0, i))


def weight(layer, shape):
    return pl.BlockSpec((None, *shape), lambda i: (layer, 0, 0), pipeline_mode=pl.Buffered(1))


def matrix(r, c, t=BF16):
    return jax.ShapeDtypeStruct((r, c), t)


def cost(matmuls):
    return pl.CostEstimate(flops=matmuls * 2 * TOKENS * D * FF, bytes_accessed=60 << 20, transcendentals=0)


def params():
    return pltpu.CompilerParams(vmem_limit_bytes=60 * 1024 * 1024)


def forward(x, wg, wu, wd):
    return pl.pallas_call(
        forward_kernel,
        grid=(TOKENS // TM,),
        in_specs=[SEQ, weight(0, (D, FF)), weight(0, (D, FF)), weight(0, (FF, D))],
        out_specs=[rows(D), COLUMNS, rows(FF), rows(FF), rows(FF)],
        out_shape=[matrix(TOKENS, D), matrix(D, TOKENS), matrix(TOKENS, FF), matrix(TOKENS, FF, F32), matrix(TOKENS, FF, F32)],
        compiler_params=params(),
        cost_estimate=cost(3),
        name="forward",
    )(x, wg, wu, wd)


def last(h1, dy, wg, wu, wd):
    return pl.pallas_call(
        last_kernel,
        grid=(TOKENS // TM,),
        in_specs=[rows(D), SEQ, weight(1, (D, FF)), weight(1, (D, FF)), weight(1, (FF, D))],
        out_specs=[COLUMNS, COLUMNS, rows(FF), rows(FF), rows(FF)],
        out_shape=[matrix(D, TOKENS)] * 2 + [matrix(TOKENS, FF)] * 3,
        compiler_params=params(),
        cost_estimate=cost(3),
        name="last",
    )(h1, dy, wg, wu, wd)


def between(dg1, du1, h1, dy, gate, up, wg, wu, wd):
    return pl.pallas_call(
        between_kernel,
        grid=(TOKENS // TM,),
        in_specs=[rows(FF), rows(FF), rows(D), SEQ, rows(FF), rows(FF)]
        + [weight(1, (D, FF)), weight(1, (D, FF)), weight(0, (FF, D))],
        out_specs=[COLUMNS, rows(FF), rows(FF)],
        out_shape=[matrix(D, TOKENS)] + [matrix(TOKENS, FF)] * 2,
        compiler_params=params(),
        cost_estimate=cost(3),
        name="between",
    )(dg1, du1, h1, dy, gate, up, wg, wu, wd)


def wide_kernel(at, dg, du, og, ou):
    og[...] = dot(at[...], dg[...]).astype(BF16)
    ou[...] = dot(at[...], du[...]).astype(BF16)


def tall_kernel(dt, act, o):
    o[...] = dot(dt[...], act[...]).astype(BF16).T


WHOLE_T = pl.BlockSpec((D, TOKENS), lambda i: (0, 0), pipeline_mode=pl.Buffered(1))
BY_COLUMN = pl.BlockSpec((TOKENS, NB), lambda i: (0, i))


def wide_gradients(at, dg, du):
    out = pl.BlockSpec((D, NB), lambda i: (0, i))
    return pl.pallas_call(
        wide_kernel,
        grid=(FF // NB,),
        in_specs=[WHOLE_T, BY_COLUMN, BY_COLUMN],
        out_specs=[out, out],
        out_shape=[matrix(D, FF)] * 2,
        compiler_params=params(),
        cost_estimate=cost(2),
        name="wide_gradients",
    )(at, dg, du)


def tall_gradient(dt, act):
    return pl.pallas_call(
        tall_kernel,
        grid=(FF // NB,),
        in_specs=[WHOLE_T, BY_COLUMN],
        out_specs=pl.BlockSpec((NB, D), lambda i: (i, 0)),
        out_shape=matrix(FF, D),
        compiler_params=params(),
        cost_estimate=cost(1),
        name="tall_gradient",
    )(dt, act)


def adamw(w, m, v, g):
    m = 0.9 * m + 0.1 * g
    v = 0.95 * v + 0.05 * g * g
    step = m * lax.rsqrt(v + 1e-8) + 0.1 * w
    return (w - 0.02 * step).astype(BF16), m, v


def solution(mesh):
    def step(x, dy, wg, wu, wd, *moments):
        h1, a0, act0, gate0, up0 = forward(x, wg, wu, wd)
        a1, dyt, act1, dg1, du1 = last(h1, dy, wg, wu, wd)
        gd1 = tall_gradient(dyt, act1)
        gg1, gu1 = wide_gradients(a1, dg1, du1)
        dht, dg0, du0 = between(dg1, du1, h1, dy, gate0, up0, wg, wu, wd)
        gd0 = tall_gradient(dht, act0)
        gg0, gu0 = wide_gradients(a0, dg0, du0)
        r1 = reduce_scatter((TALL, WIDE, WIDE), (gd1, gg1, gu1), ())
        d1, g1, u1 = r1[:3]
        d0, g0, u0, factor = reduce_scatter((TALL, WIDE, WIDE), (gd0, gg0, gu0), (d1, g1, u1))
        shards = [jnp.stack(pair).astype(F32) for pair in ((g0, g1), (u0, u1), (d0, d1))]
        me = lax.axis_index("dp")
        f = factor[0, 0]
        new = []
        for k, w in enumerate((wg, wu, wd)):
            r = w.shape[1] // DEVICES
            own = lax.dynamic_slice_in_dim(w, me * r, r, 1).astype(F32)
            new.append(adamw(own, moments[k], moments[3 + k], shards[k] * f))
        gathered = all_gather([n[0] for n in new])
        return (*gathered, *(n[1] for n in new), *(n[2] for n in new))

    seq = P(("rep", "dp"), None, None)
    whole = P(None, None, None)
    part = P(None, "dp", None)
    return jax.shard_map(
        step,
        mesh=mesh,
        in_specs=(seq, seq, whole, whole, whole) + (part,) * 6,
        out_specs=(P("rep", None, None),) * 3 + (P("rep", "dp", None),) * 6,
        check_vma=False,
    )
```

time: 834 us -> 478 us (0.57)
  Pallas kernels: 0 us -> 441 us
  waiting for transfers between devices: 420 us -> 0 us
  matrix products: 294 us -> 0 us
  blocking collectives: 32.6 us -> 0 us
  between operations: 17.1 us -> 0.72 us
  local copies, waits for them, and re-layouts: 39.4 us -> 24.9 us
  other arithmetic: 21.5 us -> 10.5 us
    pallas_call x0 -> x10, Pallas kernels: none -> 441 us  [the longest x2 124 us: reduce_scatter(): pl.pallas_call(functools.partial(reduce_kernel, kinds, len(before)), out_...]
    dot_general x15 -> x0, matrix products: 294 us -> none  [the longest x5 112 us: layer(): gate = jnp.dot(a, w['w_gate'], preferred_element_type=jnp.float32)]
    reduce_scatter x6 -> x0, waiting for transfers between devices: 266 us -> none  [step(): lax.psum_scatter(dw[n], 'dp', scatter_dimension=0, tiled=True)]
    all_gather x3 -> x0, waiting for transfers between devices: 154 us -> none  [step(): news.append(lax.all_gather(nw, 'dp', axis=1, tiled=True))]
    psum x1 -> x0, blocking collectives: 32.6 us -> none  [step(): total = lax.psum(sum((jnp.sum(t * t) for t in g)), 'dp')]
    unnamed x31 -> x15, local copies, waits for them, and re-layouts: 39.4 us -> 23.7 us
    reduce_sum x4 -> x0, other arithmetic: 8.64 us -> none  [the longest x3 5.83 us: step(): total = lax.psum(sum((jnp.sum(t * t) for t in g)), 'dp')]
  transfers between devices with their start and end apart: 9 -> 0, of which waited for: 8 -> 0; matrix products, arithmetic and copies ran while one was open for 15% -> 0% of each run, Pallas kernels for 0% -> 0%
where the time goes in v2:
time: 478 us; the launch traced here: 477 us
  Pallas kernels  441 us (92%)
  local copies, waits for them, and re-layouts  24.9 us (5%)
  other arithmetic  10.5 us (2%)
    pallas_call x2, Pallas kernels, reduce_scatter(): pl.pallas_call(functools.partial(reduce_kernel, kinds, len(before)), out_...  124 us
    pallas_call x1, Pallas kernels, all_gather(): pl.pallas_call(gather_kernel, out_shape=[jax.ShapeDtypeStruct((2, 2, 2, 2...  99.6 us
    pallas_call x1, Pallas kernels, between(): pl.pallas_call(between_kernel, grid=(TOKENS // TM,), in_specs=[rows(FF),...  49.6 us
    pallas_call x2, Pallas kernels, wide_gradients(): pl.pallas_call(wide_kernel, grid=(FF // NB,), in_specs=[WHOLE_T, BY_COLUM...  48.9 us
    pallas_call x1, Pallas kernels, last(): pl.pallas_call(last_kernel, grid=(TOKENS // TM,), in_specs=[rows(D), SEQ,...  44.4 us
    pallas_call x1, Pallas kernels, forward(): pl.pallas_call(forward_kernel, grid=(TOKENS // TM,), in_specs=[SEQ, weigh...  42.5 us
    pallas_call x2, Pallas kernels, tall_gradient(): pl.pallas_call(tall_kernel, grid=(FF // NB,), in_specs=[WHOLE_T, BY_COLUM...  31.9 us
    unnamed x15, local copies, waits for them, and re-layouts  23.7 us

profile of v2, /device:TPU:0, one launch (start us, length us, event | category | flops | bytes accessed | tf_op | source)
XLA Modules:
  0.0 477.1 jit_solution(15663725955390333353)
XLA Ops:
  0.6 42.5 %forward.1 = (bf16[2048,896]{1,0:T(8,128)(2,1)}, bf16[896,2048]{1,0:T(8,128)(2,1)}, bf16[2048,2560]{1,0:T(8,128)(2,1)}, f32[2048,2560]{1,0:T(8,128)}, f32[2048,2560]{1,0:T(8,128)}) custom-call(bf16[1,2048,896]{2,1,0:T(8,128)(2,1)} %x.1, bf16[2,896,2560]{2,1,0:T(8,128)(2,1)} %wg.5, bf16[2,896,2560]{2,1,0:T(8,128)(2,1)} %wu.5, bf16[2,2560,896]{2,1,0:T(8,128)(2,1)} %wd.5), custom_call_target="tpu_custom_call" | custom-call | flops 28185722880 | bytes 62914560 | tf_op jit(solution)/shard_map/forward/pallas_call | solution.py:388
  43.2 44.4 %last.1 = (bf16[896,2048]{1,0:T(8,128)(2,1)}, bf16[896,2048]{1,0:T(8,128)(2,1)}, bf16[2048,2560]{1,0:T(8,128)(2,1)}, bf16[2048,2560]{1,0:T(8,128)(2,1)}, bf16[2048,2560]{1,0:T(8,128)(2,1)}) custom-call(bf16[2048,896]{1,0:T(8,128)(2,1)} %get-tuple-element.36.h1, bf16[1,2048,896]{2,1,0:T(8,128)(2,1)} %dy.3, bf16[2,896,2560]{2,1,0:T(8,128)(2,1)} %wg.5, ...), custom_call_target="tpu_custom_call" | custom-call | flops 28185722880 | bytes 62914560 | tf_op jit(solution)/shard_map/last/pallas_call | solution.py:401
  87.6 24.5 %wide_gradients.3 = (bf16[896,2560]{1,0:T(8,128)(2,1)}, bf16[896,2560]{1,0:T(8,128)(2,1)}) custom-call(bf16[896,2048]{1,0:T(8,128)(2,1)} %get-tuple-element.50.at, bf16[2048,2560]{1,0:T(8,128)(2,1)} %get-tuple-element.37.dg1.dg, bf16[2048,2560]{1,0:T(8,128)(2,1)} %get-tuple-element.38.du1.du), custom_call_target="tpu_custom_call" | custom-call | flops 18790481920 | bytes 62914560 | tf_op jit(solution)/shard_map/wide_gradients/pallas_call | solution.py:442
  112.1 16.0 %tall_gradient.3 = bf16[2560,896]{1,0:T(8,128)(2,1)} custom-call(bf16[896,2048]{1,0:T(8,128)(2,1)} %get-tuple-element.48.dt, bf16[2048,2560]{1,0:T(8,128)(2,1)} %get-tuple-element.49.act), custom_call_target="tpu_custom_call" | custom-call | flops 9395240960 | bytes 62914560 | tf_op jit(solution)/shard_map/tall_gradient/pallas_call | solution.py:455
  128.0 63.1 %reduce_scatter.2 = (bf16[160,896]{1,0:T(8,128)(2,1)}, bf16[56,2560]{1,0:T(8,128)(2,1)}, bf16[56,2560]{1,0:T(8,128)(2,1)}, f32[8,128]{1,0:T(8,128)}) custom-call(bf16[8,2,160,896]{3,2,1,0:T(8,128)(2,1)} %bitcast.24, bf16[8,2,56,2560]{3,2,1,0:T(8,128)(2,1)} %bitcast.22, bf16[8,2,56,2560]{3,2,1,0:T(8,128)(2,1)} %bitcast.23), custom_call_target="tpu_custom_call" | custom-call | tf_op jit(solution)/shard_map/reduce_scatter/pallas_call | solution.py:181
  191.2 49.6 %between.1 = (bf16[896,2048]{1,0:T(8,128)(2,1)}, bf16[2048,2560]{1,0:T(8,128)(2,1)}, bf16[2048,2560]{1,0:T(8,128)(2,1)}) custom-call(bf16[2048,2560]{1,0:T(8,128)(2,1)} %get-tuple-element.37.dg1.dg, bf16[2048,2560]{1,0:T(8,128)(2,1)} %get-tuple-element.38.du1.du, bf16[2048,896]{1,0:T(8,128)(2,1)} %get-tuple-element.36.h1, bf16[1,2048,896]{2,1,0:T(8,128)(2,1)} %dy.3, ...), custom_call_target="tpu_custom_call" | custom-call | flops 28185722880 | bytes 62914560 | tf_op jit(solution)/shard_map/between/pallas_call | solution.py:414
  240.8 24.5 %wide_gradients.2 = (bf16[896,2560]{1,0:T(8,128)(2,1)}, bf16[896,2560]{1,0:T(8,128)(2,1)}) custom-call(bf16[896,2048]{1,0:T(8,128)(2,1)} %get-tuple-element.43.at, bf16[2048,2560]{1,0:T(8,128)(2,1)} %get-tuple-element.44.dg, bf16[2048,2560]{1,0:T(8,128)(2,1)} %get-tuple-element.45.du), custom_call_target="tpu_custom_call" | custom-call | flops 18790481920 | bytes 62914560 | tf_op jit(solution)/shard_map/wide_gradients/pallas_call | solution.py:442
  265.3 16.0 %tall_gradient.2 = bf16[2560,896]{1,0:T(8,128)(2,1)} custom-call(bf16[896,2048]{1,0:T(8,128)(2,1)} %get-tuple-element.41.dt, bf16[2048,2560]{1,0:T(8,128)(2,1)} %get-tuple-element.42.act), custom_call_target="tpu_custom_call" | custom-call | flops 9395240960 | bytes 62914560 | tf_op jit(solution)/shard_map/tall_gradient/pallas_call | solution.py:455
  281.2 60.8 %reduce_scatter.3 = (bf16[160,896]{1,0:T(8,128)(2,1)}, bf16[56,2560]{1,0:T(8,128)(2,1)}, bf16[56,2560]{1,0:T(8,128)(2,1)}, f32[8,128]{1,0:T(8,128)}) custom-call(bf16[8,2,160,896]{3,2,1,0:T(8,128)(2,1)} %bitcast.21, bf16[8,2,56,2560]{3,2,1,0:T(8,128)(2,1)} %bitcast.19, bf16[8,2,56,2560]{3,2,1,0:T(8,128)(2,1)} %bitcast.20, ...), custom_call_target="tpu_custom_call" | custom-call | tf_op jit(solution)/shard_map/reduce_scatter/pallas_call | solution.py:181
  342.1 1.2 slice.3
  343.3 0.0 copy-done.2
  343.3 0.0 copy-start.4
  343.3 0.0 copy-start.5
  343.3 4.6 fusion.8
  348.0 0.0 copy-done
  348.0 0.0 copy-done.1
  348.0 0.0 copy-done.3
  348.0 0.0 copy-done.4
  348.0 0.0 copy-done.5
  348.0 5.9 %fusion.2 = (bf16[2,56,2560]{2,1,0:T(8,128)(2,1)}, f32[2,56,2560]{2,1,0:T(8,128)}, f32[2,56,2560]{2,1,0:T(8,128)}, bf16[2,56,2560]{2,1,0:T(8,128)(2,1)}, f32[2,56,2560]{2,1,0:T(8,128)}, /*index=5*/f32[2,56,2560]{2,1,0:T(8,128)}) fusion(bf16[2,896,2560]{2,1,0:T(8,128)(2,1)} %wg.5, s32[]{:T(128)S(6)} %select_n.7, f32[]{:T(128)} %bitcast.8, ...), kind=kLoop, calls=%fused_computation.11 | loop fusion | flops 11468800 | bytes 12615688 | tf_op jit(solution)/shard_map/convert_element_type | solution.py:471
  353.9 99.6 %all_gather.1 = (bf16[2,2,2,2,2,56,2560]{6,5,4,3,2,1,0:T(8,128)(2,1)}, bf16[2,2,2,2,2,56,2560]{6,5,4,3,2,1,0:T(8,128)(2,1)}, bf16[2,2,2,2,2,160,896]{6,5,4,3,2,1,0:T(8,128)(2,1)}) custom-call(bf16[2,56,2560]{2,1,0:T(8,128)(2,1)} %get-tuple-element.69.refs_0_, bf16[2,56,2560]{2,1,0:T(8,128)(2,1)} %get-tuple-element.72.refs_1_, ...), custom_call_target="tpu_custom_call" | custom-call | tf_op jit(solution)/shard_map/all_gather/pallas_call | solution.py:290
  453.4 7.9 %copy.23 = bf16[2,896,2560]{2,1,0:T(8,128)(2,1)} copy(bf16[2,896,2560]{2,1,0:T(8,128)(2,1)} %bitcast.18) | data formatting | bytes 18350080
  461.3 7.8 %copy.24 = bf16[2,896,2560]{2,1,0:T(8,128)(2,1)} copy(bf16[2,896,2560]{2,1,0:T(8,128)(2,1)} %bitcast.17) | data formatting | bytes 18350080
  469.1 8.0 %copy.25 = bf16[2,2560,896]{2,1,0:T(8,128)(2,1)} copy(bf16[2,2560,896]{2,1,0:T(8,128)(2,1)} %bitcast.16) | data formatting | bytes 18350080
  (4 shorter events, 0.0 us)
Async XLA Ops:
  281.2 62.1 %copy-start.2 = (bf16[160,896]{1,0:T(8,128)(2,1)S(1)}, bf16[160,896]{1,0:T(8,128)(2,1)}, u32[]{:S(2)}) copy-start(bf16[160,896]{1,0:T(8,128)(2,1)} %get-tuple-element.53.refs_3_) | copy-start | bytes 860164
  343.3 4.7 copy-start
  343.3 4.7 copy-start.1
  343.3 4.7 copy-start.3
  343.3 4.7 copy-start.4
  343.3 4.7 copy-start.5

commit v3 on v2

--- a/solution.py
+++ b/solution.py
@@ -12,7 +12,8 @@
 DEVICES, TOKENS, D, FF = 16, 2048, 896, 2560
 COUNT = 2 * 3 * D * FF
 TM = 256
-NB = 256
+NB = 512
+STEPS = FF // NB
 ANY = pl.BlockSpec(memory_space=pl.ANY)
 WHOLE = pl.BlockSpec(memory_space=pltpu.VMEM)
 
@@ -39,9 +40,9 @@
     return me + 1 - 2 * core
 
 
-def rs_scratch(kind):
+def rs_scratch(kind, here):
     r, c, parts = kind
-    flat = [pltpu.VMEM((8, r, c), BF16), pltpu.VMEM((8, r, c), BF16)]
+    flat = [pltpu.VMEM((8, 2, r, c) if here else (8, r, c), BF16), pltpu.VMEM((8, r, c), BF16)]
     for rows, cols in parts:
         flat += [pltpu.VMEM((7, size(rows), size(cols)), BF16)] * 2
     return flat + [pltpu.SemaphoreType.DMA((10,)), pltpu.SemaphoreType.DMA((10,)), pltpu.SemaphoreType.DMA(())]
@@ -52,8 +53,9 @@
 
 class Reduce:
     def __init__(self, kind, g, out, scratch):
-        self.kind, self.g, self.out = kind, g, out
+        self.kind, self.out, self.here = kind, out, g is None
         self.own, self.other = scratch[:2]
+        self.g = self.own if self.here else g
         self.send, self.got = scratch[2:8:2], scratch[3:8:2]
         self.ssem, self.rsem, self.lsem = scratch[8:]
         self.me, self.xyz, self.core = place()
@@ -85,18 +87,21 @@
     def total(self, t, at, got):
         rows, cols = self.kind[2][t]
         block = sum(p * (4, 2, 1)[axis] for p, axis in zip(at, ORDER[t], strict=True))
-        sum_ = self.own[block, rows, cols].astype(F32) + self.other[block, rows, cols].astype(F32)
+        own = self.own[block, self.core, rows, cols] if self.here else self.own[block, rows, cols]
+        sum_ = own.astype(F32) + self.other[block, rows, cols].astype(F32)
         for i in got:
             sum_ = sum_ + self.got[t][i].astype(F32)
         return sum_
 
     def start(self):
         self.swap().start()
-        self.load().start()
+        if not self.here:
+            self.load().start()
 
     def stage(self, n):
         if n == 0:
-            self.load().wait()
+            if not self.here:
+                self.load().wait()
             self.swap().wait_recv()
         for t in range(3):
             p1, p2, p3 = (self.xyz[axis] for axis in ORDER[t])
@@ -153,40 +158,26 @@
     factor[...] = jnp.broadcast_to(f, factor.shape)
 
 
-def reduce_kernel(kinds, earlier, *refs):
-    n = len(kinds)
-    grads, before, outs, factor = refs[:n], refs[n : n + earlier], refs[n + earlier : 2 * n + earlier], refs[2 * n + earlier]
-    scratch = refs[2 * n + earlier + 1 :]
-    units = [
-        Reduce(kinds[i], grads[i], outs[i], scratch[RS_SCRATCH * i : RS_SCRATCH * (i + 1)]) for i in range(n)
-    ]
-    for u in units:
-        u.start()
-    for s in range(4):
-        for u in units:
-            u.stage(s)
-    for u in units:
-        u.finish()
-    clip_factor([*before, *outs], factor, *scratch[RS_SCRATCH * n :])
-
-
-def reduce_scatter(kinds, grads, before):
-    scratch = sum((rs_scratch(k) for k in kinds), [])
-    scratch += [
-        pltpu.VMEM((8, 128), F32),
-        pltpu.VMEM((DEVICES, 8, 128), F32),
-        pltpu.SemaphoreType.DMA((DEVICES,)),
-        pltpu.SemaphoreType.DMA((DEVICES,)),
-    ]
-    return pl.pallas_call(
-        functools.partial(reduce_kernel, kinds, len(before)),
-        out_shape=[jax.ShapeDtypeStruct(k[:2], BF16) for k in kinds] + [jax.ShapeDtypeStruct((8, 128), F32)],
-        in_specs=[ANY] * len(kinds) + [WHOLE] * len(before),
-        out_specs=[WHOLE] * (len(kinds) + 1),
-        scratch_shapes=scratch,
-        compiler_params=pltpu.CompilerParams(has_side_effects=True, vmem_limit_bytes=60 * 1024 * 1024),
-        name="reduce_scatter",
-    )(*[g.reshape(8, 2, *k[:2]) for g, k in zip(grads, kinds, strict=True)], *before)
+CLIP_SCRATCH = [
+    pltpu.VMEM((8, 128), F32),
+    pltpu.VMEM((DEVICES, 8, 128), F32),
+    pltpu.SemaphoreType.DMA((DEVICES,)),
+    pltpu.SemaphoreType.DMA((DEVICES,)),
+]
+
+
+def at_end_of(step, plan):
+    for when, entries in plan.items():
+
+        @pl.when(step == when)
+        def _(entries=entries):
+            for unit, stage in entries:
+                if stage == "start":
+                    unit.start()
+                elif stage == "finish":
+                    unit.finish()
+                else:
+                    unit.stage(stage)
 
 
 class Gather:
@@ -349,7 +340,15 @@
     dgate[...], dup[...] = gated_back(g, u, dact)
 
 
-def between_kernel(dg1, du1, h1, dy, gate, up, wg, wu, wd, dht, dgate, dup):
+def between_kernel(dg1, du1, h1, dy, gate, up, wg, wu, wd, gg, gu, dht, dgate, dup, og, ou, *scratch):
+    step = pl.program_id(0)
+    units = [Reduce(WIDE, gg, og, scratch[:RS_SCRATCH]), Reduce(WIDE, gu, ou, scratch[RS_SCRATCH:])]
+
+    @pl.when(step == 0)
+    def _():
+        for u in units:
+            u.start()
+
     da = dot_t(dg1[...], wg[...]).astype(BF16) + dot_t(du1[...], wu[...]).astype(BF16)
     wide, scale, _ = norm(h1[...])
     d = da.astype(F32)
@@ -358,6 +357,9 @@
     dht[...] = dh.T
     dact = dot_t(dh, wd[...]).astype(BF16)
     dgate[...], dup[...] = gated_back(gate[...], up[...], dact)
+    plan = {when: [(u, stage) for u in units] for when, stage in ((1, 0), (4, 1), (6, 2))}
+    plan[7] = [(u, stage) for stage in (3, "finish") for u in units]
+    at_end_of(step, plan)
 
 
 def rows(cols):
@@ -380,8 +382,8 @@
     return pl.CostEstimate(flops=matmuls * 2 * TOKENS * D * FF, bytes_accessed=60 << 20, transcendentals=0)
 
 
-def params():
-    return pltpu.CompilerParams(vmem_limit_bytes=60 * 1024 * 1024)
+def params(remote=False):
+    return pltpu.CompilerParams(vmem_limit_bytes=60 * 1024 * 1024, has_side_effects=remote)
 
 
 def forward(x, wg, wu, wd):
@@ -410,58 +412,123 @@
     )(h1, dy, wg, wu, wd)
 
 
-def between(dg1, du1, h1, dy, gate, up, wg, wu, wd):
+def shard(kind):
+    return pl.BlockSpec(kind[:2], lambda i: (0, 0))
+
+
+def between(dg1, du1, h1, dy, gate, up, wg, wu, wd, gg, gu):
     return pl.pallas_call(
         between_kernel,
         grid=(TOKENS // TM,),
         in_specs=[rows(FF), rows(FF), rows(D), SEQ, rows(FF), rows(FF)]
-        + [weight(1, (D, FF)), weight(1, (D, FF)), weight(0, (FF, D))],
-        out_specs=[COLUMNS, rows(FF), rows(FF)],
-        out_shape=[matrix(D, TOKENS)] + [matrix(TOKENS, FF)] * 2,
-        compiler_params=params(),
+        + [weight(1, (D, FF)), weight(1, (D, FF)), weight(0, (FF, D)), ANY, ANY],
+        out_specs=[COLUMNS, rows(FF), rows(FF), shard(WIDE), shard(WIDE)],
+        out_shape=[matrix(D, TOKENS)] + [matrix(TOKENS, FF)] * 2 + [matrix(*WIDE[:2])] * 2,
+        scratch_shapes=rs_scratch(WIDE, False) * 2,
+        compiler_params=params(True),
         cost_estimate=cost(3),
         name="between",
-    )(dg1, du1, h1, dy, gate, up, wg, wu, wd)
-
-
-def wide_kernel(at, dg, du, og, ou):
-    og[...] = dot(at[...], dg[...]).astype(BF16)
-    ou[...] = dot(at[...], du[...]).astype(BF16)
-
-
-def tall_kernel(dt, act, o):
-    o[...] = dot(dt[...], act[...]).astype(BF16).T
+    )(dg1, du1, h1, dy, gate, up, wg, wu, wd, gg, gu)
+
+
+def tall_into(g, i, dt, act):
+    g.reshape(FF, D)[pl.ds(pl.multiple_of(i * NB, NB), NB)] = dot(dt[...], act[...]).astype(BF16).T
+
+
+def wide_block(at, dg):
+    return dot(at[...], dg[...]).reshape(8, 2, 56, NB).astype(BF16)
+
+
+def upper_kernel(dt, at, act, dg, du, gg, gu, od, *scratch):
+    step = pl.program_id(0)
+    d = Reduce(TALL, None, od, scratch)
+
+    @pl.when(step < STEPS)
+    def _():
+        tall_into(d.g, step, dt, act)
+
+    @pl.when((step >= STEPS) & (step < 2 * STEPS))
+    def _():
+        gg[...] = wide_block(at, dg)
+
+    @pl.when(step >= 2 * STEPS)
+    def _():
+        gu[...] = wide_block(at, du)
+
+    at_end_of(step, {4: [(d, "start")], 6: [(d, 0)], 11: [(d, 1)], 13: [(d, 2)], 14: [(d, 3), (d, "finish")]})
+
+
+def lower_kernel(dt, at, act, dg, du, d1, g1, u1, od, og, ou, factor, *scratch):
+    step = pl.program_id(0)
+    d, g, u = (
+        Reduce(kind, None, o, scratch[RS_SCRATCH * i : RS_SCRATCH * (i + 1)])
+        for i, (kind, o) in enumerate(((TALL, od), (WIDE, og), (WIDE, ou)))
+    )
+
+    @pl.when(step < STEPS)
+    def _():
+        tall_into(d.g, step, dt, act)
+
+    def columns(first):
+        return pl.ds(pl.multiple_of((step - first) * NB, NB), NB)
+
+    @pl.when((step >= STEPS) & (step < 2 * STEPS))
+    def _():
+        g.g[:, :, :, columns(STEPS)] = wide_block(at, dg)
+
+    @pl.when(step >= 2 * STEPS)
+    def _():
+        u.g[:, :, :, columns(2 * STEPS)] = wide_block(at, du)
+
+    tail = [(u, "start"), (d, 3), (g, 1), (u, 0), (g, 2), (u, 1), (g, 3), (u, 2), (u, 3)]
+    at_end_of(
+        step,
+        {4: [(d, "start")], 6: [(d, 0)], 9: [(g, "start")], 11: [(d, 1), (g, 0)], 13: [(d, 2)]}
+        | {14: tail + [(unit, "finish") for unit in (d, g, u)]},
+    )
+
+    @pl.when(step == 3 * STEPS - 1)
+    def _():
+        clip_factor([d1, g1, u1, od, og, ou], factor, *scratch[3 * RS_SCRATCH :])
 
 
 WHOLE_T = pl.BlockSpec((D, TOKENS), lambda i: (0, 0), pipeline_mode=pl.Buffered(1))
-BY_COLUMN = pl.BlockSpec((TOKENS, NB), lambda i: (0, i))
-
-
-def wide_gradients(at, dg, du):
-    out = pl.BlockSpec((D, NB), lambda i: (0, i))
+
+
+def in_turn(turn, block, index):
+    return pl.BlockSpec(block, lambda i: index(jnp.clip(i - turn * STEPS, 0, STEPS - 1)))
+
+
+COLUMNS_IN_TURN = [in_turn(turn, (TOKENS, NB), lambda i: (0, i)) for turn in range(3)]
+
+
+def upper_gradients(dt, at, act, dg, du):
     return pl.pallas_call(
-        wide_kernel,
-        grid=(FF // NB,),
-        in_specs=[WHOLE_T, BY_COLUMN, BY_COLUMN],
-        out_specs=[out, out],
-        out_shape=[matrix(D, FF)] * 2,
-        compiler_params=params(),
-        cost_estimate=cost(2),
-        name="wide_gradients",
-    )(at, dg, du)
-
-
-def tall_gradient(dt, act):
+        upper_kernel,
+        grid=(3 * STEPS,),
+        in_specs=[WHOLE_T, WHOLE_T, *COLUMNS_IN_TURN],
+        out_specs=[in_turn(turn, (8, 2, 56, NB), lambda i: (0, 0, 0, i)) for turn in (1, 2)] + [shard(TALL)],
+        out_shape=[jax.ShapeDtypeStruct((8, 2, 56, FF), BF16)] * 2 + [matrix(*TALL[:2])],
+        scratch_shapes=rs_scratch(TALL, True),
+        compiler_params=params(True),
+        cost_estimate=cost(3),
+        name="upper_gradients",
+    )(dt, at, act, dg, du)
+
+
+def lower_gradients(dt, at, act, dg, du, before):
+    kinds = (TALL, WIDE, WIDE)
     return pl.pallas_call(
-        tall_kernel,
-        grid=(FF // NB,),
-        in_specs=[WHOLE_T, BY_COLUMN],
-        out_specs=pl.BlockSpec((NB, D), lambda i: (i, 0)),
-        out_shape=matrix(FF, D),
-        compiler_params=params(),
-        cost_estimate=cost(1),
-        name="tall_gradient",
-    )(dt, act)
+        lower_kernel,
+        grid=(3 * STEPS,),
+        in_specs=[WHOLE_T, WHOLE_T, *COLUMNS_IN_TURN] + [shard(k) for k in kinds],
+        out_specs=[shard(k) for k in kinds] + [pl.BlockSpec((8, 128), lambda i: (0, 0))],
+        out_shape=[matrix(*k[:2]) for k in kinds] + [matrix(8, 128, F32)],
+        scratch_shapes=sum((rs_scratch(k, True) for k in kinds), []) + CLIP_SCRATCH,
+        compiler_params=params(True),
+        cost_estimate=cost(3),
+        name="lower_gradients",
+    )(dt, at, act, dg, du, *before)
 
 
 def adamw(w, m, v, g):
@@ -475,14 +542,9 @@
     def step(x, dy, wg, wu, wd, *moments):
         h1, a0, act0, gate0, up0 = forward(x, wg, wu, wd)
         a1, dyt, act1, dg1, du1 = last(h1, dy, wg, wu, wd)
-        gd1 = tall_gradient(dyt, act1)
-        gg1, gu1 = wide_gradients(a1, dg1, du1)
-        dht, dg0, du0 = between(dg1, du1, h1, dy, gate0, up0, wg, wu, wd)
-        gd0 = tall_gradient(dht, act0)
-        gg0, gu0 = wide_gradients(a0, dg0, du0)
-        r1 = reduce_scatter((TALL, WIDE, WIDE), (gd1, gg1, gu1), ())
-        d1, g1, u1 = r1[:3]
-        d0, g0, u0, factor = reduce_scatter((TALL, WIDE, WIDE), (gd0, gg0, gu0), (d1, g1, u1))
+        gg1, gu1, d1 = upper_gradients(dyt, a1, act1, dg1, du1)
+        dht, dg0, du0, g1, u1 = between(dg1, du1, h1, dy, gate0, up0, wg, wu, wd, gg1, gu1)
+        d0, g0, u0, factor = lower_gradients(dht, a0, act0, dg0, du0, (d1, g1, u1))
         shards = [jnp.stack(pair).astype(F32) for pair in ((g0, g1), (u0, u1), (d0, d1))]
         me = lax.axis_index("dp")
         f = factor[0, 0]

time: 478 us -> 417 us (0.87)
  Pallas kernels: 441 us -> 381 us
    pallas_call x6 -> x2, Pallas kernels: 205 us -> 134 us  [the longest x1 83.4 us: lower_gradients(): pl.pallas_call(lower_kernel, grid=(3 * STEPS,), in_specs=[WHOLE_T, WHOLE_...]
    pallas_call x1, Pallas kernels: 49.6 us -> 59.7 us  [between(): pl.pallas_call(between_kernel, grid=(TOKENS // TM,), in_specs=[rows(FF),...]
    unnamed x15 -> x9, local copies, waits for them, and re-layouts: 23.7 us -> 23.7 us
where the time goes in v3:
time: 417 us
  Pallas kernels  381 us (91%)
  local copies, waits for them, and re-layouts  24.9 us (6%)
  other arithmetic  10.6 us (3%)
    pallas_call x1, Pallas kernels, all_gather(): pl.pallas_call(gather_kernel, out_shape=[jax.ShapeDtypeStruct((2, 2, 2, 2...  100 us
    pallas_call x1, Pallas kernels, lower_gradients(): pl.pallas_call(lower_kernel, grid=(3 * STEPS,), in_specs=[WHOLE_T, WHOLE_...  83.4 us
    pallas_call x1, Pallas kernels, between(): pl.pallas_call(between_kernel, grid=(TOKENS // TM,), in_specs=[rows(FF),...  59.7 us
    pallas_call x1, Pallas kernels, upper_gradients(): pl.pallas_call(upper_kernel, grid=(3 * STEPS,), in_specs=[WHOLE_T, WHOLE_...  50.3 us
    pallas_call x1, Pallas kernels, last(): pl.pallas_call(last_kernel, grid=(TOKENS // TM,), in_specs=[rows(D), SEQ,...  44.4 us
    pallas_call x1, Pallas kernels, forward(): pl.pallas_call(forward_kernel, grid=(TOKENS // TM,), in_specs=[SEQ, weigh...  42.5 us
    unnamed x9, local copies, waits for them, and re-layouts  23.7 us
    convert_element_type x2, other arithmetic, adamw(): return ((w - 0.02 * step).astype(BF16), m, v)  10.6 us

profile of v3, /device:TPU:0, one launch (start us, length us, event | category | flops | bytes accessed | tf_op | source)
XLA Modules:
  0.0 416.7 jit_solution(2797609632708052538)
XLA Ops:
  0.6 42.5 %forward.1 = (bf16[2048,896]{1,0:T(8,128)(2,1)}, bf16[896,2048]{1,0:T(8,128)(2,1)}, bf16[2048,2560]{1,0:T(8,128)(2,1)}, f32[2048,2560]{1,0:T(8,128)}, f32[2048,2560]{1,0:T(8,128)}) custom-call(bf16[1,2048,896]{2,1,0:T(8,128)(2,1)} %x.1, bf16[2,896,2560]{2,1,0:T(8,128)(2,1)} %wg.5, bf16[2,896,2560]{2,1,0:T(8,128)(2,1)} %wu.5, bf16[2,2560,896]{2,1,0:T(8,128)(2,1)} %wd.5), custom_call_target="tpu_custom_call" | custom-call | flops 28185722880 | bytes 62914560 | tf_op jit(solution)/shard_map/forward/pallas_call | solution.py:390
  43.2 44.4 %last.1 = (bf16[896,2048]{1,0:T(8,128)(2,1)}, bf16[896,2048]{1,0:T(8,128)(2,1)}, bf16[2048,2560]{1,0:T(8,128)(2,1)}, bf16[2048,2560]{1,0:T(8,128)(2,1)}, bf16[2048,2560]{1,0:T(8,128)(2,1)}) custom-call(bf16[2048,896]{1,0:T(8,128)(2,1)} %get-tuple-element.34.h1, bf16[1,2048,896]{2,1,0:T(8,128)(2,1)} %dy.3, bf16[2,896,2560]{2,1,0:T(8,128)(2,1)} %wg.5, ...), custom_call_target="tpu_custom_call" | custom-call | flops 28185722880 | bytes 62914560 | tf_op jit(solution)/shard_map/last/pallas_call | solution.py:403
  87.6 50.3 %upper_gradients.1 = (bf16[8,2,56,2560]{3,2,1,0:T(8,128)(2,1)}, bf16[8,2,56,2560]{3,2,1,0:T(8,128)(2,1)}, bf16[160,896]{1,0:T(8,128)(2,1)}) custom-call(bf16[896,2048]{1,0:T(8,128)(2,1)} %get-tuple-element.39.dt, bf16[896,2048]{1,0:T(8,128)(2,1)} %get-tuple-element.40.at, bf16[2048,2560]{1,0:T(8,128)(2,1)} %get-tuple-element.41.act, ...), custom_call_target="tpu_custom_call" | custom-call | flops 28185722880 | bytes 62914560 | tf_op jit(solution)/shard_map/upper_gradients/pallas_call | solution.py:506
  137.9 59.7 %between.1 = (bf16[896,2048]{1,0:T(8,128)(2,1)}, bf16[2048,2560]{1,0:T(8,128)(2,1)}, bf16[2048,2560]{1,0:T(8,128)(2,1)}, bf16[56,2560]{1,0:T(8,128)(2,1)}, bf16[56,2560]{1,0:T(8,128)(2,1)}) custom-call(bf16[2048,2560]{1,0:T(8,128)(2,1)} %get-tuple-element.35.dg.dg1, bf16[2048,2560]{1,0:T(8,128)(2,1)} %get-tuple-element.36.du.du1, ...), custom_call_target="tpu_custom_call" | custom-call | flops 28185722880 | bytes 62914560 | tf_op jit(solution)/shard_map/between/pallas_call | solution.py:420
  197.6 83.4 %lower_gradients.1 = (bf16[160,896]{1,0:T(8,128)(2,1)}, bf16[56,2560]{1,0:T(8,128)(2,1)}, bf16[56,2560]{1,0:T(8,128)(2,1)}, f32[8,128]{1,0:T(8,128)}) custom-call(bf16[896,2048]{1,0:T(8,128)(2,1)} %get-tuple-element.44.dt, bf16[896,2048]{1,0:T(8,128)(2,1)} %get-tuple-element.45.at, bf16[2048,2560]{1,0:T(8,128)(2,1)} %get-tuple-element.46.act, ...), custom_call_target="tpu_custom_call" | custom-call | flops 28185722880 | bytes 62914560 | tf_op jit(solution)/shard_map/lower_gradients/pallas_call | solution.py:521
  281.0 1.2 slice.3
  282.2 0.0 copy-start
  282.2 0.0 copy-start.1
  282.2 0.0 copy-start.2
  282.2 4.8 %fusion.8 = (bf16[2,160,896]{2,1,0:T(8,128)(2,1)}, f32[2,160,896]{2,1,0:T(8,128)}, f32[2,160,896]{2,1,0:T(8,128)}) fusion(bf16[2,2560,896]{2,1,0:T(8,128)(2,1)} %wd.5, s32[]{:T(128)S(6)} %select_n.8, f32[]{:T(128)} %bitcast.2, bf16[1,160,896]{2,1,0:T(8,128)(2,1)} %bitcast.17, bf16[1,160,896]{2,1,0:T(8,128)(2,1)} %bitcast.18, f32[2,160,896]{2,1,0:T(8,128)} %param.21, ...), kind=kLoop, calls=%fused_computation.17 | loop fusion | flops 5734400 | bytes 6307848 | tf_op jit(solution)/shard_map/convert_element_type | solution.py:538
  287.1 0.0 copy-done
  287.1 0.0 copy-done.1
  287.1 0.0 copy-done.2
  287.1 5.7 %fusion.2 = (bf16[2,56,2560]{2,1,0:T(8,128)(2,1)}, f32[2,56,2560]{2,1,0:T(8,128)}, f32[2,56,2560]{2,1,0:T(8,128)}, bf16[2,56,2560]{2,1,0:T(8,128)(2,1)}, f32[2,56,2560]{2,1,0:T(8,128)}, /*index=5*/f32[2,56,2560]{2,1,0:T(8,128)}) fusion(bf16[2,896,2560]{2,1,0:T(8,128)(2,1)} %wg.5, s32[]{:T(128)S(6)} %select_n.7, f32[]{:T(128)} %bitcast.2, ...), kind=kLoop, calls=%fused_computation.11 | loop fusion | flops 11468800 | bytes 12615688 | tf_op jit(solution)/shard_map/convert_element_type | solution.py:538
  292.8 100.2 %all_gather.1 = (bf16[2,2,2,2,2,56,2560]{6,5,4,3,2,1,0:T(8,128)(2,1)}, bf16[2,2,2,2,2,56,2560]{6,5,4,3,2,1,0:T(8,128)(2,1)}, bf16[2,2,2,2,2,160,896]{6,5,4,3,2,1,0:T(8,128)(2,1)}) custom-call(bf16[2,56,2560]{2,1,0:T(8,128)(2,1)} %get-tuple-element.65.refs_0_, bf16[2,56,2560]{2,1,0:T(8,128)(2,1)} %get-tuple-element.68.refs_1_, ...), custom_call_target="tpu_custom_call" | custom-call | tf_op jit(solution)/shard_map/all_gather/pallas_call | solution.py:281
  393.0 7.9 %copy.23 = bf16[2,896,2560]{2,1,0:T(8,128)(2,1)} copy(bf16[2,896,2560]{2,1,0:T(8,128)(2,1)} %bitcast.12) | data formatting | bytes 18350080
  400.9 7.8 %copy.24 = bf16[2,896,2560]{2,1,0:T(8,128)(2,1)} copy(bf16[2,896,2560]{2,1,0:T(8,128)(2,1)} %bitcast.11) | data formatting | bytes 18350080
  408.8 8.0 %copy.25 = bf16[2,2560,896]{2,1,0:T(8,128)(2,1)} copy(bf16[2,2560,896]{2,1,0:T(8,128)(2,1)} %bitcast.10) | data formatting | bytes 18350080
Async XLA Ops:
  282.2 4.8 %copy-start = (f32[2,56,2560]{2,1,0:T(8,128)S(1)}, f32[2,56,2560]{2,1,0:T(8,128)}, u32[]{:S(2)}) copy-start(f32[2,56,2560]{2,1,0:T(8,128)} %param.19) | copy-start | bytes 3440644
  282.2 4.8 %copy-start.1 = (f32[2,56,2560]{2,1,0:T(8,128)S(1)}, f32[2,56,2560]{2,1,0:T(8,128)}, u32[]{:S(2)}) copy-start(f32[2,56,2560]{2,1,0:T(8,128)} %param.16) | copy-start | bytes 3440644
  282.2 4.8 %copy-start.2 = (f32[2,56,2560]{2,1,0:T(8,128)S(1)}, f32[2,56,2560]{2,1,0:T(8,128)}, u32[]{:S(2)}) copy-start(f32[2,56,2560]{2,1,0:T(8,128)} %param.20) | copy-start | bytes 3440644

commit v4 on v3

--- a/solution.py
+++ b/solution.py
@@ -280,18 +280,38 @@
 def all_gather(owns):
     outs = pl.pallas_call(
         gather_kernel,
-        out_shape=[jax.ShapeDtypeStruct((2, 2, 2, 2, 2, *o.shape[1:]), BF16) for o in owns],
+        out_shape=[pltpu.VMEM((2, 2, 2, 2, 2, *o.shape[1:]), BF16) for o in owns],
         in_specs=[WHOLE] * 3,
-        out_specs=[ANY] * 3,
+        out_specs=[WHOLE] * 3,
         scratch_shapes=[
             pltpu.SemaphoreType.DMA((6, 19)),
             pltpu.SemaphoreType.DMA((6, 19)),
             pltpu.SemaphoreType.DMA((6,)),
         ],
-        compiler_params=pltpu.CompilerParams(has_side_effects=True),
+        compiler_params=pltpu.CompilerParams(has_side_effects=True, vmem_limit_bytes=8 << 20),
         name="all_gather",
     )(*owns)
+    outs = pl.pallas_call(
+        flush_kernel,
+        out_shape=[jax.ShapeDtypeStruct(o.shape, BF16) for o in outs],
+        in_specs=[WHOLE] * 3,
+        out_specs=[ANY] * 3,
+        scratch_shapes=[pltpu.SemaphoreType.DMA((6,))],
+        compiler_params=pltpu.CompilerParams(vmem_limit_bytes=1 << 20),
+        name="flush",
+    )(*outs)
     return [o.reshape(2, DEVICES * o.shape[-2], o.shape[-1]) for o in outs]
+
+
+def flush_kernel(*refs):
+    copies = []
+    for i in range(3):
+        for layer in range(2):
+            copies.append(pltpu.make_async_copy(refs[i].at[layer], refs[3 + i].at[layer], refs[6].at[2 * i + layer]))
+    for c in copies:
+        c.start()
+    for c in copies:
+        c.wait()
 
 
 def dot(a, b):

time: 417 us -> 401 us (0.962)
  local copies, waits for them, and re-layouts: 24.9 us -> 1.21 us
  Pallas kernels: 381 us -> 388 us
    unnamed x9 -> x8, local copies, waits for them, and re-layouts: 23.7 us -> 0.01 us
    pallas_call x1 -> x2, Pallas kernels: 100 us -> 108 us  [the longest x1 98.5 us: all_gather(): pl.pallas_call(gather_kernel, out_shape=[pltpu.VMEM((2, 2, 2, 2, 2, *o.sh...]
where the time goes in v4:
time: 401 us
  Pallas kernels  388 us (97%)
  other arithmetic  10.7 us (3%)
    pallas_call x1, Pallas kernels, all_gather(): pl.pallas_call(gather_kernel, out_shape=[pltpu.VMEM((2, 2, 2, 2, 2, *o.sh...  98.5 us
    pallas_call x1, Pallas kernels, lower_gradients(): pl.pallas_call(lower_kernel, grid=(3 * STEPS,), in_specs=[WHOLE_T, WHOLE_...  83.2 us
    pallas_call x1, Pallas kernels, between(): pl.pallas_call(between_kernel, grid=(TOKENS // TM,), in_specs=[rows(FF),...  59.7 us
    pallas_call x1, Pallas kernels, upper_gradients(): pl.pallas_call(upper_kernel, grid=(3 * STEPS,), in_specs=[WHOLE_T, WHOLE_...  50.5 us
    pallas_call x1, Pallas kernels, last(): pl.pallas_call(last_kernel, grid=(TOKENS // TM,), in_specs=[rows(D), SEQ,...  44.4 us
    pallas_call x1, Pallas kernels, forward(): pl.pallas_call(forward_kernel, grid=(TOKENS // TM,), in_specs=[SEQ, weigh...  42.5 us
    convert_element_type x2, other arithmetic, adamw(): return ((w - 0.02 * step).astype(BF16), m, v)  10.7 us
    pallas_call x1, Pallas kernels, all_gather(): pl.pallas_call(flush_kernel, out_shape=[jax.ShapeDtypeStruct(o.shape, BF1...  9.23 us

profile of v4, /device:TPU:0, one launch (start us, length us, event | category | flops | bytes accessed | tf_op | source)
XLA Modules:
  0.0 400.8 jit_solution(14776599447107166164)
XLA Ops:
  0.6 42.5 %forward.1 = (bf16[2048,896]{1,0:T(8,128)(2,1)}, bf16[896,2048]{1,0:T(8,128)(2,1)}, bf16[2048,2560]{1,0:T(8,128)(2,1)}, f32[2048,2560]{1,0:T(8,128)}, f32[2048,2560]{1,0:T(8,128)}) custom-call(bf16[1,2048,896]{2,1,0:T(8,128)(2,1)} %x.1, bf16[2,896,2560]{2,1,0:T(8,128)(2,1)} %wg.5, bf16[2,896,2560]{2,1,0:T(8,128)(2,1)} %wu.5, bf16[2,2560,896]{2,1,0:T(8,128)(2,1)} %wd.5), custom_call_target="tpu_custom_call" | custom-call | flops 28185722880 | bytes 62914560 | tf_op jit(solution)/shard_map/forward/pallas_call | solution.py:410
  43.2 44.4 %last.1 = (bf16[896,2048]{1,0:T(8,128)(2,1)}, bf16[896,2048]{1,0:T(8,128)(2,1)}, bf16[2048,2560]{1,0:T(8,128)(2,1)}, bf16[2048,2560]{1,0:T(8,128)(2,1)}, bf16[2048,2560]{1,0:T(8,128)(2,1)}) custom-call(bf16[2048,896]{1,0:T(8,128)(2,1)} %get-tuple-element.37.h1, bf16[1,2048,896]{2,1,0:T(8,128)(2,1)} %dy.3, bf16[2,896,2560]{2,1,0:T(8,128)(2,1)} %wg.5, ...), custom_call_target="tpu_custom_call" | custom-call | flops 28185722880 | bytes 62914560 | tf_op jit(solution)/shard_map/last/pallas_call | solution.py:423
  87.5 50.5 %upper_gradients.1 = (bf16[8,2,56,2560]{3,2,1,0:T(8,128)(2,1)}, bf16[8,2,56,2560]{3,2,1,0:T(8,128)(2,1)}, bf16[160,896]{1,0:T(8,128)(2,1)}) custom-call(bf16[896,2048]{1,0:T(8,128)(2,1)} %get-tuple-element.42.dt, bf16[896,2048]{1,0:T(8,128)(2,1)} %get-tuple-element.43.at, bf16[2048,2560]{1,0:T(8,128)(2,1)} %get-tuple-element.44.act, ...), custom_call_target="tpu_custom_call" | custom-call | flops 28185722880 | bytes 62914560 | tf_op jit(solution)/shard_map/upper_gradients/pallas_call | solution.py:526
  138.0 59.7 %between.1 = (bf16[896,2048]{1,0:T(8,128)(2,1)}, bf16[2048,2560]{1,0:T(8,128)(2,1)}, bf16[2048,2560]{1,0:T(8,128)(2,1)}, bf16[56,2560]{1,0:T(8,128)(2,1)}, bf16[56,2560]{1,0:T(8,128)(2,1)}) custom-call(bf16[2048,2560]{1,0:T(8,128)(2,1)} %get-tuple-element.38.dg.dg1, bf16[2048,2560]{1,0:T(8,128)(2,1)} %get-tuple-element.39.du.du1, ...), custom_call_target="tpu_custom_call" | custom-call | flops 28185722880 | bytes 62914560 | tf_op jit(solution)/shard_map/between/pallas_call | solution.py:440
  197.8 83.2 %lower_gradients.1 = (bf16[160,896]{1,0:T(8,128)(2,1)}, bf16[56,2560]{1,0:T(8,128)(2,1)}, bf16[56,2560]{1,0:T(8,128)(2,1)}, f32[8,128]{1,0:T(8,128)}) custom-call(bf16[896,2048]{1,0:T(8,128)(2,1)} %get-tuple-element.47.dt, bf16[896,2048]{1,0:T(8,128)(2,1)} %get-tuple-element.48.at, bf16[2048,2560]{1,0:T(8,128)(2,1)} %get-tuple-element.49.act, ...), custom_call_target="tpu_custom_call" | custom-call | flops 28185722880 | bytes 62914560 | tf_op jit(solution)/shard_map/lower_gradients/pallas_call | solution.py:541
  281.0 1.2 slice.3
  282.2 0.0 copy-start
  282.2 0.0 copy-start.1
  282.2 0.0 copy-start.2
  282.2 0.0 copy-start.3
  282.2 4.8 %fusion.8 = (bf16[2,160,896]{2,1,0:T(8,128)(2,1)S(1)}, f32[2,160,896]{2,1,0:T(8,128)}, f32[2,160,896]{2,1,0:T(8,128)}) fusion(bf16[2,2560,896]{2,1,0:T(8,128)(2,1)} %wd.5, s32[]{:T(128)S(6)} %select_n.8, f32[]{:T(128)} %bitcast.2, bf16[1,160,896]{2,1,0:T(8,128)(2,1)} %bitcast.14, bf16[1,160,896]{2,1,0:T(8,128)(2,1)} %bitcast.15, f32[2,160,896]{2,1,0:T(8,128)} %param.21, ...), kind=kLoop, calls=%fused_computation.17 | loop fusion | flops 5734400 | bytes 6307848 | tf_op jit(solution)/shard_map/convert_element_type | solution.py:558
  287.1 0.0 copy-done
  287.1 0.0 copy-done.1
  287.1 0.0 copy-done.2
  287.1 0.0 copy-done.3
  287.1 5.9 %fusion.2 = (bf16[2,56,2560]{2,1,0:T(8,128)(2,1)S(1)}, f32[2,56,2560]{2,1,0:T(8,128)}, f32[2,56,2560]{2,1,0:T(8,128)}, bf16[2,56,2560]{2,1,0:T(8,128)(2,1)S(1)},...) fusion(bf16[2,896,2560]{2,1,0:T(8,128)(2,1)} %wg.5, s32[]{:T(128)S(6)} %select_n.7, f32[]{:T(128)} %bitcast.2, ...), kind=kLoop, calls=%fused_computation.11 | loop fusion | flops 11468800 | bytes 12615688 | tf_op jit(solution)/shard_map/convert_element_type | solution.py:558
  292.9 98.5 %all_gather.1 = (bf16[2,2,2,2,2,56,2560]{6,5,4,3,2,1,0:T(8,128)(2,1)S(1)}, bf16[2,2,2,2,2,56,2560]{6,5,4,3,2,1,0:T(8,128)(2,1)S(1)}, bf16[2,2,2,2,2,160,896]{6,5,4,3,2,1,0:T(8,128)(2,1)S(1)}) custom-call(bf16[2,56,2560]{2,1,0:T(8,128)(2,1)S(1)} %get-tuple-element.71.refs_0_, bf16[2,56,2560]{2,1,0:T(8,128)(2,1)S(1)} %get-tuple-element.74.refs_1_, ...), custom_call_target="tpu_custom_call" | custom-call | tf_op jit(solution)/shard_map/all_gather/pallas_call | solution.py:281
  391.4 9.2 %flush.1 = (bf16[2,2,2,2,2,56,2560]{6,5,4,3,2,1,0:T(8,128)(2,1)}, bf16[2,2,2,2,2,56,2560]{6,5,4,3,2,1,0:T(8,128)(2,1)}, bf16[2,2,2,2,2,160,896]{6,5,4,3,2,1,0:T(8,128)(2,1)}) custom-call(bf16[2,2,2,2,2,56,2560]{6,5,4,3,2,1,0:T(8,128)(2,1)S(1)} %get-tuple-element.59.refs_0_, bf16[2,2,2,2,2,56,2560]{6,5,4,3,2,1,0:T(8,128)(2,1)S(1)} %get-tuple-element.60.refs_1_, ...), custom_call_target="tpu_custom_call" | custom-call | tf_op jit(solution)/shard_map/flush/pallas_call | solution.py:294
Async XLA Ops:
  282.2 4.9 %copy-start = (f32[2,56,2560]{2,1,0:T(8,128)S(1)}, f32[2,56,2560]{2,1,0:T(8,128)}, u32[]{:S(2)}) copy-start(f32[2,56,2560]{2,1,0:T(8,128)} %param.19) | copy-start | bytes 3440644
  282.2 4.9 %copy-start.1 = (f32[2,56,2560]{2,1,0:T(8,128)S(1)}, f32[2,56,2560]{2,1,0:T(8,128)}, u32[]{:S(2)}) copy-start(f32[2,56,2560]{2,1,0:T(8,128)} %param.16) | copy-start | bytes 3440644
  282.2 4.9 %copy-start.2 = (bf16[56,2560]{1,0:T(8,128)(2,1)S(1)}, bf16[56,2560]{1,0:T(8,128)(2,1)}, u32[]{:S(2)}) copy-start(bf16[56,2560]{1,0:T(8,128)(2,1)} %get-tuple-element.53.g1) | copy-start | bytes 860164
  282.2 4.9 %copy-start.3 = (bf16[56,2560]{1,0:T(8,128)(2,1)S(1)}, bf16[56,2560]{1,0:T(8,128)(2,1)}, u32[]{:S(2)}) copy-start(bf16[56,2560]{1,0:T(8,128)(2,1)} %get-tuple-element.54.u1) | copy-start | bytes 860164

commit v5 on v4

--- a/solution.py
+++ b/solution.py
@@ -314,6 +314,68 @@
         c.wait()
 
 
+KINDS = (WIDE, WIDE, TALL)
+
+
+def adamw_kernel(*refs):
+    factor, shards, ms, vs, weights = refs[0], refs[1:7], refs[7:10], refs[10:13], refs[13:16]
+    new_ws, new_ms, new_vs = refs[16:19], refs[19:22], refs[22:25]
+    in_ms, in_vs, gs, (isem, osem) = refs[25:28], refs[28:31], refs[31:34], refs[34:]
+    me = lax.axis_index("dp")
+    loads, stores = [], []
+    for i, kind in enumerate(KINDS):
+        mine = pl.ds(pl.multiple_of(me * kind[0], 8), kind[0])
+        for layer in range(2):
+            pairs = (
+                (shards[3 * layer + i], gs[i].at[layer]),
+                (ms[i].at[layer], in_ms[i].at[layer]),
+                (vs[i].at[layer], in_vs[i].at[layer]),
+                (weights[i].at[layer, mine], new_ws[i].at[layer]),
+            )
+            loads.append([pltpu.make_async_copy(src, dst, isem.at[2 * i + layer, k]) for k, (src, dst) in enumerate(pairs)])
+            pairs = (in_ms[i], new_ms[i]), (in_vs[i], new_vs[i])
+            stores.append(
+                [
+                    pltpu.make_async_copy(src.at[layer], dst.at[layer], osem.at[2 * i + layer, k])
+                    for k, (src, dst) in enumerate(pairs)
+                ]
+            )
+    for copies in loads:
+        for c in copies:
+            c.start()
+    f = factor[0:1, 0:1]
+    for u in range(6):
+        i, layer = divmod(u, 2)
+        for c in loads[u]:
+            c.wait()
+        g = gs[i][layer].astype(F32) * f
+        w = new_ws[i][layer].astype(F32)
+        m = 0.9 * in_ms[i][layer] + 0.1 * g
+        v = 0.95 * in_vs[i][layer] + 0.05 * g * g
+        step = m * lax.rsqrt(v + 1e-8) + 0.1 * w
+        new_ws[i][layer], in_ms[i][layer], in_vs[i][layer] = (w - 0.02 * step).astype(BF16), m, v
+        for c in stores[u]:
+            c.start()
+    for copies in stores:
+        for c in copies:
+            c.wait()
+
+
+def adamw(factor, shards, ms, vs, weights):
+    own = [(2, *k[:2]) for k in KINDS]
+    outs = pl.pallas_call(
+        adamw_kernel,
+        out_shape=[pltpu.VMEM(s, BF16) for s in own] + [jax.ShapeDtypeStruct(s, F32) for s in own * 2],
+        in_specs=[WHOLE] + [ANY] * 15,
+        out_specs=[WHOLE] * 3 + [ANY] * 6,
+        scratch_shapes=[pltpu.VMEM(s, t) for t in (F32, F32, BF16) for s in own]
+        + [pltpu.SemaphoreType.DMA((6, 4)), pltpu.SemaphoreType.DMA((6, 2))],
+        compiler_params=pltpu.CompilerParams(vmem_limit_bytes=60 * 1024 * 1024),
+        name="adamw",
+    )(factor, *shards, *ms, *vs, *weights)
+    return outs[:3], outs[3:]
+
+
 def dot(a, b):
     return jnp.dot(a, b, preferred_element_type=F32)
 
@@ -551,13 +613,6 @@
     )(dt, at, act, dg, du, *before)
 
 
-def adamw(w, m, v, g):
-    m = 0.9 * m + 0.1 * g
-    v = 0.95 * v + 0.05 * g * g
-    step = m * lax.rsqrt(v + 1e-8) + 0.1 * w
-    return (w - 0.02 * step).astype(BF16), m, v
-
-
 def solution(mesh):
     def step(x, dy, wg, wu, wd, *moments):
         h1, a0, act0, gate0, up0 = forward(x, wg, wu, wd)
@@ -565,16 +620,8 @@
         gg1, gu1, d1 = upper_gradients(dyt, a1, act1, dg1, du1)
         dht, dg0, du0, g1, u1 = between(dg1, du1, h1, dy, gate0, up0, wg, wu, wd, gg1, gu1)
         d0, g0, u0, factor = lower_gradients(dht, a0, act0, dg0, du0, (d1, g1, u1))
-        shards = [jnp.stack(pair).astype(F32) for pair in ((g0, g1), (u0, u1), (d0, d1))]
-        me = lax.axis_index("dp")
-        f = factor[0, 0]
-        new = []
-        for k, w in enumerate((wg, wu, wd)):
-            r = w.shape[1] // DEVICES
-            own = lax.dynamic_slice_in_dim(w, me * r, r, 1).astype(F32)
-            new.append(adamw(own, moments[k], moments[3 + k], shards[k] * f))
-        gathered = all_gather([n[0] for n in new])
-        return (*gathered, *(n[1] for n in new), *(n[2] for n in new))
+        own, new_moments = adamw(factor, (g0, u0, d0, g1, u1, d1), moments[:3], moments[3:], (wg, wu, wd))
+        return (*all_gather(own), *new_moments)
 
     seq = P(("rep", "dp"), None, None)
     whole = P(None, None, None)

time: 401 us -> 397 us (0.990)
  other arithmetic: 10.7 us -> 0 us
  Pallas kernels: 388 us -> 396 us
    convert_element_type x2 -> x0, other arithmetic: 10.7 us -> none  [adamw(): return ((w - 0.02 * step).astype(BF16), m, v)]
    pallas_call x0 -> x1, Pallas kernels: none -> 7.68 us  [adamw(): pl.pallas_call(adamw_kernel, out_shape=[pltpu.VMEM(s, BF16) for s in own]...]
where the time goes in v5:
time: 397 us
  Pallas kernels  396 us (100%)
    pallas_call x1, Pallas kernels, all_gather(): pl.pallas_call(gather_kernel, out_shape=[pltpu.VMEM((2, 2, 2, 2, 2, *o.sh...  98.5 us
    pallas_call x1, Pallas kernels, lower_gradients(): pl.pallas_call(lower_kernel, grid=(3 * STEPS,), in_specs=[WHOLE_T, WHOLE_...  83.2 us
    pallas_call x1, Pallas kernels, between(): pl.pallas_call(between_kernel, grid=(TOKENS // TM,), in_specs=[rows(FF),...  59.7 us
    pallas_call x1, Pallas kernels, upper_gradients(): pl.pallas_call(upper_kernel, grid=(3 * STEPS,), in_specs=[WHOLE_T, WHOLE_...  50.5 us
    pallas_call x1, Pallas kernels, last(): pl.pallas_call(last_kernel, grid=(TOKENS // TM,), in_specs=[rows(D), SEQ,...  44.4 us
    pallas_call x1, Pallas kernels, forward(): pl.pallas_call(forward_kernel, grid=(TOKENS // TM,), in_specs=[SEQ, weigh...  42.5 us
    pallas_call x1, Pallas kernels, all_gather(): pl.pallas_call(flush_kernel, out_shape=[jax.ShapeDtypeStruct(o.shape, BF1...  9.23 us

profile of v5, /device:TPU:0, one launch (start us, length us, event | category | flops | bytes accessed | tf_op | source)
XLA Modules:
  0.0 396.5 jit_solution(7655377467239782909)
XLA Ops:
  0.6 42.5 %forward.1 = (bf16[2048,896]{1,0:T(8,128)(2,1)}, bf16[896,2048]{1,0:T(8,128)(2,1)}, bf16[2048,2560]{1,0:T(8,128)(2,1)}, f32[2048,2560]{1,0:T(8,128)}, f32[2048,2560]{1,0:T(8,128)}) custom-call(bf16[1,2048,896]{2,1,0:T(8,128)(2,1)} %x.1, bf16[2,896,2560]{2,1,0:T(8,128)(2,1)} %refs_13_.1, bf16[2,896,2560]{2,1,0:T(8,128)(2,1)} %refs_14_.1, ...), custom_call_target="tpu_custom_call" | custom-call | flops 28185722880 | bytes 62914560 | tf_op jit(solution)/shard_map/forward/pallas_call | solution.py:472
  43.2 44.4 %last.1 = (bf16[896,2048]{1,0:T(8,128)(2,1)}, bf16[896,2048]{1,0:T(8,128)(2,1)}, bf16[2048,2560]{1,0:T(8,128)(2,1)}, bf16[2048,2560]{1,0:T(8,128)(2,1)}, bf16[2048,2560]{1,0:T(8,128)(2,1)}) custom-call(bf16[2048,896]{1,0:T(8,128)(2,1)} %get-tuple-element.46.h1, bf16[1,2048,896]{2,1,0:T(8,128)(2,1)} %dy.3, bf16[2,896,2560]{2,1,0:T(8,128)(2,1)} %refs_13_.1, ...), custom_call_target="tpu_custom_call" | custom-call | flops 28185722880 | bytes 62914560 | tf_op jit(solution)/shard_map/last/pallas_call | solution.py:485
  87.6 50.5 %upper_gradients.1 = (bf16[8,2,56,2560]{3,2,1,0:T(8,128)(2,1)}, bf16[8,2,56,2560]{3,2,1,0:T(8,128)(2,1)}, bf16[160,896]{1,0:T(8,128)(2,1)}) custom-call(bf16[896,2048]{1,0:T(8,128)(2,1)} %get-tuple-element.51.dt, bf16[896,2048]{1,0:T(8,128)(2,1)} %get-tuple-element.52.at, bf16[2048,2560]{1,0:T(8,128)(2,1)} %get-tuple-element.53.act, ...), custom_call_target="tpu_custom_call" | custom-call | flops 28185722880 | bytes 62914560 | tf_op jit(solution)/shard_map/upper_gradients/pallas_call | solution.py:588
  138.0 59.7 %between.1 = (bf16[896,2048]{1,0:T(8,128)(2,1)}, bf16[2048,2560]{1,0:T(8,128)(2,1)}, bf16[2048,2560]{1,0:T(8,128)(2,1)}, bf16[56,2560]{1,0:T(8,128)(2,1)}, bf16[56,2560]{1,0:T(8,128)(2,1)}) custom-call(bf16[2048,2560]{1,0:T(8,128)(2,1)} %get-tuple-element.47.dg.dg1, bf16[2048,2560]{1,0:T(8,128)(2,1)} %get-tuple-element.48.du.du1, ...), custom_call_target="tpu_custom_call" | custom-call | flops 28185722880 | bytes 62914560 | tf_op jit(solution)/shard_map/between/pallas_call | solution.py:502
  197.7 83.2 %lower_gradients.1 = (bf16[160,896]{1,0:T(8,128)(2,1)}, bf16[56,2560]{1,0:T(8,128)(2,1)}, bf16[56,2560]{1,0:T(8,128)(2,1)}, f32[8,128]{1,0:T(8,128)}) custom-call(bf16[896,2048]{1,0:T(8,128)(2,1)} %get-tuple-element.56.dt, bf16[896,2048]{1,0:T(8,128)(2,1)} %get-tuple-element.57.at, bf16[2048,2560]{1,0:T(8,128)(2,1)} %get-tuple-element.58.act, ...), custom_call_target="tpu_custom_call" | custom-call | flops 28185722880 | bytes 62914560 | tf_op jit(solution)/shard_map/lower_gradients/pallas_call | solution.py:603
  281.0 7.7 %adamw.1 = (bf16[2,56,2560]{2,1,0:T(8,128)(2,1)S(1)}, bf16[2,56,2560]{2,1,0:T(8,128)(2,1)S(1)}, bf16[2,160,896]{2,1,0:T(8,128)(2,1)S(1)}, f32[2,56,2560]{2,1,0:T...) custom-call(f32[8,128]{1,0:T(8,128)} %get-tuple-element.64.refs_0_, ...), custom_call_target="tpu_custom_call" | custom-call | tf_op jit(solution)/shard_map/adamw/pallas_call | solution.py:366
  288.7 98.5 %all_gather.1 = (bf16[2,2,2,2,2,56,2560]{6,5,4,3,2,1,0:T(8,128)(2,1)S(1)}, bf16[2,2,2,2,2,56,2560]{6,5,4,3,2,1,0:T(8,128)(2,1)S(1)}, bf16[2,2,2,2,2,160,896]{6,5,4,3,2,1,0:T(8,128)(2,1)S(1)}) custom-call(bf16[2,56,2560]{2,1,0:T(8,128)(2,1)S(1)} %get-tuple-element.68.refs_0_, bf16[2,56,2560]{2,1,0:T(8,128)(2,1)S(1)} %get-tuple-element.69.refs_1_, ...), custom_call_target="tpu_custom_call" | custom-call | tf_op jit(solution)/shard_map/all_gather/pallas_call | solution.py:281
  387.1 9.2 %flush.1 = (bf16[2,2,2,2,2,56,2560]{6,5,4,3,2,1,0:T(8,128)(2,1)}, bf16[2,2,2,2,2,56,2560]{6,5,4,3,2,1,0:T(8,128)(2,1)}, bf16[2,2,2,2,2,160,896]{6,5,4,3,2,1,0:T(8,128)(2,1)}) custom-call(bf16[2,2,2,2,2,56,2560]{6,5,4,3,2,1,0:T(8,128)(2,1)S(1)} %get-tuple-element.71.refs_0_, bf16[2,2,2,2,2,56,2560]{6,5,4,3,2,1,0:T(8,128)(2,1)S(1)} %get-tuple-element.72.refs_1_, ...), custom_call_target="tpu_custom_call" | custom-call | tf_op jit(solution)/shard_map/flush/pallas_call | solution.py:294

commit v6 on v5

--- a/solution.py
+++ b/solution.py
@@ -14,12 +14,15 @@
 TM = 256
 NB = 512
 STEPS = FF // NB
+BN = 256
 ANY = pl.BlockSpec(memory_space=pl.ANY)
 WHOLE = pl.BlockSpec(memory_space=pltpu.VMEM)
 
 STRIDE = (8, 4, 2)
 ORDER = ((0, 1, 2), (1, 2, 0), (2, 0, 1))
 WIDE = (56, 2560, tuple((slice(0, 56), s) for s in (slice(0, 896), slice(896, 1792), slice(1792, 2560))))
+BLOCK = (56, 256, tuple((s, slice(0, 256)) for s in (slice(0, 24), slice(24, 40), slice(40, 56))))
+PAIR = (56, 512, tuple((s, slice(0, 512)) for s in (slice(0, 24), slice(24, 40), slice(40, 56))))
 TALL = (160, 896, tuple((s, slice(0, 896)) for s in (slice(0, 56), slice(56, 112), slice(112, 160))))
 
 
@@ -40,25 +43,26 @@
     return me + 1 - 2 * core
 
 
-def rs_scratch(kind, here):
+def rs_scratch(kind, sets=()):
     r, c, parts = kind
-    flat = [pltpu.VMEM((8, 2, r, c) if here else (8, r, c), BF16), pltpu.VMEM((8, r, c), BF16)]
+    flat = [pltpu.VMEM((*sets, 8, r, c), BF16)]
     for rows, cols in parts:
-        flat += [pltpu.VMEM((7, size(rows), size(cols)), BF16)] * 2
-    return flat + [pltpu.SemaphoreType.DMA((10,)), pltpu.SemaphoreType.DMA((10,)), pltpu.SemaphoreType.DMA(())]
-
-
-RS_SCRATCH = 11
+        flat += [pltpu.VMEM((*sets, 7, size(rows), size(cols)), BF16)] * 2
+    return flat + [pltpu.SemaphoreType.DMA((*sets, 10))] * 2 + [pltpu.SemaphoreType.DMA((*sets, 1))]
+
+
+RS_SCRATCH = 10
 
 
 class Reduce:
-    def __init__(self, kind, g, out, scratch):
-        self.kind, self.out, self.here = kind, out, g is None
-        self.own, self.other = scratch[:2]
-        self.g = self.own if self.here else g
-        self.send, self.got = scratch[2:8:2], scratch[3:8:2]
-        self.ssem, self.rsem, self.lsem = scratch[8:]
+    def __init__(self, kind, g, out, scratch, own=None, turn=0):
+        self.kind, self.g, self.out, self.here = kind, g, out, own is None
+        self.own = g if self.here else own
+        self.other = scratch[0]
+        self.send, self.got = scratch[1:7:2], scratch[2:7:2]
+        self.ssem, self.rsem, self.lsem = scratch[7:]
         self.me, self.xyz, self.core = place()
+        self.order = ORDER[turn:] + ORDER[:turn]
 
     def swap(self):
         return pltpu.make_async_remote_copy(
@@ -71,7 +75,7 @@
         )
 
     def load(self):
-        return pltpu.make_async_copy(self.g.at[:, self.core], self.own, self.lsem)
+        return pltpu.make_async_copy(self.g.at[:, self.core], self.own, self.lsem.at[0])
 
     def hop(self, t, phase):
         at = pl.ds((0, 4, 6)[phase], (4, 2, 1)[phase])
@@ -80,13 +84,13 @@
             self.got[t].at[at],
             self.ssem.at[3 * t + phase],
             self.rsem.at[3 * t + phase],
-            device_id={"dp": beside(self.me, self.xyz, ORDER[t][phase])},
+            device_id={"dp": beside(self.me, self.xyz, self.order[t][phase])},
             device_id_type=MESH,
         )
 
     def total(self, t, at, got):
         rows, cols = self.kind[2][t]
-        block = sum(p * (4, 2, 1)[axis] for p, axis in zip(at, ORDER[t], strict=True))
+        block = sum(p * (4, 2, 1)[axis] for p, axis in zip(at, self.order[t], strict=True))
         own = self.own[block, self.core, rows, cols] if self.here else self.own[block, rows, cols]
         sum_ = own.astype(F32) + self.other[block, rows, cols].astype(F32)
         for i in got:
@@ -104,7 +108,7 @@
                 self.load().wait()
             self.swap().wait_recv()
         for t in range(3):
-            p1, p2, p3 = (self.xyz[axis] for axis in ORDER[t])
+            p1, p2, p3 = (self.xyz[axis] for axis in self.order[t])
             if n:
                 self.hop(t, n - 1).wait_recv()
             if n == 0:
@@ -398,50 +402,189 @@
     return dgate.astype(BF16), dup.astype(BF16)
 
 
-def forward_kernel(x, wg, wu, wd, h1, at, act, gate, up):
+def forward_kernel(x, dy, wg, wu, wd, h1, a1, a1t, dyt, at, act, gate, up):
     h = x[...]
     _, _, a = norm(h)
     at[...] = a.T
+    dyt[...] = dy[...].T
     g = dot(a, wg[...])
     u = dot(a, wu[...])
     gate[...] = g
     up[...] = u
     s = (g * jax.nn.sigmoid(g) * u).astype(BF16)
     act[...] = s
-    h1[...] = h + dot(s, wd[...]).astype(BF16)
-
-
-def last_kernel(h1, dy, wg, wu, wd, at, dyt, act, dgate, dup):
-    _, _, a = norm(h1[...])
-    at[...] = a.T
-    dyt[...] = dy[...].T
-    g = dot(a, wg[...])
-    u = dot(a, wu[...])
-    act[...] = (g * jax.nn.sigmoid(g) * u).astype(BF16)
-    dact = dot_t(dy[...], wd[...]).astype(BF16)
-    dgate[...], dup[...] = gated_back(g, u, dact)
-
-
-def between_kernel(dg1, du1, h1, dy, gate, up, wg, wu, wd, gg, gu, dht, dgate, dup, og, ou, *scratch):
+    h = h + dot(s, wd[...]).astype(BF16)
+    h1[...] = h
+    _, _, a = norm(h)
+    a1[...] = a
+    a1t[...] = a.T
+
+
+def pieces(count):
+    n = TOKENS // count
+    return [slice(n * i, n * i + n) for i in range(count)]
+
+
+def wide_block(at, dg):
+    return dot(at[...], dg[...]).reshape(8, 2, 56, dg.shape[-1]).astype(BF16)
+
+
+def last_kernel(hbm_a, hbm_at, hbm_dy, hbm_dyt, hbm_h, wg, wu, wd, gd, og, ou, out_dh, out_dht, *scratch):
+    a, at, dy, dyt, h, act, dg, du, acc_g, acc_u, own_g, own_u, lsem, osem = scratch[:14]
     step = pl.program_id(0)
-    units = [Reduce(WIDE, gg, og, scratch[:RS_SCRATCH]), Reduce(WIDE, gu, ou, scratch[RS_SCRATCH:])]
+    sources = (hbm_a, hbm_dy, hbm_at, hbm_dyt, hbm_h)
+    loads = [pltpu.make_async_copy(s, d, lsem.at[i]) for i, (s, d) in enumerate(zip(sources, (a, dy, at, dyt, h), strict=True))]
+
+    def first(i):
+        @pl.when(step == 0)
+        def _():
+            loads[i].wait()
+
+    def units(k):
+        columns = pl.ds(pl.multiple_of(k * NB, NB), NB)
+        rest = [ref.at[k % 2] for ref in scratch[14:]]
+        return [
+            Reduce(PAIR, own, out.at[:, columns], rest[RS_SCRATCH * i : RS_SCRATCH * (i + 1)], turn=i)
+            for i, (own, out) in enumerate(((own_g, og), (own_u, ou)))
+        ]
+
+    def reduce(k, *stages):
+        for stage in stages:
+            for u in units(k):
+                if stage == "start":
+                    u.start()
+                elif stage == "finish":
+                    u.finish()
+                else:
+                    u.stage(stage)
 
     @pl.when(step == 0)
     def _():
-        for u in units:
-            u.start()
-
-    da = dot_t(dg1[...], wg[...]).astype(BF16) + dot_t(du1[...], wu[...]).astype(BF16)
-    wide, scale, _ = norm(h1[...])
-    d = da.astype(F32)
-    through = d * scale - wide * (scale * scale * scale * (jnp.sum(d * wide, -1, keepdims=True) / D))
-    dh = dy[...] + through.astype(BF16)
-    dht[...] = dh.T
-    dact = dot_t(dh, wd[...]).astype(BF16)
-    dgate[...], dup[...] = gated_back(gate[...], up[...], dact)
-    plan = {when: [(u, stage) for u in units] for when, stage in ((1, 0), (4, 1), (6, 2))}
-    plan[7] = [(u, stage) for stage in (3, "finish") for u in units]
+        for c in loads:
+            c.start()
+        acc_g[...] = jnp.zeros_like(acc_g)
+        acc_u[...] = jnp.zeros_like(acc_u)
+        loads[0].wait()
+        loads[1].wait()
+
+    def projections(r):
+        g = dot(a[r], wg[...])
+        u = dot(a[r], wu[...])
+        dact = dot_t(dy[r], wd[...]).astype(BF16)
+        act[r] = (g * jax.nn.sigmoid(g) * u).astype(BF16)
+        dg[r], du[r] = gated_back(g, u, dact)
+
+    quarters = pieces(4)
+    for r in quarters[:2]:
+        projections(r)
+
+    @pl.when(step > 0)
+    def _():
+        reduce(step - 1, 2)
+
+    for r in quarters[2:]:
+        projections(r)
+
+    @pl.when(step > 0)
+    def _():
+        reduce(step - 1, 3, "finish")
+
+    first(2)
+    own_g[...] = wide_block(at, dg)
+    own_u[...] = wide_block(at, du)
+    reduce(step, "start")
+    first(3)
+    gd[...] = dot(dyt[...], act[...]).astype(BF16).T
+    reduce(step, 0)
+    for r in quarters:
+        acc_g[r] += dot_t(dg[r], wg[...])
+        acc_u[r] += dot_t(du[r], wu[...])
+    reduce(step, 1)
+
+    @pl.when(step == STEPS - 1)
+    def _():
+        loads[4].wait()
+
+        def through(i, carry):
+            r = pl.ds(pl.multiple_of(i * 256, 256), 256)
+            d = (acc_g[r].astype(BF16) + acc_u[r].astype(BF16)).astype(F32)
+            wide, scale, _ = norm(h[r])
+            d = d * scale - wide * (scale * scale * scale * (jnp.sum(d * wide, -1, keepdims=True) / D))
+            d = dy[r] + d.astype(BF16)
+            a[r] = d
+            at[:, r] = d.T
+            return carry
+
+        lax.fori_loop(0, 4, through, 0)
+        reduce(step, 2)
+        lax.fori_loop(4, 8, through, 0)
+        stores = [pltpu.make_async_copy(s, d, osem.at[i]) for i, (s, d) in enumerate(((a, out_dh), (at, out_dht)))]
+        for c in stores:
+            c.start()
+        reduce(step, 3, "finish")
+        for c in stores:
+            c.wait()
+
+
+SETS = 5
+
+
+def lower_kernel(dh, dht, at, act, gate, up, wd, gd1, g1, u1, od1, od, og, ou, factor, *scratch):
+    step = pl.program_id(0)
+    dg, du, own_g, own_u, own_d, half_d1 = scratch[:6]
+    rest = scratch[6:]
+    sets = [rest[RS_SCRATCH * i : RS_SCRATCH * (i + 1)] for i in range(2 + 2 * SETS)]
+    d1 = Reduce(TALL, gd1, od1, sets[0], half_d1)
+    d = Reduce(TALL, own_d, od, sets[1], turn=1)
+
+    @pl.when(step == 0)
+    def _():
+        d1.start()
+
+    @pl.when(step < STEPS)
+    def _():
+        rows = pl.ds(pl.multiple_of(step * NB, NB), NB)
+        own_d.reshape(FF, D)[rows] = dot(dht[...], act[...]).astype(BF16).T
+
+    @pl.when(step >= STEPS)
+    def _():
+        for r in pieces(4):
+            dact = dot_t(dh[r], wd[...]).astype(BF16)
+            dg[r], du[r] = gated_back(gate[r], up[r], dact)
+        i = (step - STEPS) % SETS
+        own_g[i] = wide_block(at, dg)
+        own_u[i] = wide_block(at, du)
+
+    plan = {when: [] for when in range(3 * STEPS)}
+    for when, unit, stage in ((2, d1, 0), (6, d1, 1), (8, d1, 2), (10, d1, 3), (4, d, "start"), (6, d, 0), (9, d, 1), (11, d, 2), (12, d, 3)):
+        plan[when].append((unit, stage))
+    tail = []
+    for j in range(2 * STEPS):
+        k = j % SETS
+        pair = [
+            Reduce(BLOCK, own.at[k], out.at[:, BN * j : BN * j + BN], sets[2 + 2 * k + i], turn=(i + j) % 3)
+            for i, (own, out) in enumerate(((own_g, og), (own_u, ou)))
+        ]
+        for n, stage in enumerate(("start", 0, 1, 2, 3)):
+            when = STEPS + j + n
+            late = when - (3 * STEPS - 1)
+            for unit in pair:
+                if late <= 0:
+                    plan[when].append((unit, stage))
+                else:
+                    tail.append((late, unit, stage))
+        last = [(unit, "finish") for unit in pair]
+        if STEPS + j + 4 < 3 * STEPS:
+            plan[STEPS + j + 4] += last
+        else:
+            tail += [(9, *entry) for entry in last]
+    tail = [entry[1:] for entry in sorted(tail, key=lambda entry: entry[0])]
+    plan[3 * STEPS - 1] += tail + [(d1, "finish"), (d, "finish")]
     at_end_of(step, plan)
+
+    @pl.when(step == 3 * STEPS - 1)
+    def _():
+        clip_factor([g1, u1, od1, od, og, ou], factor, *rest[RS_SCRATCH * (2 + 2 * SETS) :])
 
 
 def rows(cols):
@@ -468,158 +611,87 @@
     return pltpu.CompilerParams(vmem_limit_bytes=60 * 1024 * 1024, has_side_effects=remote)
 
 
-def forward(x, wg, wu, wd):
+def shard(kind):
+    return pl.BlockSpec(kind[:2], lambda i: (0, 0))
+
+
+def forward(x, dy, wg, wu, wd):
     return pl.pallas_call(
         forward_kernel,
         grid=(TOKENS // TM,),
-        in_specs=[SEQ, weight(0, (D, FF)), weight(0, (D, FF)), weight(0, (FF, D))],
-        out_specs=[rows(D), COLUMNS, rows(FF), rows(FF), rows(FF)],
-        out_shape=[matrix(TOKENS, D), matrix(D, TOKENS), matrix(TOKENS, FF), matrix(TOKENS, FF, F32), matrix(TOKENS, FF, F32)],
+        in_specs=[SEQ, SEQ, weight(0, (D, FF)), weight(0, (D, FF)), weight(0, (FF, D))],
+        out_specs=[rows(D), rows(D), COLUMNS, COLUMNS, COLUMNS, rows(FF), rows(FF), rows(FF)],
+        out_shape=[matrix(TOKENS, D)] * 2 + [matrix(D, TOKENS)] * 3 + [matrix(TOKENS, FF)] + [matrix(TOKENS, FF, F32)] * 2,
         compiler_params=params(),
         cost_estimate=cost(3),
         name="forward",
-    )(x, wg, wu, wd)
-
-
-def last(h1, dy, wg, wu, wd):
+    )(x, dy, wg, wu, wd)
+
+
+def last(a, at, dy, dyt, h, wg, wu, wd):
+    wide = pl.BlockSpec((None, D, NB), lambda i: (1, 0, i))
+    straight, turned = pltpu.VMEM((TOKENS, D), BF16), pltpu.VMEM((D, TOKENS), BF16)
+    hidden, sums = pltpu.VMEM((TOKENS, NB), BF16), pltpu.VMEM((TOKENS, D), F32)
+    own = pltpu.VMEM((8, 2, *PAIR[:2]), BF16)
     return pl.pallas_call(
         last_kernel,
-        grid=(TOKENS // TM,),
-        in_specs=[rows(D), SEQ, weight(1, (D, FF)), weight(1, (D, FF)), weight(1, (FF, D))],
-        out_specs=[COLUMNS, COLUMNS, rows(FF), rows(FF), rows(FF)],
-        out_shape=[matrix(D, TOKENS)] * 2 + [matrix(TOKENS, FF)] * 3,
-        compiler_params=params(),
-        cost_estimate=cost(3),
+        grid=(STEPS,),
+        in_specs=[ANY] * 5 + [wide, wide, pl.BlockSpec((None, NB, D), lambda i: (1, i, 0))],
+        out_specs=[pl.BlockSpec((NB, D), lambda i: (i, 0)), shard(WIDE), shard(WIDE), ANY, ANY],
+        out_shape=[matrix(FF, D), matrix(*WIDE[:2]), matrix(*WIDE[:2]), matrix(TOKENS, D), matrix(D, TOKENS)],
+        scratch_shapes=[straight, turned, straight, turned, straight, hidden, hidden, hidden, sums, sums, own, own]
+        + [pltpu.SemaphoreType.DMA((5,)), pltpu.SemaphoreType.DMA((2,))]
+        + rs_scratch(PAIR, (2,)) * 2,
+        compiler_params=params(True),
+        cost_estimate=cost(8),
         name="last",
-    )(h1, dy, wg, wu, wd)
-
-
-def shard(kind):
-    return pl.BlockSpec(kind[:2], lambda i: (0, 0))
-
-
-def between(dg1, du1, h1, dy, gate, up, wg, wu, wd, gg, gu):
-    return pl.pallas_call(
-        between_kernel,
-        grid=(TOKENS // TM,),
-        in_specs=[rows(FF), rows(FF), rows(D), SEQ, rows(FF), rows(FF)]
-        + [weight(1, (D, FF)), weight(1, (D, FF)), weight(0, (FF, D)), ANY, ANY],
-        out_specs=[COLUMNS, rows(FF), rows(FF), shard(WIDE), shard(WIDE)],
-        out_shape=[matrix(D, TOKENS)] + [matrix(TOKENS, FF)] * 2 + [matrix(*WIDE[:2])] * 2,
-        scratch_shapes=rs_scratch(WIDE, False) * 2,
-        compiler_params=params(True),
-        cost_estimate=cost(3),
-        name="between",
-    )(dg1, du1, h1, dy, gate, up, wg, wu, wd, gg, gu)
-
-
-def tall_into(g, i, dt, act):
-    g.reshape(FF, D)[pl.ds(pl.multiple_of(i * NB, NB), NB)] = dot(dt[...], act[...]).astype(BF16).T
-
-
-def wide_block(at, dg):
-    return dot(at[...], dg[...]).reshape(8, 2, 56, NB).astype(BF16)
-
-
-def upper_kernel(dt, at, act, dg, du, gg, gu, od, *scratch):
-    step = pl.program_id(0)
-    d = Reduce(TALL, None, od, scratch)
-
-    @pl.when(step < STEPS)
-    def _():
-        tall_into(d.g, step, dt, act)
-
-    @pl.when((step >= STEPS) & (step < 2 * STEPS))
-    def _():
-        gg[...] = wide_block(at, dg)
-
-    @pl.when(step >= 2 * STEPS)
-    def _():
-        gu[...] = wide_block(at, du)
-
-    at_end_of(step, {4: [(d, "start")], 6: [(d, 0)], 11: [(d, 1)], 13: [(d, 2)], 14: [(d, 3), (d, "finish")]})
-
-
-def lower_kernel(dt, at, act, dg, du, d1, g1, u1, od, og, ou, factor, *scratch):
-    step = pl.program_id(0)
-    d, g, u = (
-        Reduce(kind, None, o, scratch[RS_SCRATCH * i : RS_SCRATCH * (i + 1)])
-        for i, (kind, o) in enumerate(((TALL, od), (WIDE, og), (WIDE, ou)))
-    )
-
-    @pl.when(step < STEPS)
-    def _():
-        tall_into(d.g, step, dt, act)
-
-    def columns(first):
-        return pl.ds(pl.multiple_of((step - first) * NB, NB), NB)
-
-    @pl.when((step >= STEPS) & (step < 2 * STEPS))
-    def _():
-        g.g[:, :, :, columns(STEPS)] = wide_block(at, dg)
-
-    @pl.when(step >= 2 * STEPS)
-    def _():
-        u.g[:, :, :, columns(2 * STEPS)] = wide_block(at, du)
-
-    tail = [(u, "start"), (d, 3), (g, 1), (u, 0), (g, 2), (u, 1), (g, 3), (u, 2), (u, 3)]
-    at_end_of(
-        step,
-        {4: [(d, "start")], 6: [(d, 0)], 9: [(g, "start")], 11: [(d, 1), (g, 0)], 13: [(d, 2)]}
-        | {14: tail + [(unit, "finish") for unit in (d, g, u)]},
-    )
-
-    @pl.when(step == 3 * STEPS - 1)
-    def _():
-        clip_factor([d1, g1, u1, od, og, ou], factor, *scratch[3 * RS_SCRATCH :])
-
-
+    )(a, at, dy.reshape(TOKENS, D), dyt, h, wg, wu, wd)
+
+
+WHOLE_S = pl.BlockSpec((TOKENS, D), lambda i: (0, 0), pipeline_mode=pl.Buffered(1))
 WHOLE_T = pl.BlockSpec((D, TOKENS), lambda i: (0, 0), pipeline_mode=pl.Buffered(1))
 
 
-def in_turn(turn, block, index):
-    return pl.BlockSpec(block, lambda i: index(jnp.clip(i - turn * STEPS, 0, STEPS - 1)))
-
-
-COLUMNS_IN_TURN = [in_turn(turn, (TOKENS, NB), lambda i: (0, i)) for turn in range(3)]
-
-
-def upper_gradients(dt, at, act, dg, du):
-    return pl.pallas_call(
-        upper_kernel,
-        grid=(3 * STEPS,),
-        in_specs=[WHOLE_T, WHOLE_T, *COLUMNS_IN_TURN],
-        out_specs=[in_turn(turn, (8, 2, 56, NB), lambda i: (0, 0, 0, i)) for turn in (1, 2)] + [shard(TALL)],
-        out_shape=[jax.ShapeDtypeStruct((8, 2, 56, FF), BF16)] * 2 + [matrix(*TALL[:2])],
-        scratch_shapes=rs_scratch(TALL, True),
-        compiler_params=params(True),
-        cost_estimate=cost(3),
-        name="upper_gradients",
-    )(dt, at, act, dg, du)
-
-
-def lower_gradients(dt, at, act, dg, du, before):
-    kinds = (TALL, WIDE, WIDE)
+def lower(dh, dht, at, act, gate, up, wd, gd1, g1, u1):
+    def later(i):
+        return jnp.maximum(i - STEPS, 0)
+
+    block = pl.BlockSpec((TOKENS, BN), lambda i: (0, later(i)))
+    outs = (TALL, TALL, WIDE, WIDE)
     return pl.pallas_call(
         lower_kernel,
         grid=(3 * STEPS,),
-        in_specs=[WHOLE_T, WHOLE_T, *COLUMNS_IN_TURN] + [shard(k) for k in kinds],
-        out_specs=[shard(k) for k in kinds] + [pl.BlockSpec((8, 128), lambda i: (0, 0))],
-        out_shape=[matrix(*k[:2]) for k in kinds] + [matrix(8, 128, F32)],
-        scratch_shapes=sum((rs_scratch(k, True) for k in kinds), []) + CLIP_SCRATCH,
+        in_specs=[
+            WHOLE_S,
+            WHOLE_T,
+            WHOLE_T,
+            pl.BlockSpec((TOKENS, NB), lambda i: (0, jnp.minimum(i, STEPS - 1))),
+            block,
+            block,
+            pl.BlockSpec((None, BN, D), lambda i: (0, later(i), 0)),
+            ANY,
+            shard(WIDE),
+            shard(WIDE),
+        ],
+        out_specs=[shard(k) for k in outs] + [pl.BlockSpec((8, 128), lambda i: (0, 0))],
+        out_shape=[matrix(*k[:2]) for k in outs] + [matrix(8, 128, F32)],
+        scratch_shapes=[pltpu.VMEM((TOKENS, BN), BF16)] * 2
+        + [pltpu.VMEM((SETS, 8, 2, *BLOCK[:2]), BF16)] * 2
+        + [pltpu.VMEM((8, 2, *TALL[:2]), BF16), pltpu.VMEM((8, *TALL[:2]), BF16)]
+        + rs_scratch(TALL) * 2
+        + rs_scratch(BLOCK) * (2 * SETS)
+        + CLIP_SCRATCH,
         compiler_params=params(True),
-        cost_estimate=cost(3),
-        name="lower_gradients",
-    )(dt, at, act, dg, du, *before)
+        cost_estimate=cost(4),
+        name="lower",
+    )(dh, dht, at, act, gate, up, wd, gd1.reshape(8, 2, *TALL[:2]), g1, u1)
 
 
 def solution(mesh):
     def step(x, dy, wg, wu, wd, *moments):
-        h1, a0, act0, gate0, up0 = forward(x, wg, wu, wd)
-        a1, dyt, act1, dg1, du1 = last(h1, dy, wg, wu, wd)
-        gg1, gu1, d1 = upper_gradients(dyt, a1, act1, dg1, du1)
-        dht, dg0, du0, g1, u1 = between(dg1, du1, h1, dy, gate0, up0, wg, wu, wd, gg1, gu1)
-        d0, g0, u0, factor = lower_gradients(dht, a0, act0, dg0, du0, (d1, g1, u1))
+        h1, a1, a1t, dyt, a0t, act0, gate0, up0 = forward(x, dy, wg, wu, wd)
+        gd1, g1, u1, dh, dht = last(a1, a1t, dy, dyt, h1, wg, wu, wd)
+        d1, d0, g0, u0, factor = lower(dh, dht, a0t, act0, gate0, up0, wd, gd1, g1, u1)
         own, new_moments = adamw(factor, (g0, u0, d0, g1, u1, d1), moments[:3], moments[3:], (wg, wu, wd))
         return (*all_gather(own), *new_moments)
 

time: 397 us -> 386 us (0.972)
  Pallas kernels: 396 us -> 385 us
    pallas_call x5 -> x3, Pallas kernels: 280 us -> 270 us  [the longest x1 119 us: last(): pl.pallas_call(last_kernel, grid=(STEPS,), in_specs=[ANY] * 5 + [wide, wi...]
where the time goes in v6:
time: 386 us
  Pallas kernels  385 us (100%)
    pallas_call x1, Pallas kernels, last(): pl.pallas_call(last_kernel, grid=(STEPS,), in_specs=[ANY] * 5 + [wide, wi...  119 us
    pallas_call x1, Pallas kernels, lower(): pl.pallas_call(lower_kernel, grid=(3 * STEPS,), in_specs=[WHOLE_S, WHOLE_...  105 us
    pallas_call x1, Pallas kernels, all_gather(): pl.pallas_call(gather_kernel, out_shape=[pltpu.VMEM((2, 2, 2, 2, 2, *o.sh...  98 us
    pallas_call x1, Pallas kernels, forward(): pl.pallas_call(forward_kernel, grid=(TOKENS // TM,), in_specs=[SEQ, SEQ,...  45.7 us
    pallas_call x1, Pallas kernels, all_gather(): pl.pallas_call(flush_kernel, out_shape=[jax.ShapeDtypeStruct(o.shape, BF1...  9.23 us

profile of v6, /device:TPU:0, one launch (start us, length us, event | category | flops | bytes accessed | tf_op | source)
XLA Modules:
  0.0 385.8 jit_solution(1628934883337714358)
XLA Ops:
  0.6 45.7 %forward.1 = (bf16[2048,896]{1,0:T(8,128)(2,1)}, bf16[2048,896]{1,0:T(8,128)(2,1)}, bf16[896,2048]{1,0:T(8,128)(2,1)}, bf16[896,2048]{1,0:T(8,128)(2,1)}, bf16[8...) custom-call(bf16[1,2048,896]{2,1,0:T(8,128)(2,1)} %x.1, ...), custom_call_target="tpu_custom_call" | custom-call | flops 28185722880 | bytes 62914560 | tf_op jit(solution)/shard_map/forward/pallas_call | solution.py:619
  46.3 119.5 %last.1 = (bf16[2560,896]{1,0:T(8,128)(2,1)}, bf16[56,2560]{1,0:T(8,128)(2,1)}, bf16[56,2560]{1,0:T(8,128)(2,1)}, bf16[2048,896]{1,0:T(8,128)(2,1)}, bf16[896,2048]{1,0:T(8,128)(2,1)}) custom-call(bf16[2048,896]{1,0:T(8,128)(2,1)} %get-tuple-element.42.hbm_a, bf16[896,2048]{1,0:T(8,128)(2,1)} %get-tuple-element.43.hbm_at, bf16[2048,896]{1,0:T(8,128)(2,1)} %bitcast.8, ...), custom_call_target="tpu_custom_call" | custom-call | flops 75161927680 | bytes 62914560 | tf_op jit(solution)/shard_map/last/pallas_call | solution.py:636
  165.8 104.8 %lower.1 = (bf16[160,896]{1,0:T(8,128)(2,1)}, bf16[160,896]{1,0:T(8,128)(2,1)}, bf16[56,2560]{1,0:T(8,128)(2,1)}, bf16[56,2560]{1,0:T(8,128)(2,1)}, f32[8,128]{1,0:T(8,128)}) custom-call(bf16[2048,896]{1,0:T(8,128)(2,1)} %get-tuple-element.46.dh, bf16[896,2048]{1,0:T(8,128)(2,1)} %get-tuple-element.47.dht, bf16[896,2048]{1,0:T(8,128)(2,1)} %get-tuple-element.48.at, ...), custom_call_target="tpu_custom_call" | custom-call | flops 37580963840 | bytes 62914560 | tf_op jit(solution)/shard_map/lower/pallas_call | solution.py:661
  270.6 7.7 %adamw.1 = (bf16[2,56,2560]{2,1,0:T(8,128)(2,1)S(1)}, bf16[2,56,2560]{2,1,0:T(8,128)(2,1)S(1)}, bf16[2,160,896]{2,1,0:T(8,128)(2,1)S(1)}, f32[2,56,2560]{2,1,0:T...) custom-call(f32[8,128]{1,0:T(8,128)} %get-tuple-element.55.refs_0_, ...), custom_call_target="tpu_custom_call" | custom-call | tf_op jit(solution)/shard_map/adamw/pallas_call | solution.py:370
  278.3 98.0 %all_gather.1 = (bf16[2,2,2,2,2,56,2560]{6,5,4,3,2,1,0:T(8,128)(2,1)S(1)}, bf16[2,2,2,2,2,56,2560]{6,5,4,3,2,1,0:T(8,128)(2,1)S(1)}, bf16[2,2,2,2,2,160,896]{6,5,4,3,2,1,0:T(8,128)(2,1)S(1)}) custom-call(bf16[2,56,2560]{2,1,0:T(8,128)(2,1)S(1)} %get-tuple-element.60.refs_0_, bf16[2,56,2560]{2,1,0:T(8,128)(2,1)S(1)} %get-tuple-element.61.refs_1_, ...), custom_call_target="tpu_custom_call" | custom-call | tf_op jit(solution)/shard_map/all_gather/pallas_call | solution.py:285
  376.3 9.2 %flush.1 = (bf16[2,2,2,2,2,56,2560]{6,5,4,3,2,1,0:T(8,128)(2,1)}, bf16[2,2,2,2,2,56,2560]{6,5,4,3,2,1,0:T(8,128)(2,1)}, bf16[2,2,2,2,2,160,896]{6,5,4,3,2,1,0:T(8,128)(2,1)}) custom-call(bf16[2,2,2,2,2,56,2560]{6,5,4,3,2,1,0:T(8,128)(2,1)S(1)} %get-tuple-element.63.refs_0_, bf16[2,2,2,2,2,56,2560]{6,5,4,3,2,1,0:T(8,128)(2,1)S(1)} %get-tuple-element.64.refs_1_, ...), custom_call_target="tpu_custom_call" | custom-call | tf_op jit(solution)/shard_map/flush/pallas_call | solution.py:298

commit v7 on v6

--- a/solution.py
+++ b/solution.py
@@ -24,6 +24,10 @@
 BLOCK = (56, 256, tuple((s, slice(0, 256)) for s in (slice(0, 24), slice(24, 40), slice(40, 56))))
 PAIR = (56, 512, tuple((s, slice(0, 512)) for s in (slice(0, 24), slice(24, 40), slice(40, 56))))
 TALL = (160, 896, tuple((s, slice(0, 896)) for s in (slice(0, 56), slice(56, 112), slice(112, 160))))
+SPLIT = tuple(
+    (slice(c, c + n), (160, n, tuple((s, slice(0, n)) for s in (slice(0, 56), slice(56, 112), slice(112, 160)))))
+    for c, n in ((0, 512), (512, 384))
+)
 
 
 def size(s):
@@ -126,6 +130,14 @@
             if n < 3:
                 self.hop(t, n).start()
 
+    def run(self, stage):
+        if stage == "start":
+            self.start()
+        elif stage == "finish":
+            self.finish()
+        else:
+            self.stage(stage)
+
     def finish(self):
         self.swap().wait_send()
         for t in range(3):
@@ -176,12 +188,7 @@
         @pl.when(step == when)
         def _(entries=entries):
             for unit, stage in entries:
-                if stage == "start":
-                    unit.start()
-                elif stage == "finish":
-                    unit.finish()
-                else:
-                    unit.stage(stage)
+                unit.run(stage)
 
 
 class Gather:
@@ -429,162 +436,152 @@
     return dot(at[...], dg[...]).reshape(8, 2, 56, dg.shape[-1]).astype(BF16)
 
 
-def last_kernel(hbm_a, hbm_at, hbm_dy, hbm_dyt, hbm_h, wg, wu, wd, gd, og, ou, out_dh, out_dht, *scratch):
-    a, at, dy, dyt, h, act, dg, du, acc_g, acc_u, own_g, own_u, lsem, osem = scratch[:14]
+def upper_kernel(a, dy, dyt, wg, wu, wd, gd, dg, du, act):
+    for c in (slice(0, 256), slice(256, 512)):
+        g = dot(a[...], wg[:, c])
+        u = dot(a[...], wu[:, c])
+        dact = dot_t(dy[...], wd[c]).astype(BF16)
+        act[:, c] = (g * jax.nn.sigmoid(g) * u).astype(BF16)
+        dg[:, c], du[:, c] = gated_back(g, u, dact)
+        gd[c] = dot(dyt[...], act[:, c]).astype(BF16).T
+
+
+LAST_SETS = 3
+
+
+def last_kernel(at_in, h_in, dy, dg, du, wg, wu, gd1, og, ou, od1, out_dh, out_dht, *scratch):
+    at, acc_g, acc_u, dh, own_g, own_u, half_d1, lsem, osem = scratch[:9]
     step = pl.program_id(0)
-    sources = (hbm_a, hbm_dy, hbm_at, hbm_dyt, hbm_h)
-    loads = [pltpu.make_async_copy(s, d, lsem.at[i]) for i, (s, d) in enumerate(zip(sources, (a, dy, at, dyt, h), strict=True))]
-
-    def first(i):
-        @pl.when(step == 0)
-        def _():
-            loads[i].wait()
-
-    def units(k):
+    d1 = Reduce(TALL, gd1, od1, scratch[9 : 9 + RS_SCRATCH], half_d1)
+
+    def reduce(k, *stages):
+        i = k % LAST_SETS
+        rest = [ref.at[i] for ref in scratch[9 + RS_SCRATCH :]]
         columns = pl.ds(pl.multiple_of(k * NB, NB), NB)
-        rest = [ref.at[k % 2] for ref in scratch[14:]]
-        return [
-            Reduce(PAIR, own, out.at[:, columns], rest[RS_SCRATCH * i : RS_SCRATCH * (i + 1)], turn=i)
-            for i, (own, out) in enumerate(((own_g, og), (own_u, ou)))
+        units = [
+            Reduce(PAIR, own.at[i], out.at[:, columns], rest[RS_SCRATCH * n : RS_SCRATCH * (n + 1)], turn=n)
+            for n, (own, out) in enumerate(((own_g, og), (own_u, ou)))
         ]
-
-    def reduce(k, *stages):
         for stage in stages:
-            for u in units(k):
-                if stage == "start":
-                    u.start()
-                elif stage == "finish":
-                    u.finish()
-                else:
-                    u.stage(stage)
+            for u in units:
+                u.run(stage)
+
+    load = pltpu.make_async_copy(at_in, at, lsem.at[0])
+    load_h = pltpu.make_async_copy(h_in, dh, lsem.at[1])
 
     @pl.when(step == 0)
     def _():
-        for c in loads:
-            c.start()
+        load.start()
+        load_h.start()
+        d1.start()
         acc_g[...] = jnp.zeros_like(acc_g)
         acc_u[...] = jnp.zeros_like(acc_u)
-        loads[0].wait()
-        loads[1].wait()
-
-    def projections(r):
-        g = dot(a[r], wg[...])
-        u = dot(a[r], wu[...])
-        dact = dot_t(dy[r], wd[...]).astype(BF16)
-        act[r] = (g * jax.nn.sigmoid(g) * u).astype(BF16)
-        dg[r], du[r] = gated_back(g, u, dact)
-
-    quarters = pieces(4)
-    for r in quarters[:2]:
-        projections(r)
+        load.wait()
+
+    i = step % LAST_SETS
+    own_g[i] = wide_block(at, dg)
+    own_u[i] = wide_block(at, du)
+
+    @pl.when(step > 1)
+    def _():
+        reduce(step - 2, 3, "finish")
+
+    @pl.when(step > 0)
+    def _():
+        reduce(step - 1, 1)
+
+    reduce(step, "start")
+    at_end_of(step, {1: [(d1, 1)], 2: [(d1, 2)], 3: [(d1, 3), (d1, "finish")]})
+    blocks = [slice(c, min(c + 256, D)) for c in range(0, D, 256)]
+    for c in blocks:
+        acc_g[:, c] += dot_t(dg[...], wg[c])
+    reduce(step, 0)
+    at_end_of(step, {0: [(d1, 0)]})
+    for c in blocks:
+        acc_u[:, c] += dot_t(du[...], wu[c])
 
     @pl.when(step > 0)
     def _():
         reduce(step - 1, 2)
 
-    for r in quarters[2:]:
-        projections(r)
-
-    @pl.when(step > 0)
-    def _():
-        reduce(step - 1, 3, "finish")
-
-    first(2)
-    own_g[...] = wide_block(at, dg)
-    own_u[...] = wide_block(at, du)
-    reduce(step, "start")
-    first(3)
-    gd[...] = dot(dyt[...], act[...]).astype(BF16).T
-    reduce(step, 0)
-    for r in quarters:
-        acc_g[r] += dot_t(dg[r], wg[...])
-        acc_u[r] += dot_t(du[r], wu[...])
-    reduce(step, 1)
-
     @pl.when(step == STEPS - 1)
     def _():
-        loads[4].wait()
-
         def through(i, carry):
             r = pl.ds(pl.multiple_of(i * 256, 256), 256)
             d = (acc_g[r].astype(BF16) + acc_u[r].astype(BF16)).astype(F32)
-            wide, scale, _ = norm(h[r])
+            wide, scale, _ = norm(dh[r])
             d = d * scale - wide * (scale * scale * scale * (jnp.sum(d * wide, -1, keepdims=True) / D))
             d = dy[r] + d.astype(BF16)
-            a[r] = d
+            dh[r] = d
             at[:, r] = d.T
             return carry
 
-        lax.fori_loop(0, 4, through, 0)
-        reduce(step, 2)
-        lax.fori_loop(4, 8, through, 0)
-        stores = [pltpu.make_async_copy(s, d, osem.at[i]) for i, (s, d) in enumerate(((a, out_dh), (at, out_dht)))]
+        load_h.wait()
+        reduce(step - 1, 3, "finish")
+        lax.fori_loop(0, 3, through, 0)
+        reduce(step, 1)
+        lax.fori_loop(3, 8, through, 0)
+        stores = [pltpu.make_async_copy(s, d, osem.at[i]) for i, (s, d) in enumerate(((dh, out_dh), (at, out_dht)))]
         for c in stores:
             c.start()
-        reduce(step, 3, "finish")
+        reduce(step, 2, 3, "finish")
         for c in stores:
             c.wait()
 
 
-SETS = 5
-
-
-def lower_kernel(dh, dht, at, act, gate, up, wd, gd1, g1, u1, od1, od, og, ou, factor, *scratch):
+SETS = 7
+LOWER_STEPS = 2 * STEPS + 2 * STEPS
+
+
+def lower_kernel(dh, dht, at, act, gate, up, wd, d1, g1, u1, od, og, ou, factor, *scratch):
     step = pl.program_id(0)
-    dg, du, own_g, own_u, own_d, half_d1 = scratch[:6]
+    dg, du, own_g, own_u = scratch[:4]
+    own_d = scratch[4:6]
     rest = scratch[6:]
-    sets = [rest[RS_SCRATCH * i : RS_SCRATCH * (i + 1)] for i in range(2 + 2 * SETS)]
-    d1 = Reduce(TALL, gd1, od1, sets[0], half_d1)
-    d = Reduce(TALL, own_d, od, sets[1], turn=1)
-
-    @pl.when(step == 0)
+    sets = [rest[RS_SCRATCH * i : RS_SCRATCH * (i + 1)] for i in range(4)]
+
+    @pl.when(step < 2 * STEPS)
     def _():
-        d1.start()
-
-    @pl.when(step < STEPS)
-    def _():
-        rows = pl.ds(pl.multiple_of(step * NB, NB), NB)
-        own_d.reshape(FF, D)[rows] = dot(dht[...], act[...]).astype(BF16).T
-
-    @pl.when(step >= STEPS)
-    def _():
+        dact = dot_t(dh[...], wd[...]).astype(BF16)
         for r in pieces(4):
-            dact = dot_t(dh[r], wd[...]).astype(BF16)
-            dg[r], du[r] = gated_back(gate[r], up[r], dact)
-        i = (step - STEPS) % SETS
+            dg[r], du[r] = gated_back(gate[r], up[r], dact[r])
+        i = step % SETS
         own_g[i] = wide_block(at, dg)
         own_u[i] = wide_block(at, du)
 
-    plan = {when: [] for when in range(3 * STEPS)}
-    for when, unit, stage in ((2, d1, 0), (6, d1, 1), (8, d1, 2), (10, d1, 3), (4, d, "start"), (6, d, 0), (9, d, 1), (11, d, 2), (12, d, 3)):
-        plan[when].append((unit, stage))
-    tail = []
-    for j in range(2 * STEPS):
-        k = j % SETS
-        pair = [
-            Reduce(BLOCK, own.at[k], out.at[:, BN * j : BN * j + BN], sets[2 + 2 * k + i], turn=(i + j) % 3)
-            for i, (own, out) in enumerate(((own_g, og), (own_u, ou)))
-        ]
-        for n, stage in enumerate(("start", 0, 1, 2, 3)):
-            when = STEPS + j + n
-            late = when - (3 * STEPS - 1)
-            for unit in pair:
-                if late <= 0:
-                    plan[when].append((unit, stage))
-                else:
-                    tail.append((late, unit, stage))
-        last = [(unit, "finish") for unit in pair]
-        if STEPS + j + 4 < 3 * STEPS:
-            plan[STEPS + j + 4] += last
-        else:
-            tail += [(9, *entry) for entry in last]
-    tail = [entry[1:] for entry in sorted(tail, key=lambda entry: entry[0])]
-    plan[3 * STEPS - 1] += tail + [(d1, "finish"), (d, "finish")]
+    for part, (columns, kind) in enumerate(SPLIT):
+        first = (2 + part) * STEPS
+
+        @pl.when((step >= first) & (step < first + STEPS))
+        def _(part=part, columns=columns, first=first, n=kind[1]):
+            rows = pl.ds(pl.multiple_of((step - first) * NB, NB), NB)
+            own_d[part].reshape(FF, n)[rows] = dot(dht[columns], act[...]).astype(BF16).T
+
+    for late, stages in ((6, (3, "finish")), (5, (2,)), (3, (1,)), (1, (0,)), (0, ("start",))):
+
+        @pl.when((step >= late) & (step < 2 * STEPS + late))
+        def _(late=late, stages=stages):
+            j = step - late
+            k = j % SETS
+            columns = pl.ds(pl.multiple_of(j * BN, BN), BN)
+            for n, (own, out) in enumerate(((own_g, og), (own_u, ou))):
+                unit = Reduce(BLOCK, own.at[k], out.at[:, columns], [ref.at[k] for ref in sets[2 + n]], turn=n)
+                for stage in stages:
+                    unit.run(stage)
+
+    plan = {when: [] for when in (3 * STEPS - 1, 3 * STEPS + 2, LOWER_STEPS - 1)}
+    da, db = (
+        Reduce(kind, own_d[part], od.at[:, columns], sets[part], turn=1 + part) for part, (columns, kind) in enumerate(SPLIT)
+    )
+    plan[3 * STEPS - 1] += [(da, "start")]
+    plan[3 * STEPS + 2] += [(da, 0)]
+    plan[LOWER_STEPS - 1] += [(db, "start"), (da, 1), (db, 0), (da, 2), (db, 1), (da, 3), (db, 2), (db, 3)]
+    plan[LOWER_STEPS - 1] += [(da, "finish"), (db, "finish")]
     at_end_of(step, plan)
 
-    @pl.when(step == 3 * STEPS - 1)
+    @pl.when(step == LOWER_STEPS - 1)
     def _():
-        clip_factor([g1, u1, od1, od, og, ou], factor, *rest[RS_SCRATCH * (2 + 2 * SETS) :])
+        clip_factor([d1, g1, u1, od, og, ou], factor, *rest[RS_SCRATCH * 4 :])
 
 
 def rows(cols):
@@ -608,7 +605,7 @@
 
 
 def params(remote=False):
-    return pltpu.CompilerParams(vmem_limit_bytes=60 * 1024 * 1024, has_side_effects=remote)
+    return pltpu.CompilerParams(vmem_limit_bytes=67043328 if remote else 60 * 1024 * 1024, has_side_effects=remote)
 
 
 def shard(kind):
@@ -628,48 +625,63 @@
     )(x, dy, wg, wu, wd)
 
 
-def last(a, at, dy, dyt, h, wg, wu, wd):
-    wide = pl.BlockSpec((None, D, NB), lambda i: (1, 0, i))
-    straight, turned = pltpu.VMEM((TOKENS, D), BF16), pltpu.VMEM((D, TOKENS), BF16)
-    hidden, sums = pltpu.VMEM((TOKENS, NB), BF16), pltpu.VMEM((TOKENS, D), F32)
-    own = pltpu.VMEM((8, 2, *PAIR[:2]), BF16)
+WHOLE_S = pl.BlockSpec((TOKENS, D), lambda i: (0, 0), pipeline_mode=pl.Buffered(1))
+WHOLE_T = pl.BlockSpec((D, TOKENS), lambda i: (0, 0), pipeline_mode=pl.Buffered(1))
+HIDDEN = pl.BlockSpec((TOKENS, NB), lambda i: (0, i))
+WIDE_W = pl.BlockSpec((None, D, NB), lambda i: (1, 0, i))
+
+
+def upper(a, dy, dyt, wg, wu, wd):
+    return pl.pallas_call(
+        upper_kernel,
+        grid=(STEPS,),
+        in_specs=[WHOLE_S, WHOLE_S, WHOLE_T, WIDE_W, WIDE_W, pl.BlockSpec((None, NB, D), lambda i: (1, i, 0))],
+        out_specs=[pl.BlockSpec((NB, D), lambda i: (i, 0)), HIDDEN, HIDDEN],
+        out_shape=[matrix(FF, D), matrix(TOKENS, FF), matrix(TOKENS, FF)],
+        scratch_shapes=[pltpu.VMEM((TOKENS, NB), BF16)],
+        compiler_params=params(),
+        cost_estimate=cost(4),
+        name="upper",
+    )(a, dy, dyt, wg, wu, wd)
+
+
+def last(at, h, dy, dg, du, wg, wu, gd1):
+    straight, turned, sums = pltpu.VMEM((TOKENS, D), BF16), pltpu.VMEM((D, TOKENS), BF16), pltpu.VMEM((TOKENS, D), F32)
+    own = pltpu.VMEM((LAST_SETS, 8, 2, *PAIR[:2]), BF16)
     return pl.pallas_call(
         last_kernel,
         grid=(STEPS,),
-        in_specs=[ANY] * 5 + [wide, wide, pl.BlockSpec((None, NB, D), lambda i: (1, i, 0))],
-        out_specs=[pl.BlockSpec((NB, D), lambda i: (i, 0)), shard(WIDE), shard(WIDE), ANY, ANY],
-        out_shape=[matrix(FF, D), matrix(*WIDE[:2]), matrix(*WIDE[:2]), matrix(TOKENS, D), matrix(D, TOKENS)],
-        scratch_shapes=[straight, turned, straight, turned, straight, hidden, hidden, hidden, sums, sums, own, own]
-        + [pltpu.SemaphoreType.DMA((5,)), pltpu.SemaphoreType.DMA((2,))]
-        + rs_scratch(PAIR, (2,)) * 2,
+        in_specs=[ANY, ANY, WHOLE_S, HIDDEN, HIDDEN, WIDE_W, WIDE_W, ANY],
+        out_specs=[shard(WIDE), shard(WIDE), shard(TALL), ANY, ANY],
+        out_shape=[matrix(*k[:2]) for k in (WIDE, WIDE, TALL)] + [matrix(TOKENS, D), matrix(D, TOKENS)],
+        scratch_shapes=[turned, sums, sums, straight, own, own, pltpu.VMEM((8, *TALL[:2]), BF16)]
+        + [pltpu.SemaphoreType.DMA((2,)), pltpu.SemaphoreType.DMA((2,))]
+        + rs_scratch(TALL)
+        + rs_scratch(PAIR, (LAST_SETS,)) * 2,
         compiler_params=params(True),
-        cost_estimate=cost(8),
+        cost_estimate=cost(4),
         name="last",
-    )(a, at, dy.reshape(TOKENS, D), dyt, h, wg, wu, wd)
-
-
-WHOLE_S = pl.BlockSpec((TOKENS, D), lambda i: (0, 0), pipeline_mode=pl.Buffered(1))
-WHOLE_T = pl.BlockSpec((D, TOKENS), lambda i: (0, 0), pipeline_mode=pl.Buffered(1))
-
-
-def lower(dh, dht, at, act, gate, up, wd, gd1, g1, u1):
-    def later(i):
-        return jnp.maximum(i - STEPS, 0)
-
-    block = pl.BlockSpec((TOKENS, BN), lambda i: (0, later(i)))
-    outs = (TALL, TALL, WIDE, WIDE)
+    )(at, h, dy, dg, du, wg, wu, gd1.reshape(8, 2, *TALL[:2]))
+
+
+def lower(dh, dht, at, act, gate, up, wd, shards):
+    def column(i):
+        return jnp.minimum(i, 2 * STEPS - 1)
+
+    block = pl.BlockSpec((TOKENS, BN), lambda i: (0, column(i)))
+    outs = (TALL, WIDE, WIDE)
     return pl.pallas_call(
         lower_kernel,
-        grid=(3 * STEPS,),
+        grid=(LOWER_STEPS,),
         in_specs=[
             WHOLE_S,
             WHOLE_T,
             WHOLE_T,
-            pl.BlockSpec((TOKENS, NB), lambda i: (0, jnp.minimum(i, STEPS - 1))),
+            pl.BlockSpec((TOKENS, NB), lambda i: (0, jnp.maximum(i - 2 * STEPS, 0) % STEPS)),
             block,
             block,
-            pl.BlockSpec((None, BN, D), lambda i: (0, later(i), 0)),
-            ANY,
+            pl.BlockSpec((None, BN, D), lambda i: (0, column(i), 0)),
+            shard(TALL),
             shard(WIDE),
             shard(WIDE),
         ],
@@ -677,21 +689,23 @@
         out_shape=[matrix(*k[:2]) for k in outs] + [matrix(8, 128, F32)],
         scratch_shapes=[pltpu.VMEM((TOKENS, BN), BF16)] * 2
         + [pltpu.VMEM((SETS, 8, 2, *BLOCK[:2]), BF16)] * 2
-        + [pltpu.VMEM((8, 2, *TALL[:2]), BF16), pltpu.VMEM((8, *TALL[:2]), BF16)]
-        + rs_scratch(TALL) * 2
-        + rs_scratch(BLOCK) * (2 * SETS)
+        + [pltpu.VMEM((8, 2, *kind[:2]), BF16) for _, kind in SPLIT]
+        + sum((rs_scratch(kind) for _, kind in SPLIT), [])
+        + rs_scratch(BLOCK, (SETS,)) * 2
         + CLIP_SCRATCH,
         compiler_params=params(True),
         cost_estimate=cost(4),
         name="lower",
-    )(dh, dht, at, act, gate, up, wd, gd1.reshape(8, 2, *TALL[:2]), g1, u1)
+    )(dh, dht, at, act, gate, up, wd, *shards)
 
 
 def solution(mesh):
     def step(x, dy, wg, wu, wd, *moments):
         h1, a1, a1t, dyt, a0t, act0, gate0, up0 = forward(x, dy, wg, wu, wd)
-        gd1, g1, u1, dh, dht = last(a1, a1t, dy, dyt, h1, wg, wu, wd)
-        d1, d0, g0, u0, factor = lower(dh, dht, a0t, act0, gate0, up0, wd, gd1, g1, u1)
+        flat_dy = dy.reshape(TOKENS, D)
+        gd1, dg1, du1 = upper(a1, flat_dy, dyt, wg, wu, wd)
+        g1, u1, d1, dh, dht = last(a1t, h1, flat_dy, dg1, du1, wg, wu, gd1)
+        d0, g0, u0, factor = lower(dh, dht, a0t, act0, gate0, up0, wd, (d1, g1, u1))
         own, new_moments = adamw(factor, (g0, u0, d0, g1, u1, d1), moments[:3], moments[3:], (wg, wu, wd))
         return (*all_gather(own), *new_moments)
 

time: 386 us -> 418 us (1.083)
  Pallas kernels: 385 us -> 417 us
    pallas_call x2 -> x3, Pallas kernels: 224 us -> 256 us  [the longest x1 119 us: lower(): pl.pallas_call(lower_kernel, grid=(LOWER_STEPS,), in_specs=[WHOLE_S, WHOL...]
where the time goes in v7:
time: 418 us
  Pallas kernels  417 us (100%)
    pallas_call x1, Pallas kernels, lower(): pl.pallas_call(lower_kernel, grid=(LOWER_STEPS,), in_specs=[WHOLE_S, WHOL...  119 us
    pallas_call x1, Pallas kernels, all_gather(): pl.pallas_call(gather_kernel, out_shape=[pltpu.VMEM((2, 2, 2, 2, 2, *o.sh...  98.4 us
    pallas_call x1, Pallas kernels, last(): pl.pallas_call(last_kernel, grid=(STEPS,), in_specs=[ANY, ANY, WHOLE_S, H...  82.8 us
    pallas_call x1, Pallas kernels, upper(): pl.pallas_call(upper_kernel, grid=(STEPS,), in_specs=[WHOLE_S, WHOLE_S, W...  54.2 us
    pallas_call x1, Pallas kernels, forward(): pl.pallas_call(forward_kernel, grid=(TOKENS // TM,), in_specs=[SEQ, SEQ,...  45.7 us
    pallas_call x1, Pallas kernels, all_gather(): pl.pallas_call(flush_kernel, out_shape=[jax.ShapeDtypeStruct(o.shape, BF1...  9.23 us

profile of v7, /device:TPU:0, one launch (start us, length us, event | category | flops | bytes accessed | tf_op | source)
XLA Modules:
  0.0 417.8 jit_solution(6684431854153465569)
XLA Ops:
  0.6 45.7 %forward.1 = (bf16[2048,896]{1,0:T(8,128)(2,1)}, bf16[2048,896]{1,0:T(8,128)(2,1)}, bf16[896,2048]{1,0:T(8,128)(2,1)}, bf16[896,2048]{1,0:T(8,128)(2,1)}, bf16[8...) custom-call(bf16[1,2048,896]{2,1,0:T(8,128)(2,1)} %x.1, ...), custom_call_target="tpu_custom_call" | custom-call | flops 28185722880 | bytes 62914560 | tf_op jit(solution)/shard_map/forward/pallas_call | solution.py:616
  46.4 54.2 %upper.1 = (bf16[2560,896]{1,0:T(8,128)(2,1)}, bf16[2048,2560]{1,0:T(8,128)(2,1)}, bf16[2048,2560]{1,0:T(8,128)(2,1)}) custom-call(bf16[2048,896]{1,0:T(8,128)(2,1)} %get-tuple-element.46.a, bf16[2048,896]{1,0:T(8,128)(2,1)} %bitcast.8, bf16[896,2048]{1,0:T(8,128)(2,1)} %get-tuple-element.47.dyt, bf16[2,896,2560]{2,1,0:T(8,128)(2,1)} %refs_13_.1, ...), custom_call_target="tpu_custom_call" | custom-call | flops 37580963840 | bytes 62914560 | tf_op jit(solution)/shard_map/upper/pallas_call | solution.py:635
  100.6 82.8 %last.1 = (bf16[56,2560]{1,0:T(8,128)(2,1)}, bf16[56,2560]{1,0:T(8,128)(2,1)}, bf16[160,896]{1,0:T(8,128)(2,1)}, bf16[2048,896]{1,0:T(8,128)(2,1)}, bf16[896,2048]{1,0:T(8,128)(2,1)}) custom-call(bf16[896,2048]{1,0:T(8,128)(2,1)} %get-tuple-element.44.at_in, bf16[2048,896]{1,0:T(8,128)(2,1)} %get-tuple-element.45.h_in, bf16[2048,896]{1,0:T(8,128)(2,1)} %bitcast.9, ...), custom_call_target="tpu_custom_call" | custom-call | flops 37580963840 | bytes 62914560 | tf_op jit(solution)/shard_map/last/pallas_call | solution.py:651
  183.5 118.7 %lower.1 = (bf16[160,896]{1,0:T(8,128)(2,1)}, bf16[56,2560]{1,0:T(8,128)(2,1)}, bf16[56,2560]{1,0:T(8,128)(2,1)}, f32[8,128]{1,0:T(8,128)}) custom-call(bf16[2048,896]{1,0:T(8,128)(2,1)} %get-tuple-element.51.dh, bf16[896,2048]{1,0:T(8,128)(2,1)} %get-tuple-element.52.dht, bf16[896,2048]{1,0:T(8,128)(2,1)} %get-tuple-element.53.at, ...), custom_call_target="tpu_custom_call" | custom-call | flops 37580963840 | bytes 62914560 | tf_op jit(solution)/shard_map/lower/pallas_call | solution.py:673
  302.2 7.7 %adamw.1 = (bf16[2,56,2560]{2,1,0:T(8,128)(2,1)S(1)}, bf16[2,56,2560]{2,1,0:T(8,128)(2,1)S(1)}, bf16[2,160,896]{2,1,0:T(8,128)(2,1)S(1)}, f32[2,56,2560]{2,1,0:T...) custom-call(f32[8,128]{1,0:T(8,128)} %get-tuple-element.60.refs_0_, ...), custom_call_target="tpu_custom_call" | custom-call | tf_op jit(solution)/shard_map/adamw/pallas_call | solution.py:377
  309.9 98.4 %all_gather.1 = (bf16[2,2,2,2,2,56,2560]{6,5,4,3,2,1,0:T(8,128)(2,1)S(1)}, bf16[2,2,2,2,2,56,2560]{6,5,4,3,2,1,0:T(8,128)(2,1)S(1)}, bf16[2,2,2,2,2,160,896]{6,5,4,3,2,1,0:T(8,128)(2,1)S(1)}) custom-call(bf16[2,56,2560]{2,1,0:T(8,128)(2,1)S(1)} %get-tuple-element.64.refs_0_, bf16[2,56,2560]{2,1,0:T(8,128)(2,1)S(1)} %get-tuple-element.65.refs_1_, ...), custom_call_target="tpu_custom_call" | custom-call | tf_op jit(solution)/shard_map/all_gather/pallas_call | solution.py:292
  408.3 9.2 %flush.1 = (bf16[2,2,2,2,2,56,2560]{6,5,4,3,2,1,0:T(8,128)(2,1)}, bf16[2,2,2,2,2,56,2560]{6,5,4,3,2,1,0:T(8,128)(2,1)}, bf16[2,2,2,2,2,160,896]{6,5,4,3,2,1,0:T(8,128)(2,1)}) custom-call(bf16[2,2,2,2,2,56,2560]{6,5,4,3,2,1,0:T(8,128)(2,1)S(1)} %get-tuple-element.67.refs_0_, bf16[2,2,2,2,2,56,2560]{6,5,4,3,2,1,0:T(8,128)(2,1)S(1)} %get-tuple-element.68.refs_1_, ...), custom_call_target="tpu_custom_call" | custom-call | tf_op jit(solution)/shard_map/flush/pallas_call | solution.py:305

commit v8 on v7

--- a/solution.py
+++ b/solution.py
@@ -12,6 +12,7 @@
 DEVICES, TOKENS, D, FF = 16, 2048, 896, 2560
 COUNT = 2 * 3 * D * FF
 TM = 256
+Z = 0
 NB = 512
 STEPS = FF // NB
 BN = 256
@@ -20,12 +21,15 @@
 
 STRIDE = (8, 4, 2)
 ORDER = ((0, 1, 2), (1, 2, 0), (2, 0, 1))
-WIDE = (56, 2560, tuple((slice(0, 56), s) for s in (slice(0, 896), slice(896, 1792), slice(1792, 2560))))
-BLOCK = (56, 256, tuple((s, slice(0, 256)) for s in (slice(0, 24), slice(24, 40), slice(40, 56))))
-PAIR = (56, 512, tuple((s, slice(0, 512)) for s in (slice(0, 24), slice(24, 40), slice(40, 56))))
-TALL = (160, 896, tuple((s, slice(0, 896)) for s in (slice(0, 56), slice(56, 112), slice(112, 160))))
+def cuts(*at):
+    return [slice(*pair) for pair in zip(at, at[1:])]
+
+
+WIDE = (56, FF, tuple((slice(Z, 56), s) for s in cuts(Z, 896, 1792, FF)))
+BOTH = (56, 1024, tuple((slice(Z, 56), s) for s in cuts(Z, 384, 768, 1024)))
+TALL = (160, D, tuple((s, slice(Z, D)) for s in cuts(Z, 56, 112, 160)))
 SPLIT = tuple(
-    (slice(c, c + n), (160, n, tuple((s, slice(0, n)) for s in (slice(0, 56), slice(56, 112), slice(112, 160)))))
+    (slice(c, c + n), (160, n, tuple((s, slice(Z, n)) for s in cuts(Z, 56, 112, 160))))
     for c, n in ((0, 512), (512, 384))
 )
 
@@ -146,7 +150,7 @@
 
 
 def squares(g):
-    wide = g.astype(F32)
+    wide = g.astype(F32).reshape(-1, g.shape[-1])
     rows, cols = wide.shape
     s = jnp.sum((wide * wide).reshape(rows // 8, 8, cols), 0)
     return sum(s[:, i : i + 128] for i in range(0, cols, 128))
@@ -192,14 +196,14 @@
 
 
 class Gather:
-    def __init__(self, kind, own, out, layer, ssem, rsem, csem):
-        self.kind, self.own, self.out, self.layer = kind, own, out, layer
+    def __init__(self, kind, own, out, ssem, rsem, csem):
+        self.kind, self.own, self.out = kind, own, out
         self.ssem, self.rsem, self.csem = ssem, rsem, csem
         self.me, self.xyz, self.core = place()
 
     def local(self):
         x, y, z = self.xyz
-        return pltpu.make_async_copy(self.own, self.out.at[self.layer, x, y, z, self.core], self.csem)
+        return pltpu.make_async_copy(self.own, self.out.at[:, x, y, z, self.core], self.csem)
 
     def blocks(self, t, core, known, other=None):
         rows, cols = self.kind[2][t]
@@ -207,7 +211,7 @@
         for axis in range(3):
             p = self.xyz[axis]
             index.append(slice(None) if axis in known else (1 - p if axis == other else p))
-        return self.out.at[(self.layer, *index, core, rows, cols)]
+        return self.out.at[(slice(None), *index, core, rows, cols)]
 
     def hop(self, t, phase, arriving=False):
         axis = ORDER[t][phase]
@@ -215,7 +219,7 @@
         src = self.blocks(t, self.core, known)
         dst = self.blocks(t, self.core, known, axis) if arriving else src
         if phase == 0 and not arriving:
-            src = self.own.at[self.kind[2][t]]
+            src = self.own.at[(slice(None), *self.kind[2][t])]
         return pltpu.make_async_remote_copy(
             src,
             dst,
@@ -240,7 +244,7 @@
         x, y, z = self.xyz
         return pltpu.make_async_remote_copy(
             self.own,
-            self.out.at[self.layer, x, y, z, core],
+            self.out.at[:, x, y, z, core],
             self.ssem.at[9],
             self.rsem.at[9],
             device_id={"dp": partner(self.me, self.core)},
@@ -274,11 +278,7 @@
 
 def gather_kernel(*refs):
     owns, outs, (ssem, rsem, csem) = refs[:3], refs[3:6], refs[6:]
-    units = []
-    for layer in range(2):
-        for i, kind in enumerate((WIDE, WIDE, TALL)):
-            u = 3 * layer + i
-            units.append(Gather(kind, owns[i].at[layer], outs[i], layer, ssem.at[u], rsem.at[u], csem.at[u]))
+    units = [Gather(kind, owns[i], outs[i], ssem.at[i], rsem.at[i], csem.at[i]) for i, kind in enumerate((WIDE, WIDE, TALL))]
     for u in units:
         u.start()
     for phase in range(3):
@@ -295,9 +295,9 @@
         in_specs=[WHOLE] * 3,
         out_specs=[WHOLE] * 3,
         scratch_shapes=[
-            pltpu.SemaphoreType.DMA((6, 19)),
-            pltpu.SemaphoreType.DMA((6, 19)),
-            pltpu.SemaphoreType.DMA((6,)),
+            pltpu.SemaphoreType.DMA((3, 19)),
+            pltpu.SemaphoreType.DMA((3, 19)),
+            pltpu.SemaphoreType.DMA((3,)),
         ],
         compiler_params=pltpu.CompilerParams(has_side_effects=True, vmem_limit_bytes=8 << 20),
         name="all_gather",
@@ -329,20 +329,26 @@
 
 
 def adamw_kernel(*refs):
-    factor, shards, ms, vs, weights = refs[0], refs[1:7], refs[7:10], refs[10:13], refs[13:16]
-    new_ws, new_ms, new_vs = refs[16:19], refs[19:22], refs[22:25]
-    in_ms, in_vs, gs, (isem, osem) = refs[25:28], refs[28:31], refs[31:34], refs[34:]
+    factor, shards, ms, vs, weights = refs[0], refs[1:5], refs[5:8], refs[8:11], refs[11:14]
+    new_ws, new_ms, new_vs = refs[14:17], refs[17:20], refs[20:23]
+    in_ms, in_vs, gs, (isem, osem) = refs[23:26], refs[26:29], refs[29:32], refs[32:]
     me = lax.axis_index("dp")
     loads, stores = [], []
     for i, kind in enumerate(KINDS):
         mine = pl.ds(pl.multiple_of(me * kind[0], 8), kind[0])
         for layer in range(2):
-            pairs = (
-                (shards[3 * layer + i], gs[i].at[layer]),
+            pairs = [
                 (ms[i].at[layer], in_ms[i].at[layer]),
                 (vs[i].at[layer], in_vs[i].at[layer]),
                 (weights[i].at[layer, mine], new_ws[i].at[layer]),
-            )
+            ]
+            if kind is TALL:
+                pairs.append((shards[2 * layer + 1], gs[i].at[layer]))
+            else:
+                at = slice(i * NB, i * NB + NB)
+                pairs += [
+                    (shards[2 * layer].at[k, :, at], gs[i].at[layer, :, k * NB : k * NB + NB]) for k in range(STEPS)
+                ]
             loads.append([pltpu.make_async_copy(src, dst, isem.at[2 * i + layer, k]) for k, (src, dst) in enumerate(pairs)])
             pairs = (in_ms[i], new_ms[i]), (in_vs[i], new_vs[i])
             stores.append(
@@ -377,10 +383,10 @@
     outs = pl.pallas_call(
         adamw_kernel,
         out_shape=[pltpu.VMEM(s, BF16) for s in own] + [jax.ShapeDtypeStruct(s, F32) for s in own * 2],
-        in_specs=[WHOLE] + [ANY] * 15,
+        in_specs=[WHOLE] + [ANY] * 13,
         out_specs=[WHOLE] * 3 + [ANY] * 6,
         scratch_shapes=[pltpu.VMEM(s, t) for t in (F32, F32, BF16) for s in own]
-        + [pltpu.SemaphoreType.DMA((6, 4)), pltpu.SemaphoreType.DMA((6, 2))],
+        + [pltpu.SemaphoreType.DMA((6, 8)), pltpu.SemaphoreType.DMA((6, 2))],
         compiler_params=pltpu.CompilerParams(vmem_limit_bytes=60 * 1024 * 1024),
         name="adamw",
     )(factor, *shards, *ms, *vs, *weights)
@@ -449,22 +455,16 @@
 LAST_SETS = 3
 
 
-def last_kernel(at_in, h_in, dy, dg, du, wg, wu, gd1, og, ou, od1, out_dh, out_dht, *scratch):
-    at, acc_g, acc_u, dh, own_g, own_u, half_d1, lsem, osem = scratch[:9]
+def last_kernel(at_in, h_in, dy, dg, du, wg, wu, gd1, ogu, od1, out_dh, out_dht, *scratch):
+    at, acc_g, acc_u, dh, own, half_d1, lsem, osem = scratch[:8]
     step = pl.program_id(0)
-    d1 = Reduce(TALL, gd1, od1, scratch[9 : 9 + RS_SCRATCH], half_d1)
+    d1 = Reduce(TALL, gd1, od1, scratch[8 : 8 + RS_SCRATCH], half_d1)
 
     def reduce(k, *stages):
         i = k % LAST_SETS
-        rest = [ref.at[i] for ref in scratch[9 + RS_SCRATCH :]]
-        columns = pl.ds(pl.multiple_of(k * NB, NB), NB)
-        units = [
-            Reduce(PAIR, own.at[i], out.at[:, columns], rest[RS_SCRATCH * n : RS_SCRATCH * (n + 1)], turn=n)
-            for n, (own, out) in enumerate(((own_g, og), (own_u, ou)))
-        ]
+        unit = Reduce(BOTH, own.at[i], ogu.at[k], [ref.at[i] for ref in scratch[8 + RS_SCRATCH :]])
         for stage in stages:
-            for u in units:
-                u.run(stage)
+            unit.run(stage)
 
     load = pltpu.make_async_copy(at_in, at, lsem.at[0])
     load_h = pltpu.make_async_copy(h_in, dh, lsem.at[1])
@@ -479,8 +479,8 @@
         load.wait()
 
     i = step % LAST_SETS
-    own_g[i] = wide_block(at, dg)
-    own_u[i] = wide_block(at, du)
+    own[i, :, :, :, :NB] = wide_block(at, dg)
+    own[i, :, :, :, NB:] = wide_block(at, du)
 
     @pl.when(step > 1)
     def _():
@@ -529,25 +529,25 @@
             c.wait()
 
 
-SETS = 7
-LOWER_STEPS = 2 * STEPS + 2 * STEPS
-
-
-def lower_kernel(dh, dht, at, act, gate, up, wd, d1, g1, u1, od, og, ou, factor, *scratch):
+SETS = 4
+LOWER_STEPS = 4 * STEPS
+
+
+def lower_kernel(dh, dht, at, act, gate, up, wd, d1, gu1, od, ogu, factor, *scratch):
     step = pl.program_id(0)
-    dg, du, own_g, own_u = scratch[:4]
-    own_d = scratch[4:6]
-    rest = scratch[6:]
-    sets = [rest[RS_SCRATCH * i : RS_SCRATCH * (i + 1)] for i in range(4)]
+    dg, du, own = scratch[:3]
+    own_d = scratch[3:5]
+    rest = scratch[5:]
+    sets = [rest[RS_SCRATCH * i : RS_SCRATCH * (i + 1)] for i in range(3)]
 
     @pl.when(step < 2 * STEPS)
     def _():
         dact = dot_t(dh[...], wd[...]).astype(BF16)
         for r in pieces(4):
             dg[r], du[r] = gated_back(gate[r], up[r], dact[r])
-        i = step % SETS
-        own_g[i] = wide_block(at, dg)
-        own_u[i] = wide_block(at, du)
+        i = step // 2 % SETS
+        for first, grad in ((0, dg), (NB, du)):
+            own[i, :, :, :, pl.ds(pl.multiple_of(first + step % 2 * BN, BN), BN)] = wide_block(at, grad)
 
     for part, (columns, kind) in enumerate(SPLIT):
         first = (2 + part) * STEPS
@@ -557,17 +557,15 @@
             rows = pl.ds(pl.multiple_of((step - first) * NB, NB), NB)
             own_d[part].reshape(FF, n)[rows] = dot(dht[columns], act[...]).astype(BF16).T
 
-    for late, stages in ((6, (3, "finish")), (5, (2,)), (3, (1,)), (1, (0,)), (0, ("start",))):
-
-        @pl.when((step >= late) & (step < 2 * STEPS + late))
+    for late, stages in ((7, (3, "finish")), (6, (2,)), (4, (1,)), (2, (0,)), (1, ("start",))):
+
+        @pl.when((step >= late) & (step < 2 * STEPS + late) & ((step - late) % 2 == 0))
         def _(late=late, stages=stages):
-            j = step - late
+            j = (step - late) // 2
             k = j % SETS
-            columns = pl.ds(pl.multiple_of(j * BN, BN), BN)
-            for n, (own, out) in enumerate(((own_g, og), (own_u, ou))):
-                unit = Reduce(BLOCK, own.at[k], out.at[:, columns], [ref.at[k] for ref in sets[2 + n]], turn=n)
-                for stage in stages:
-                    unit.run(stage)
+            unit = Reduce(BOTH, own.at[k], ogu.at[j], [ref.at[k] for ref in sets[2]])
+            for stage in stages:
+                unit.run(stage)
 
     plan = {when: [] for when in (3 * STEPS - 1, 3 * STEPS + 2, LOWER_STEPS - 1)}
     da, db = (
@@ -581,19 +579,19 @@
 
     @pl.when(step == LOWER_STEPS - 1)
     def _():
-        clip_factor([d1, g1, u1, od, og, ou], factor, *rest[RS_SCRATCH * 4 :])
+        clip_factor([d1, gu1, od, ogu], factor, *rest[RS_SCRATCH * 3 :])
 
 
 def rows(cols):
-    return pl.BlockSpec((TM, cols), lambda i: (i, 0))
-
-
-SEQ = pl.BlockSpec((None, TM, D), lambda i: (0, i, 0))
-COLUMNS = pl.BlockSpec((D, TM), lambda i: (0, i))
+    return pl.BlockSpec((TM, cols), lambda i: (i, Z))
+
+
+SEQ = pl.BlockSpec((None, TM, D), lambda i: (Z, i, Z))
+COLUMNS = pl.BlockSpec((D, TM), lambda i: (Z, i))
 
 
 def weight(layer, shape):
-    return pl.BlockSpec((None, *shape), lambda i: (layer, 0, 0), pipeline_mode=pl.Buffered(1))
+    return pl.BlockSpec((None, *shape), lambda i: (layer, Z, Z), pipeline_mode=pl.Buffered(1))
 
 
 def matrix(r, c, t=BF16):
@@ -609,7 +607,11 @@
 
 
 def shard(kind):
-    return pl.BlockSpec(kind[:2], lambda i: (0, 0))
+    return pl.BlockSpec(kind[:2], lambda i: (Z, Z))
+
+
+SHARDS = (STEPS, *BOTH[:2])
+BOTH_SHARD = pl.BlockSpec(SHARDS, lambda i: (Z, Z, Z))
 
 
 def forward(x, dy, wg, wu, wd):
@@ -625,18 +627,18 @@
     )(x, dy, wg, wu, wd)
 
 
-WHOLE_S = pl.BlockSpec((TOKENS, D), lambda i: (0, 0), pipeline_mode=pl.Buffered(1))
-WHOLE_T = pl.BlockSpec((D, TOKENS), lambda i: (0, 0), pipeline_mode=pl.Buffered(1))
-HIDDEN = pl.BlockSpec((TOKENS, NB), lambda i: (0, i))
-WIDE_W = pl.BlockSpec((None, D, NB), lambda i: (1, 0, i))
+WHOLE_S = pl.BlockSpec((TOKENS, D), lambda i: (Z, Z), pipeline_mode=pl.Buffered(1))
+WHOLE_T = pl.BlockSpec((D, TOKENS), lambda i: (Z, Z), pipeline_mode=pl.Buffered(1))
+HIDDEN = pl.BlockSpec((TOKENS, NB), lambda i: (Z, i))
+WIDE_W = pl.BlockSpec((None, D, NB), lambda i: (1, Z, i))
 
 
 def upper(a, dy, dyt, wg, wu, wd):
     return pl.pallas_call(
         upper_kernel,
         grid=(STEPS,),
-        in_specs=[WHOLE_S, WHOLE_S, WHOLE_T, WIDE_W, WIDE_W, pl.BlockSpec((None, NB, D), lambda i: (1, i, 0))],
-        out_specs=[pl.BlockSpec((NB, D), lambda i: (i, 0)), HIDDEN, HIDDEN],
+        in_specs=[WHOLE_S, WHOLE_S, WHOLE_T, WIDE_W, WIDE_W, pl.BlockSpec((None, NB, D), lambda i: (1, i, Z))],
+        out_specs=[pl.BlockSpec((NB, D), lambda i: (i, Z)), HIDDEN, HIDDEN],
         out_shape=[matrix(FF, D), matrix(TOKENS, FF), matrix(TOKENS, FF)],
         scratch_shapes=[pltpu.VMEM((TOKENS, NB), BF16)],
         compiler_params=params(),
@@ -647,17 +649,17 @@
 
 def last(at, h, dy, dg, du, wg, wu, gd1):
     straight, turned, sums = pltpu.VMEM((TOKENS, D), BF16), pltpu.VMEM((D, TOKENS), BF16), pltpu.VMEM((TOKENS, D), F32)
-    own = pltpu.VMEM((LAST_SETS, 8, 2, *PAIR[:2]), BF16)
+    own = pltpu.VMEM((LAST_SETS, 8, 2, *BOTH[:2]), BF16)
     return pl.pallas_call(
         last_kernel,
         grid=(STEPS,),
         in_specs=[ANY, ANY, WHOLE_S, HIDDEN, HIDDEN, WIDE_W, WIDE_W, ANY],
-        out_specs=[shard(WIDE), shard(WIDE), shard(TALL), ANY, ANY],
-        out_shape=[matrix(*k[:2]) for k in (WIDE, WIDE, TALL)] + [matrix(TOKENS, D), matrix(D, TOKENS)],
-        scratch_shapes=[turned, sums, sums, straight, own, own, pltpu.VMEM((8, *TALL[:2]), BF16)]
+        out_specs=[BOTH_SHARD, shard(TALL), ANY, ANY],
+        out_shape=[jax.ShapeDtypeStruct(SHARDS, BF16), matrix(*TALL[:2]), matrix(TOKENS, D), matrix(D, TOKENS)],
+        scratch_shapes=[turned, sums, sums, straight, own, pltpu.VMEM((8, *TALL[:2]), BF16)]
         + [pltpu.SemaphoreType.DMA((2,)), pltpu.SemaphoreType.DMA((2,))]
         + rs_scratch(TALL)
-        + rs_scratch(PAIR, (LAST_SETS,)) * 2,
+        + rs_scratch(BOTH, (LAST_SETS,)),
         compiler_params=params(True),
         cost_estimate=cost(4),
         name="last",
@@ -668,8 +670,7 @@
     def column(i):
         return jnp.minimum(i, 2 * STEPS - 1)
 
-    block = pl.BlockSpec((TOKENS, BN), lambda i: (0, column(i)))
-    outs = (TALL, WIDE, WIDE)
+    block = pl.BlockSpec((TOKENS, BN), lambda i: (Z, column(i)))
     return pl.pallas_call(
         lower_kernel,
         grid=(LOWER_STEPS,),
@@ -677,21 +678,20 @@
             WHOLE_S,
             WHOLE_T,
             WHOLE_T,
-            pl.BlockSpec((TOKENS, NB), lambda i: (0, jnp.maximum(i - 2 * STEPS, 0) % STEPS)),
+            pl.BlockSpec((TOKENS, NB), lambda i: (Z, jnp.maximum(i - 2 * STEPS, Z) % STEPS)),
             block,
             block,
-            pl.BlockSpec((None, BN, D), lambda i: (0, column(i), 0)),
+            pl.BlockSpec((None, BN, D), lambda i: (Z, column(i), Z)),
             shard(TALL),
-            shard(WIDE),
-            shard(WIDE),
+            BOTH_SHARD,
         ],
-        out_specs=[shard(k) for k in outs] + [pl.BlockSpec((8, 128), lambda i: (0, 0))],
-        out_shape=[matrix(*k[:2]) for k in outs] + [matrix(8, 128, F32)],
+        out_specs=[shard(TALL), BOTH_SHARD, pl.BlockSpec((8, 128), lambda i: (Z, Z))],
+        out_shape=[matrix(*TALL[:2]), jax.ShapeDtypeStruct(SHARDS, BF16), matrix(8, 128, F32)],
         scratch_shapes=[pltpu.VMEM((TOKENS, BN), BF16)] * 2
-        + [pltpu.VMEM((SETS, 8, 2, *BLOCK[:2]), BF16)] * 2
+        + [pltpu.VMEM((SETS, 8, 2, *BOTH[:2]), BF16)]
         + [pltpu.VMEM((8, 2, *kind[:2]), BF16) for _, kind in SPLIT]
         + sum((rs_scratch(kind) for _, kind in SPLIT), [])
-        + rs_scratch(BLOCK, (SETS,)) * 2
+        + rs_scratch(BOTH, (SETS,))
         + CLIP_SCRATCH,
         compiler_params=params(True),
         cost_estimate=cost(4),
@@ -704,9 +704,9 @@
         h1, a1, a1t, dyt, a0t, act0, gate0, up0 = forward(x, dy, wg, wu, wd)
         flat_dy = dy.reshape(TOKENS, D)
         gd1, dg1, du1 = upper(a1, flat_dy, dyt, wg, wu, wd)
-        g1, u1, d1, dh, dht = last(a1t, h1, flat_dy, dg1, du1, wg, wu, gd1)
-        d0, g0, u0, factor = lower(dh, dht, a0t, act0, gate0, up0, wd, (d1, g1, u1))
-        own, new_moments = adamw(factor, (g0, u0, d0, g1, u1, d1), moments[:3], moments[3:], (wg, wu, wd))
+        gu1, d1, dh, dht = last(a1t, h1, flat_dy, dg1, du1, wg, wu, gd1)
+        d0, gu0, factor = lower(dh, dht, a0t, act0, gate0, up0, wd, (d1, gu1))
+        own, new_moments = adamw(factor, (gu0, d0, gu1, d1), moments[:3], moments[3:], (wg, wu, wd))
         return (*all_gather(own), *new_moments)
 
     seq = P(("rep", "dp"), None, None)

time: 418 us -> 415 us (level)
  no operation moved by 1% of the time
where the time goes in v8:
time: 415 us
  Pallas kernels  414 us (100%)
    pallas_call x1, Pallas kernels, lower(): pl.pallas_call(lower_kernel, grid=(LOWER_STEPS,), in_specs=[WHOLE_S, WHOL...  115 us
    pallas_call x1, Pallas kernels, all_gather(): pl.pallas_call(gather_kernel, out_shape=[pltpu.VMEM((2, 2, 2, 2, 2, *o.sh...  99.2 us
    pallas_call x1, Pallas kernels, last(): pl.pallas_call(last_kernel, grid=(STEPS,), in_specs=[ANY, ANY, WHOLE_S, H...  83.3 us
    pallas_call x1, Pallas kernels, upper(): pl.pallas_call(upper_kernel, grid=(STEPS,), in_specs=[WHOLE_S, WHOLE_S, W...  54.2 us
    pallas_call x1, Pallas kernels, forward(): pl.pallas_call(forward_kernel, grid=(TOKENS // TM,), in_specs=[SEQ, SEQ,...  45.7 us
    pallas_call x1, Pallas kernels, all_gather(): pl.pallas_call(flush_kernel, out_shape=[jax.ShapeDtypeStruct(o.shape, BF1...  9.23 us

profile of v8, /device:TPU:0, one launch (start us, length us, event | category | flops | bytes accessed | tf_op | source)
XLA Modules:
  0.0 415.1 jit_solution(7222502185806633463)
XLA Ops:
  0.6 45.7 %forward.1 = (bf16[2048,896]{1,0:T(8,128)(2,1)}, bf16[2048,896]{1,0:T(8,128)(2,1)}, bf16[896,2048]{1,0:T(8,128)(2,1)}, bf16[896,2048]{1,0:T(8,128)(2,1)}, bf16[8...) custom-call(bf16[1,2048,896]{2,1,0:T(8,128)(2,1)} %x.1, ...), custom_call_target="tpu_custom_call" | custom-call | flops 28185722880 | bytes 62914560 | tf_op jit(solution)/shard_map/forward/pallas_call | solution.py:618
  46.4 54.2 %upper.1 = (bf16[2560,896]{1,0:T(8,128)(2,1)}, bf16[2048,2560]{1,0:T(8,128)(2,1)}, bf16[2048,2560]{1,0:T(8,128)(2,1)}) custom-call(bf16[2048,896]{1,0:T(8,128)(2,1)} %get-tuple-element.44.a, bf16[2048,896]{1,0:T(8,128)(2,1)} %bitcast.8, bf16[896,2048]{1,0:T(8,128)(2,1)} %get-tuple-element.45.dyt, bf16[2,896,2560]{2,1,0:T(8,128)(2,1)} %refs_11_.1, ...), custom_call_target="tpu_custom_call" | custom-call | flops 37580963840 | bytes 62914560 | tf_op jit(solution)/shard_map/upper/pallas_call | solution.py:637
  100.6 83.3 %last.1 = (bf16[5,56,1024]{2,1,0:T(8,128)(2,1)}, bf16[160,896]{1,0:T(8,128)(2,1)}, bf16[2048,896]{1,0:T(8,128)(2,1)}, bf16[896,2048]{1,0:T(8,128)(2,1)}) custom-call(bf16[896,2048]{1,0:T(8,128)(2,1)} %get-tuple-element.42.at_in, bf16[2048,896]{1,0:T(8,128)(2,1)} %get-tuple-element.43.h_in, bf16[2048,896]{1,0:T(8,128)(2,1)} %bitcast.9, ...), custom_call_target="tpu_custom_call" | custom-call | flops 37580963840 | bytes 62914560 | tf_op jit(solution)/shard_map/last/pallas_call | solution.py:653
  183.9 114.7 %lower.1 = (bf16[160,896]{1,0:T(8,128)(2,1)}, bf16[5,56,1024]{2,1,0:T(8,128)(2,1)}, f32[8,128]{1,0:T(8,128)}) custom-call(bf16[2048,896]{1,0:T(8,128)(2,1)} %get-tuple-element.49.dh, bf16[896,2048]{1,0:T(8,128)(2,1)} %get-tuple-element.50.dht, bf16[896,2048]{1,0:T(8,128)(2,1)} %get-tuple-element.51.at, bf16[2048,2560]{1,0:T(8,128)(2,1)} %get-tuple-element.52.act, ...), custom_call_target="tpu_custom_call" | custom-call | flops 37580963840 | bytes 62914560 | tf_op jit(solution)/shard_map/lower/pallas_call | solution.py:674
  298.7 7.9 %adamw.1 = (bf16[2,56,2560]{2,1,0:T(8,128)(2,1)S(1)}, bf16[2,56,2560]{2,1,0:T(8,128)(2,1)S(1)}, bf16[2,160,896]{2,1,0:T(8,128)(2,1)S(1)}, f32[2,56,2560]{2,1,0:T...) custom-call(f32[8,128]{1,0:T(8,128)} %get-tuple-element.57.refs_0_, ...), custom_call_target="tpu_custom_call" | custom-call | tf_op jit(solution)/shard_map/adamw/pallas_call | solution.py:383
  306.5 99.2 %all_gather.1 = (bf16[2,2,2,2,2,56,2560]{6,5,4,3,2,1,0:T(8,128)(2,1)S(1)}, bf16[2,2,2,2,2,56,2560]{6,5,4,3,2,1,0:T(8,128)(2,1)S(1)}, bf16[2,2,2,2,2,160,896]{6,5,4,3,2,1,0:T(8,128)(2,1)S(1)}) custom-call(bf16[2,56,2560]{2,1,0:T(8,128)(2,1)S(1)} %get-tuple-element.60.refs_0_, bf16[2,56,2560]{2,1,0:T(8,128)(2,1)S(1)} %get-tuple-element.61.refs_1_, ...), custom_call_target="tpu_custom_call" | custom-call | tf_op jit(solution)/shard_map/all_gather/pallas_call | solution.py:292
  405.7 9.2 %flush.1 = (bf16[2,2,2,2,2,56,2560]{6,5,4,3,2,1,0:T(8,128)(2,1)}, bf16[2,2,2,2,2,56,2560]{6,5,4,3,2,1,0:T(8,128)(2,1)}, bf16[2,2,2,2,2,160,896]{6,5,4,3,2,1,0:T(8,128)(2,1)}) custom-call(bf16[2,2,2,2,2,56,2560]{6,5,4,3,2,1,0:T(8,128)(2,1)S(1)} %get-tuple-element.63.refs_0_, bf16[2,2,2,2,2,56,2560]{6,5,4,3,2,1,0:T(8,128)(2,1)S(1)} %get-tuple-element.64.refs_1_, ...), custom_call_target="tpu_custom_call" | custom-call | tf_op jit(solution)/shard_map/flush/pallas_call | solution.py:305

commit v9 on v6

--- a/solution.py
+++ b/solution.py
@@ -12,6 +12,7 @@
 DEVICES, TOKENS, D, FF = 16, 2048, 896, 2560
 COUNT = 2 * 3 * D * FF
 TM = 256
+Z = 0
 NB = 512
 STEPS = FF // NB
 BN = 256
@@ -442,9 +443,9 @@
 
     def units(k):
         columns = pl.ds(pl.multiple_of(k * NB, NB), NB)
-        rest = [ref.at[k % 2] for ref in scratch[14:]]
+        rest = [ref.at[k % 3] for ref in scratch[14:]]
         return [
-            Reduce(PAIR, own, out.at[:, columns], rest[RS_SCRATCH * i : RS_SCRATCH * (i + 1)], turn=i)
+            Reduce(PAIR, own.at[k % 2], out.at[:, columns], rest[RS_SCRATCH * i : RS_SCRATCH * (i + 1)], turn=i)
             for i, (own, out) in enumerate(((own_g, og), (own_u, ou)))
         ]
 
@@ -475,31 +476,33 @@
         dg[r], du[r] = gated_back(g, u, dact)
 
     quarters = pieces(4)
-    for r in quarters[:2]:
+    for r in quarters:
         projections(r)
 
     @pl.when(step > 0)
     def _():
-        reduce(step - 1, 2)
-
-    for r in quarters[2:]:
-        projections(r)
-
-    @pl.when(step > 0)
-    def _():
-        reduce(step - 1, 3, "finish")
+        reduce(step - 1, 1)
 
     first(2)
-    own_g[...] = wide_block(at, dg)
-    own_u[...] = wide_block(at, du)
+    own_g[step % 2] = wide_block(at, dg)
+    own_u[step % 2] = wide_block(at, du)
     reduce(step, "start")
     first(3)
     gd[...] = dot(dyt[...], act[...]).astype(BF16).T
-    reduce(step, 0)
+
+    @pl.when(step > 0)
+    def _():
+        reduce(step - 1, 2)
+
     for r in quarters:
         acc_g[r] += dot_t(dg[r], wg[...])
         acc_u[r] += dot_t(du[r], wu[...])
-    reduce(step, 1)
+
+    @pl.when(step > 0)
+    def _():
+        reduce(step - 1, 3, "finish")
+
+    reduce(step, 0)
 
     @pl.when(step == STEPS - 1)
     def _():
@@ -515,18 +518,17 @@
             at[:, r] = d.T
             return carry
 
-        lax.fori_loop(0, 4, through, 0)
-        reduce(step, 2)
-        lax.fori_loop(4, 8, through, 0)
+        lax.fori_loop(0, 8, through, 0)
+        reduce(step, 1)
         stores = [pltpu.make_async_copy(s, d, osem.at[i]) for i, (s, d) in enumerate(((a, out_dh), (at, out_dht)))]
         for c in stores:
             c.start()
-        reduce(step, 3, "finish")
+        reduce(step, 2, 3, "finish")
         for c in stores:
             c.wait()
 
 
-SETS = 5
+SETS = 7
 
 
 def lower_kernel(dh, dht, at, act, gate, up, wd, gd1, g1, u1, od1, od, og, ou, factor, *scratch):
@@ -565,7 +567,7 @@
             Reduce(BLOCK, own.at[k], out.at[:, BN * j : BN * j + BN], sets[2 + 2 * k + i], turn=(i + j) % 3)
             for i, (own, out) in enumerate(((own_g, og), (own_u, ou)))
         ]
-        for n, stage in enumerate(("start", 0, 1, 2, 3)):
+        for n, stage in zip((0, 1, 3, 5, 6), ("start", 0, 1, 2, 3), strict=True):
             when = STEPS + j + n
             late = when - (3 * STEPS - 1)
             for unit in pair:
@@ -574,8 +576,8 @@
                 else:
                     tail.append((late, unit, stage))
         last = [(unit, "finish") for unit in pair]
-        if STEPS + j + 4 < 3 * STEPS:
-            plan[STEPS + j + 4] += last
+        if STEPS + j + 6 < 3 * STEPS:
+            plan[STEPS + j + 6] += last
         else:
             tail += [(9, *entry) for entry in last]
     tail = [entry[1:] for entry in sorted(tail, key=lambda entry: entry[0])]
@@ -588,15 +590,15 @@
 
 
 def rows(cols):
-    return pl.BlockSpec((TM, cols), lambda i: (i, 0))
-
-
-SEQ = pl.BlockSpec((None, TM, D), lambda i: (0, i, 0))
-COLUMNS = pl.BlockSpec((D, TM), lambda i: (0, i))
+    return pl.BlockSpec((TM, cols), lambda i: (i, Z))
+
+
+SEQ = pl.BlockSpec((None, TM, D), lambda i: (Z, i, Z))
+COLUMNS = pl.BlockSpec((D, TM), lambda i: (Z, i))
 
 
 def weight(layer, shape):
-    return pl.BlockSpec((None, *shape), lambda i: (layer, 0, 0), pipeline_mode=pl.Buffered(1))
+    return pl.BlockSpec((None, *shape), lambda i: (layer, Z, Z), pipeline_mode=pl.Buffered(1))
 
 
 def matrix(r, c, t=BF16):
@@ -608,11 +610,11 @@
 
 
 def params(remote=False):
-    return pltpu.CompilerParams(vmem_limit_bytes=60 * 1024 * 1024, has_side_effects=remote)
+    return pltpu.CompilerParams(vmem_limit_bytes=67043328 if remote else 60 * 1024 * 1024, has_side_effects=remote)
 
 
 def shard(kind):
-    return pl.BlockSpec(kind[:2], lambda i: (0, 0))
+    return pl.BlockSpec(kind[:2], lambda i: (Z, Z))
 
 
 def forward(x, dy, wg, wu, wd):
@@ -629,34 +631,34 @@
 
 
 def last(a, at, dy, dyt, h, wg, wu, wd):
-    wide = pl.BlockSpec((None, D, NB), lambda i: (1, 0, i))
+    wide = pl.BlockSpec((None, D, NB), lambda i: (1, Z, i))
     straight, turned = pltpu.VMEM((TOKENS, D), BF16), pltpu.VMEM((D, TOKENS), BF16)
     hidden, sums = pltpu.VMEM((TOKENS, NB), BF16), pltpu.VMEM((TOKENS, D), F32)
-    own = pltpu.VMEM((8, 2, *PAIR[:2]), BF16)
+    own = pltpu.VMEM((2, 8, 2, *PAIR[:2]), BF16)
     return pl.pallas_call(
         last_kernel,
         grid=(STEPS,),
-        in_specs=[ANY] * 5 + [wide, wide, pl.BlockSpec((None, NB, D), lambda i: (1, i, 0))],
-        out_specs=[pl.BlockSpec((NB, D), lambda i: (i, 0)), shard(WIDE), shard(WIDE), ANY, ANY],
+        in_specs=[ANY] * 5 + [wide, wide, pl.BlockSpec((None, NB, D), lambda i: (1, i, Z))],
+        out_specs=[pl.BlockSpec((NB, D), lambda i: (i, Z)), shard(WIDE), shard(WIDE), ANY, ANY],
         out_shape=[matrix(FF, D), matrix(*WIDE[:2]), matrix(*WIDE[:2]), matrix(TOKENS, D), matrix(D, TOKENS)],
         scratch_shapes=[straight, turned, straight, turned, straight, hidden, hidden, hidden, sums, sums, own, own]
         + [pltpu.SemaphoreType.DMA((5,)), pltpu.SemaphoreType.DMA((2,))]
-        + rs_scratch(PAIR, (2,)) * 2,
+        + rs_scratch(PAIR, (3,)) * 2,
         compiler_params=params(True),
         cost_estimate=cost(8),
         name="last",
     )(a, at, dy.reshape(TOKENS, D), dyt, h, wg, wu, wd)
 
 
-WHOLE_S = pl.BlockSpec((TOKENS, D), lambda i: (0, 0), pipeline_mode=pl.Buffered(1))
-WHOLE_T = pl.BlockSpec((D, TOKENS), lambda i: (0, 0), pipeline_mode=pl.Buffered(1))
+WHOLE_S = pl.BlockSpec((TOKENS, D), lambda i: (Z, Z), pipeline_mode=pl.Buffered(1))
+WHOLE_T = pl.BlockSpec((D, TOKENS), lambda i: (Z, Z), pipeline_mode=pl.Buffered(1))
 
 
 def lower(dh, dht, at, act, gate, up, wd, gd1, g1, u1):
     def later(i):
         return jnp.maximum(i - STEPS, 0)
 
-    block = pl.BlockSpec((TOKENS, BN), lambda i: (0, later(i)))
+    block = pl.BlockSpec((TOKENS, BN), lambda i: (Z, later(i)))
     outs = (TALL, TALL, WIDE, WIDE)
     return pl.pallas_call(
         lower_kernel,
@@ -665,15 +667,15 @@
             WHOLE_S,
             WHOLE_T,
             WHOLE_T,
-            pl.BlockSpec((TOKENS, NB), lambda i: (0, jnp.minimum(i, STEPS - 1))),
+            pl.BlockSpec((TOKENS, NB), lambda i: (Z, jnp.minimum(i, STEPS - 1))),
             block,
             block,
-            pl.BlockSpec((None, BN, D), lambda i: (0, later(i), 0)),
+            pl.BlockSpec((None, BN, D), lambda i: (Z, later(i), Z)),
             ANY,
             shard(WIDE),
             shard(WIDE),
         ],
-        out_specs=[shard(k) for k in outs] + [pl.BlockSpec((8, 128), lambda i: (0, 0))],
+        out_specs=[shard(k) for k in outs] + [pl.BlockSpec((8, 128), lambda i: (Z, Z))],
         out_shape=[matrix(*k[:2]) for k in outs] + [matrix(8, 128, F32)],
         scratch_shapes=[pltpu.VMEM((TOKENS, BN), BF16)] * 2
         + [pltpu.VMEM((SETS, 8, 2, *BLOCK[:2]), BF16)] * 2

time: 386 us -> 380 us (0.984)
  Pallas kernels: 385 us -> 379 us
    pallas_call x1, Pallas kernels: 105 us -> 97.3 us  [lower(): pl.pallas_call(lower_kernel, grid=(3 * STEPS,), in_specs=[WHOLE_S, WHOLE_...]
where the time goes in v9:
time: 380 us
  Pallas kernels  379 us (100%)
    pallas_call x1, Pallas kernels, last(): pl.pallas_call(last_kernel, grid=(STEPS,), in_specs=[ANY] * 5 + [wide, wi...  121 us
    pallas_call x1, Pallas kernels, all_gather(): pl.pallas_call(gather_kernel, out_shape=[pltpu.VMEM((2, 2, 2, 2, 2, *o.sh...  98.2 us
    pallas_call x1, Pallas kernels, lower(): pl.pallas_call(lower_kernel, grid=(3 * STEPS,), in_specs=[WHOLE_S, WHOLE_...  97.3 us
    pallas_call x1, Pallas kernels, forward(): pl.pallas_call(forward_kernel, grid=(TOKENS // TM,), in_specs=[SEQ, SEQ,...  45.7 us
    pallas_call x1, Pallas kernels, all_gather(): pl.pallas_call(flush_kernel, out_shape=[jax.ShapeDtypeStruct(o.shape, BF1...  9.23 us
    pallas_call x1, Pallas kernels, adamw(): pl.pallas_call(adamw_kernel, out_shape=[pltpu.VMEM(s, BF16) for s in own]...  7.69 us

profile of v9, /device:TPU:0, one launch (start us, length us, event | category | flops | bytes accessed | tf_op | source)
XLA Modules:
  0.0 379.6 jit_solution(15939950685207338346)
XLA Ops:
  0.6 45.7 %forward.1 = (bf16[2048,896]{1,0:T(8,128)(2,1)}, bf16[2048,896]{1,0:T(8,128)(2,1)}, bf16[896,2048]{1,0:T(8,128)(2,1)}, bf16[896,2048]{1,0:T(8,128)(2,1)}, bf16[8...) custom-call(bf16[1,2048,896]{2,1,0:T(8,128)(2,1)} %x.1, ...), custom_call_target="tpu_custom_call" | custom-call | flops 28185722880 | bytes 62914560 | tf_op jit(solution)/shard_map/forward/pallas_call | solution.py:621
  46.3 120.6 %last.1 = (bf16[2560,896]{1,0:T(8,128)(2,1)}, bf16[56,2560]{1,0:T(8,128)(2,1)}, bf16[56,2560]{1,0:T(8,128)(2,1)}, bf16[2048,896]{1,0:T(8,128)(2,1)}, bf16[896,2048]{1,0:T(8,128)(2,1)}) custom-call(bf16[2048,896]{1,0:T(8,128)(2,1)} %get-tuple-element.42.hbm_a, bf16[896,2048]{1,0:T(8,128)(2,1)} %get-tuple-element.43.hbm_at, bf16[2048,896]{1,0:T(8,128)(2,1)} %bitcast.8, ...), custom_call_target="tpu_custom_call" | custom-call | flops 75161927680 | bytes 62914560 | tf_op jit(solution)/shard_map/last/pallas_call | solution.py:638
  166.9 97.3 %lower.1 = (bf16[160,896]{1,0:T(8,128)(2,1)}, bf16[160,896]{1,0:T(8,128)(2,1)}, bf16[56,2560]{1,0:T(8,128)(2,1)}, bf16[56,2560]{1,0:T(8,128)(2,1)}, f32[8,128]{1,0:T(8,128)}) custom-call(bf16[2048,896]{1,0:T(8,128)(2,1)} %get-tuple-element.46.dh, bf16[896,2048]{1,0:T(8,128)(2,1)} %get-tuple-element.47.dht, bf16[896,2048]{1,0:T(8,128)(2,1)} %get-tuple-element.48.at, ...), custom_call_target="tpu_custom_call" | custom-call | flops 37580963840 | bytes 62914560 | tf_op jit(solution)/shard_map/lower/pallas_call | solution.py:663
  264.3 7.7 %adamw.1 = (bf16[2,56,2560]{2,1,0:T(8,128)(2,1)S(1)}, bf16[2,56,2560]{2,1,0:T(8,128)(2,1)S(1)}, bf16[2,160,896]{2,1,0:T(8,128)(2,1)S(1)}, f32[2,56,2560]{2,1,0:T...) custom-call(f32[8,128]{1,0:T(8,128)} %get-tuple-element.55.refs_0_, ...), custom_call_target="tpu_custom_call" | custom-call | tf_op jit(solution)/shard_map/adamw/pallas_call | solution.py:371
  272.0 98.2 %all_gather.1 = (bf16[2,2,2,2,2,56,2560]{6,5,4,3,2,1,0:T(8,128)(2,1)S(1)}, bf16[2,2,2,2,2,56,2560]{6,5,4,3,2,1,0:T(8,128)(2,1)S(1)}, bf16[2,2,2,2,2,160,896]{6,5,4,3,2,1,0:T(8,128)(2,1)S(1)}) custom-call(bf16[2,56,2560]{2,1,0:T(8,128)(2,1)S(1)} %get-tuple-element.60.refs_0_, bf16[2,56,2560]{2,1,0:T(8,128)(2,1)S(1)} %get-tuple-element.61.refs_1_, ...), custom_call_target="tpu_custom_call" | custom-call | tf_op jit(solution)/shard_map/all_gather/pallas_call | solution.py:286
  370.2 9.2 %flush.1 = (bf16[2,2,2,2,2,56,2560]{6,5,4,3,2,1,0:T(8,128)(2,1)}, bf16[2,2,2,2,2,56,2560]{6,5,4,3,2,1,0:T(8,128)(2,1)}, bf16[2,2,2,2,2,160,896]{6,5,4,3,2,1,0:T(8,128)(2,1)}) custom-call(bf16[2,2,2,2,2,56,2560]{6,5,4,3,2,1,0:T(8,128)(2,1)S(1)} %get-tuple-element.63.refs_0_, bf16[2,2,2,2,2,56,2560]{6,5,4,3,2,1,0:T(8,128)(2,1)S(1)} %get-tuple-element.64.refs_1_, ...), custom_call_target="tpu_custom_call" | custom-call | tf_op jit(solution)/shard_map/flush/pallas_call | solution.py:299
